TPU v7x, 32 devices: a whole 2x2x4 slice. The times are simulated.
32 devices in a mesh: sub: 8 (over y, x, core), mode: 4 (over z).
Axes of the slice: x: 2, y: 2, z: 4, core: 2. Of those that a mesh axis runs over, the one named last changes fastest.
Arguments:
- leaf_coords: bfloat16 [64, 768, 128], P('sub', 'mode'), may hold values from -6 to 6
- leaf_modes: bfloat16 [64, 128, 512], P('sub'), may hold values from -0.5 to 0.5
- constraint_modes: bfloat16 [64, 3, 256, 512], P('sub'), may hold values from -0.375 to 0.375
- sep_one: bfloat16 [768, 1024], P('mode', 'sub'), may hold values from -6 to 6
- sep_two: bfloat16 [768, 512], P('mode', 'sub'), may hold values from -6 to 6
- sep_three: bfloat16 [768, 256], P('mode', 'sub'), may hold values from -6 to 6
- cluster_rows: int32 [24, 512], P('sub'), may hold values from 0 to 32767, as said below
- operators: bfloat16 [24, 512, 384], P('sub'), may hold values from -0.25 to 0.25
- compliance: float32 [24, 384], P('sub'), may hold values from 0.05 to 0.5
- modal_weight: float32 [768], P('mode'), may hold values from 0.5 to 2
Outputs:
- stresses: float32 [24, 768, 384], P('sub', 'mode')
- strain_energy: float32 [1536], P(('sub', 'mode'))
Inputs may be any that keep to these rules, and one draw needn't show every extreme that they name: cluster_rows[c, j] = s * 4096 + r names column r of the displacement columns of the leaves of sub index s (its leaves laid end to end). The clusters of sub index d read only from sub indices d - 2 to d + 2 taken around the axis, and at most 384 of their 1536 rows from any one of these indices; that most is reached for every d from one of the five.
All inputs are finite; a program needn't handle non-finite values.
Results may differ from a plain program's by a relative error of at most 0.0029.
Values may be sent and summed in bfloat16 or wider, within the bound.
No kernel may reach another device: no remote copies, remote signals or barrier semaphores. Data moves between devices by JAX's collectives and lax.ppermute only.
A program may use at most 64 MiB of HBM per device.

v0:
```python
import jax
import jax.numpy as jnp
from jax import lax
from jax.sharding import PartitionSpec as P

M = 768


def passed_along(shard, axis, by):
    peers = lax.axis_size(axis)
    return lax.ppermute(shard, axis, [(i, (i + by) % peers) for i in range(peers)])


def from_partner(value, axis, bit):
    mask = 2**bit
    pairs = [(source, source ^ mask) for source in range(lax.axis_size(axis))]
    return lax.ppermute(value, axis, pairs)


def join_halves(mine, partner, upper_half):
    return jnp.where(
        upper_half,
        jnp.concatenate([partner, mine], axis=1),
        jnp.concatenate([mine, partner], axis=1),
    )


def shards(
    leaf_coords,
    leaf_modes,
    constraint_modes,
    sep_one,
    sep_two,
    sep_three,
    cluster_rows,
    operators,
    compliance,
    modal_weight,
):
    sub_index = lax.axis_index("sub")
    sub_count = lax.axis_size("sub")
    mode_cols = leaf_coords.shape[1]
    leaf_count = leaf_coords.shape[0]
    leaf_rows = leaf_modes.shape[2]
    dof_count = leaf_count * leaf_rows
    row_ids = cluster_rows.reshape(-1)
    source_dev = row_ids // dof_count
    local_row = row_ids % dof_count
    distance = (source_dev - sub_index) % sub_count
    slot_offset = jnp.where(distance > sub_count // 2, distance - sub_count, distance)
    slot_total = row_ids.shape[0]
    capacity = slot_total // 4
    wanted_lists = []
    slot_ranks = []
    for offset in (-2, -1, 1, 2):
        slot_mask = slot_offset == offset
        slot_rank = jnp.cumsum(slot_mask.astype(jnp.int32)) - 1
        picks = (slot_rank[None, :] == jnp.arange(capacity, dtype=jnp.int32)[:, None]) & slot_mask[
            None, :
        ]
        wanted = jnp.sum(jnp.where(picks, local_row[None, :], 0), axis=1)
        wanted_lists.append(passed_along(wanted, "sub", offset))
        slot_ranks.append(jnp.clip(slot_rank, 0, capacity - 1))
    direct = jnp.einsum("lmk,lkr->mlr", leaf_coords, leaf_modes, preferred_element_type=jnp.float32)
    pieces = [sep_one, sep_two, sep_three]
    first_part = pieces[0]
    partner = from_partner(first_part, "sub", 0)
    first_part = join_halves(first_part, partner, sub_index & 1 == 1)
    second_part = pieces[1]
    for level_bit in range(2):
        partner = from_partner(second_part, "sub", level_bit)
        second_part = join_halves(second_part, partner, sub_index >> level_bit & 1 == 1)
    third_part = pieces[2]
    for level_bit in range(3):
        partner = from_partner(third_part, "sub", level_bit)
        third_part = join_halves(third_part, partner, sub_index >> level_bit & 1 == 1)
    pieces = [first_part, second_part, third_part]
    ancestry = jnp.stack(pieces, axis=0)
    coupled = jnp.einsum(
        "amb,labr->mlr", ancestry, constraint_modes, preferred_element_type=jnp.float32
    )
    displaced = (direct + coupled).astype(jnp.bfloat16).reshape(mode_cols, dof_count)
    assembled = jnp.where(
        (slot_offset == 0)[None, :],
        jnp.take(displaced, local_row, axis=1),
        jnp.zeros((), jnp.bfloat16),
    )
    for number, offset in enumerate((-2, -1, 1, 2)):
        outgoing = jnp.take(displaced, wanted_lists[number], axis=1)
        returned = passed_along(outgoing, "sub", -offset)
        placed = jnp.take(returned, slot_ranks[number], axis=1)
        assembled = jnp.where((slot_offset == offset)[None, :], placed, assembled)
    cluster_count = operators.shape[0]
    cluster_width = operators.shape[1]
    blocks = assembled.reshape(mode_cols, cluster_count, cluster_width)
    stresses = jnp.einsum("mck,cks->cms", blocks, operators, preferred_element_type=jnp.float32)
    squared = jnp.sum(stresses * stresses * modal_weight[None, :, None], axis=1) * compliance
    energy_terms = jnp.sum(squared.reshape(cluster_count, 6, -1), axis=1) * (0.5 / M)
    strain_energy = lax.psum_scatter(
        energy_terms.reshape(-1), "mode", scatter_dimension=0, tiled=True
    )
    return (stresses, strain_energy)


def solution(mesh):
    return jax.shard_map(
        shards,
        mesh=mesh,
        in_specs=(
            P("sub", "mode", None),
            P("sub", None, None),
            P("sub", None, None, None),
            P("mode", "sub"),
            P("mode", "sub"),
            P("mode", "sub"),
            P("sub", None),
            P("sub", None, None),
            P("sub", None),
            P("mode"),
        ),
        out_specs=(P("sub", "mode", None), P(("sub", "mode"))),
        check_vma=False,
    )
```

profile of v0, /device:TPU:0, one launch (start us, length us, event | category | flops | bytes accessed | tf_op | source)
XLA Modules:
  0.0 107.8 jit_solution(8662409188790933868)
XLA Ops:
  6.2 2.3 %select_reduce_fusion.3 = (s32[384]{0:T(512)S(1)}, s32[384]{0:T(512)S(1)}, s32[384]{0:T(512)S(1)}, s32[384]{0:T(512)S(1)}) fusion(s32[1536]{0:T(1024)S(1)} %get-tuple-element.30, s32[1536]{0:T(1024)S(1)} %get-tuple-element.36, pred[1536]{0:T(1024)(128)(4,1)S(1)} %get-tuple-element.25, pred[1536]{0:T(1024)(128)(4,1)S(1)} %get-tuple-element.23, ...), kind=kLoop, calls=%fused_computation.17 | loop fusion | flops 9435648 | bytes 43008 | tf_op jit(solution)/shard_map/reduce_sum | solution.py:61
  8.5 3.0 %collective-permute-start.6 = (s32[384]{0:T(512)S(1)}, s32[384]{0:T(512)S(1)}, u32[]{:S(2)}, u32[]{:S(2)}) collective-permute-start(s32[384]{0:T(512)S(1)} %get-tuple-element.4), channel_id=1, source_target_pairs={{0,8},{4,12},{8,16},{12,20},{16,24},{20,28},{24,0},{28,4},{1,9},{5... | collective-permute-start | bytes 4616 | tf_op jit(solution)/shard_map/ppermute | solution.py:11
  15.7 3.6 %fusion.23 = f32[8,512,192]{1,2,0:T(8,128)} fusion(bf16[8,192,128]{2,1,0:T(8,128)(2,1)} %param.14, bf16[8,128,512]{2,1,0:T(8,128)(2,1)} %param.15), kind=kOutput, calls=%fused_computation.122 | convolution fusion | flops 201326592 | bytes 4587520 | tf_op jit(solution)/shard_map/lmk,lkr->mlr/dot_general | solution.py:64
  20.3 2.3 %collective-permute-start.4 = (bf16[192,64]{1,0:T(8,128)(2,1)S(1)}, bf16[192,64]{1,0:T(8,128)(2,1)S(1)}, u32[]{:S(2)}, u32[]{:S(2)}) collective-permute-start(bf16[192,64]{1,0:T(8,128)(2,1)S(1)} %maximum_select_fusion.4), channel_id=1, source_target_pairs={{0,8},{4,12},{8,0},{12,4},{16,24},{20,28},{24,16},{28,20},{1,9},{5... | collective-permute-start | bytes 73736 | tf_op jit(solution)/shard_map/ppermute | solution.py:17
  23.1 1.6 %collective-permute-done.4 = bf16[192,64]{1,0:T(8,128)(2,1)S(1)} collective-permute-done((bf16[192,64]{1,0:T(8,128)(2,1)S(1)}, bf16[192,64]{1,0:T(8,128)(2,1)S(1)}, u32[]{:S(2)}, u32[]{:S(2)}) %collective-permute-start.4) | collective-permute-done | bytes 24608 | tf_op jit(solution)/shard_map/ppermute | solution.py:17
  24.8 1.6 %collective-permute-start.5 = (bf16[192,128]{1,0:T(8,128)(2,1)S(1)}, bf16[192,128]{1,0:T(8,128)(2,1)S(1)}, u32[]{:S(2)}, u32[]{:S(2)}) collective-permute-start(bf16[192,128]{1,0:T(8,128)(2,1)S(1)} %maximum_select_fusion.5), channel_id=1, source_target_pairs={{0,16},{4,20},{8,24},{12,28},{16,0},{20,4},{24,8},{28,12},{1,17},{... | collective-permute-start | bytes 147464 | tf_op jit(solution)/shard_map/ppermute | solution.py:17
  26.9 2.0 %collective-permute-done.5 = bf16[192,128]{1,0:T(8,128)(2,1)S(1)} collective-permute-done((bf16[192,128]{1,0:T(8,128)(2,1)S(1)}, bf16[192,128]{1,0:T(8,128)(2,1)S(1)}, u32[]{:S(2)}, u32[]{:S(2)}) %collective-permute-start.5) | collective-permute-done | bytes 49184 | tf_op jit(solution)/shard_map/ppermute | solution.py:17
  28.9 6.3 %fusion = bf16[192,8,512]{2,0,1:T(8,128)(2,1)} fusion(f32[8,512,192]{1,2,0:T(8,128)} %fusion.23, bf16[8,3,256,512]{3,2,1,0:T(8,128)(2,1)} %param.16, bf16[1,192,256]{2,1,0:T(8,128)(2,1)S(1)} %maximum_select_fusion.2, bf16[1,192,256]{2,1,0:T(8,128)(2,1)S(1)} %maximum_select_fusion.1, bf16[1,192,256]{2,1,0:T(8,128)(2,1)S(1)} %maximum_select_fusion), kind=kOutput, calls=%fused_computation.10 | convolution fusion | flops 1210417152 | bytes 11304960 | tf_op jit(solution)/shard_map/amb,labr->mlr/dot_general | solution.py:79
  35.2 2.7 %copy.60 = bf16[192,8,512]{0,2,1:T(8,128)(2,1)S(1)} copy(bf16[192,8,512]{2,0,1:T(8,128)(2,1)} %fusion) | data formatting | bytes 3145728 | tf_op jit(solution)/shard_map/reshape | solution.py:82
  38.0 2.1 %gather_fusion.7 = bf16[384,192]{1,0:T(8,128)(2,1)S(1)} fusion(bf16[192,4096]{0,1:T(8,128)(2,1)S(1)} %bitcast.64, s32[1024]{0:T(1024)S(1)} %pad_clamp_fusion.5), kind=kCustom, calls=%fused_computation.4.clone | custom fusion | bytes 296448 | tf_op jit(solution)/shard_map/jit(_take)/gather | solution.py:89
  40.0 2.6 %gather_fusion.5 = bf16[384,192]{1,0:T(8,128)(2,1)} fusion(bf16[192,4096]{0,1:T(8,128)(2,1)S(1)} %bitcast.65, s32[1024]{0:T(1024)S(1)} %pad_clamp_fusion.6), kind=kCustom, calls=%fused_computation.3.clone | custom fusion | bytes 296448 | tf_op jit(solution)/shard_map/jit(_take)/gather | solution.py:89
  42.6 2.5 %gather_fusion.3 = bf16[384,192]{1,0:T(8,128)(2,1)} fusion(bf16[192,4096]{0,1:T(8,128)(2,1)S(1)} %bitcast.66, s32[1024]{0:T(1024)S(1)} %pad_clamp_fusion.7), kind=kCustom, calls=%fused_computation.2.clone | custom fusion | bytes 296448 | tf_op jit(solution)/shard_map/jit(_take)/gather | solution.py:89
  45.1 2.5 %gather_fusion.1 = bf16[384,192]{1,0:T(8,128)(2,1)} fusion(bf16[192,4096]{0,1:T(8,128)(2,1)S(1)} %bitcast.67, s32[1024]{0:T(1024)S(1)} %pad_clamp_fusion.8), kind=kCustom, calls=%fused_computation.clone | custom fusion | bytes 296448 | tf_op jit(solution)/shard_map/jit(_take)/gather | solution.py:89
  47.7 1.7 %select_bitcast_fusion.3 = bf16[192,384]{0,1:T(8,128)(2,1)} fusion(bf16[384,192]{1,0:T(8,128)(2,1)} %gather_fusion.1, pred[384]{0:T(512)(128)(4,1)S(1)} %compare_and_fusion.8), kind=kLoop, calls=%fused_computation.36 | loop fusion | flops 73728 | bytes 295296 | tf_op jit(solution)/shard_map/jit(_take)/select_n | solution.py:89
  49.4 2.6 %collective-permute-start.7 = (bf16[192,384]{0,1:T(8,128)(2,1)}, bf16[192,384]{0,1:T(8,128)(2,1)S(1)}, u32[]{:S(2)}, u32[]{:S(2)}) collective-permute-start(bf16[192,384]{0,1:T(8,128)(2,1)} %select_bitcast_fusion.3), channel_id=1, source_target_pairs={{0,24},{4,28},{8,0},{12,4},{16,8},{20,12},{24,16},{28,20},{1,25},{... | collective-permute-start | bytes 442376 | tf_op jit(solution)/shard_map/ppermute | solution.py:11
  51.9 1.7 %select_bitcast_fusion.2 = bf16[192,384]{0,1:T(8,128)(2,1)} fusion(bf16[384,192]{1,0:T(8,128)(2,1)} %gather_fusion.3, pred[384]{0:T(512)(128)(4,1)S(1)} %compare_and_fusion.7), kind=kLoop, calls=%fused_computation.35 | loop fusion | flops 73728 | bytes 295296 | tf_op jit(solution)/shard_map/jit(_take)/select_n | solution.py:89
  53.7 1.7 %select_bitcast_fusion.1 = bf16[192,384]{0,1:T(8,128)(2,1)} fusion(bf16[384,192]{1,0:T(8,128)(2,1)} %gather_fusion.5, pred[384]{0:T(512)(128)(4,1)S(1)} %compare_and_fusion.6), kind=kLoop, calls=%fused_computation.34 | loop fusion | flops 73728 | bytes 295296 | tf_op jit(solution)/shard_map/jit(_take)/select_n | solution.py:89
  58.7 5.5 %gather_fusion = bf16[1536,192]{1,0:T(8,128)(2,1)S(1)} fusion(bf16[192,4096]{0,1:T(8,128)(2,1)} %bitcast.68, s32[2048]{0:T(1024)S(1)} %pad_clamp_fusion), kind=kCustom, calls=%fused_computation.8 | custom fusion | bytes 1185792 | tf_op jit(solution)/shard_map/jit(_take)/gather | solution.py:85
  64.9 4.9 %gather_fusion.8 = bf16[1536,192]{1,0:T(8,128)(2,1)S(1)} fusion(bf16[192,384]{0,1:T(8,128)(2,1)S(1)} %collective-permute-done.13, s32[2048]{0:T(1024)} %pad_clamp_fusion.1), kind=kCustom, calls=%fused_computation.7.clone | custom fusion | bytes 1185792 | tf_op jit(solution)/shard_map/jit(_take)/gather | solution.py:91
  69.8 5.5 %gather_fusion.6 = bf16[1536,192]{1,0:T(8,128)(2,1)} fusion(bf16[192,384]{0,1:T(8,128)(2,1)S(1)} %collective-permute-done.11, s32[2048]{0:T(1024)} %pad_clamp_fusion.2), kind=kCustom, calls=%fused_computation.6.clone | custom fusion | bytes 1185792 | tf_op jit(solution)/shard_map/jit(_take)/gather | solution.py:91
  75.3 5.3 %gather_fusion.4 = bf16[1536,192]{1,0:T(8,128)(2,1)} fusion(bf16[192,384]{0,1:T(8,128)(2,1)S(1)} %collective-permute-done.9, s32[2048]{0:T(1024)S(1)} %pad_clamp_fusion.3), kind=kCustom, calls=%fused_computation.5.clone | custom fusion | bytes 1185792 | tf_op jit(solution)/shard_map/jit(_take)/gather | solution.py:91
  80.8 5.4 %gather_fusion.2 = bf16[1536,192]{1,0:T(8,128)(2,1)} fusion(bf16[192,384]{0,1:T(8,128)(2,1)S(1)} %collective-permute-done.7, s32[2048]{0:T(1024)S(1)} %pad_clamp_fusion.4), kind=kCustom, calls=%fused_computation.1.clone | custom fusion | bytes 1185792 | tf_op jit(solution)/shard_map/jit(_take)/gather | solution.py:91
  86.2 7.4 %fusion.7 = bf16[192,1536]{0,1:T(8,128)(2,1)S(1)} fusion(bf16[1536,192]{1,0:T(8,128)(2,1)S(1)} %gather_fusion.8, bf16[1536,192]{1,0:T(8,128)(2,1)} %gather_fusion.6, bf16[1536,192]{1,0:T(8,128)(2,1)} %gather_fusion.4, bf16[1536,192]{1,0:T(8,128)(2,1)} %gather_fusion.2, bf16[1536,192]{1,0:T(8,128)(2,1)S(1)} %gather_fusion, pred[1536]{0:T(1024)(128)(4,1)S(1)} %copy-done.16, ...), kind=kLoop, calls=%fused_computation.27 | loop fusion | flops 2949120 | bytes 3554304 | tf_op jit(solution)/shard_map/jit(_where)/select_n | solution.py:92
  95.3 11.9 %all-reduce = f32[192]{0:T(256)S(1)} all-reduce(f32[192]{0:T(256)S(1)} %mul.30), channel_id=2, replica_groups=mesh['sub'=8,'mode'=4] {'mode'}, use_global_device_ids=true, to_apply=%region_14.17.clone | all-reduce | flops 192 | bytes 1536
  (128 shorter events, 17.3 us)
Async XLA Ops:
  0.6 93.0 %copy-start = (bf16[3,512,384]{2,1,0:T(8,128)(2,1)S(1)}, bf16[3,512,384]{2,1,0:T(8,128)(2,1)}, u32[]{:S(2)}) copy-start(bf16[3,512,384]{2,1,0:T(8,128)(2,1)} %param.21) | copy-start | bytes 3538948
  3.3 10.1 %copy-start.4 = (pred[1536]{0:T(1024)(128)(4,1)}, pred[1536]{0:T(1024)(128)(4,1)S(1)}, u32[]{:S(2)}) copy-start(pred[1536]{0:T(1024)(128)(4,1)S(1)} %get-tuple-element.22) | copy-start | bytes 4612
  3.3 10.1 %copy-start.6 = (pred[1536]{0:T(1024)(128)(4,1)}, pred[1536]{0:T(1024)(128)(4,1)S(1)}, u32[]{:S(2)}) copy-start(pred[1536]{0:T(1024)(128)(4,1)S(1)} %get-tuple-element.23) | copy-start | bytes 4612
  3.3 10.1 %copy-start.8 = (pred[1536]{0:T(1024)(128)(4,1)}, pred[1536]{0:T(1024)(128)(4,1)S(1)}, u32[]{:S(2)}) copy-start(pred[1536]{0:T(1024)(128)(4,1)S(1)} %get-tuple-element.24) | copy-start | bytes 4612
  3.3 10.1 %copy-start.10 = (pred[1536]{0:T(1024)(128)(4,1)}, pred[1536]{0:T(1024)(128)(4,1)S(1)}, u32[]{:S(2)}) copy-start(pred[1536]{0:T(1024)(128)(4,1)S(1)} %get-tuple-element.25) | copy-start | bytes 4612
  8.5 10.8 %collective-permute-start.6 = (s32[384]{0:T(512)S(1)}, s32[384]{0:T(512)S(1)}, u32[]{:S(2)}, u32[]{:S(2)}) collective-permute-start(s32[384]{0:T(512)S(1)} %get-tuple-element.4), channel_id=1, source_target_pairs={{0,8},{4,12},{8,16},{12,20},{16,24},{20,28},{24,0},{28,4},{1,9},{5... | collective-permute-start | bytes 4616 | tf_op jit(solution)/shard_map/ppermute | solution.py:11
  11.5 8.0 %collective-permute-start.12 = (s32[384]{0:T(512)S(1)}, s32[384]{0:T(512)S(1)}, u32[]{:S(2)}, u32[]{:S(2)}) collective-permute-start(s32[384]{0:T(512)S(1)} %get-tuple-element.5), channel_id=1, source_target_pairs={{0,24},{4,28},{8,0},{12,4},{16,8},{20,12},{24,16},{28,20},{1,25},{... | collective-permute-start | bytes 4616 | tf_op jit(solution)/shard_map/ppermute | solution.py:11
  12.5 7.5 %collective-permute-start.10 = (s32[384]{0:T(512)S(1)}, s32[384]{0:T(512)S(1)}, u32[]{:S(2)}, u32[]{:S(2)}) collective-permute-start(s32[384]{0:T(512)S(1)} %get-tuple-element.6), channel_id=1, source_target_pairs={{0,28},{4,0},{8,4},{12,8},{16,12},{20,16},{24,20},{28,24},{1,29},{... | collective-permute-start | bytes 4616 | tf_op jit(solution)/shard_map/ppermute | solution.py:11
  13.4 6.7 %collective-permute-start.8 = (s32[384]{0:T(512)S(1)}, s32[384]{0:T(512)S(1)}, u32[]{:S(2)}, u32[]{:S(2)}) collective-permute-start(s32[384]{0:T(512)S(1)} %get-tuple-element.7), channel_id=1, source_target_pairs={{0,4},{4,8},{8,12},{12,16},{16,20},{20,24},{24,28},{28,0},{1,5},{5... | collective-permute-start | bytes 4616 | tf_op jit(solution)/shard_map/ppermute | solution.py:11
  14.3 5.9 %collective-permute-start.3 = (bf16[192,32]{1,0:T(8,128)(2,1)S(1)}, bf16[192,32]{1,0:T(8,128)(2,1)S(1)}, u32[]{:S(2)}, u32[]{:S(2)}) collective-permute-start(bf16[192,32]{1,0:T(8,128)(2,1)S(1)} %copy.48), channel_id=1, source_target_pairs={{0,4},{4,0},{8,12},{12,8},{16,20},{20,16},{24,28},{28,24},{1,5},{5... | collective-permute-start | bytes 36872 | tf_op jit(solution)/shard_map/ppermute | solution.py:17
  19.4 3.2 %collective-permute-start.1 = (bf16[192,64]{1,0:T(8,128)(2,1)S(1)}, bf16[192,64]{1,0:T(8,128)(2,1)S(1)}, u32[]{:S(2)}, u32[]{:S(2)}) collective-permute-start(bf16[192,64]{1,0:T(8,128)(2,1)S(1)} %copy.45), channel_id=1, source_target_pairs={{0,4},{4,0},{8,12},{12,8},{16,20},{20,16},{24,28},{28,24},{1,5},{5... | collective-permute-start | bytes 73736 | tf_op jit(solution)/shard_map/ppermute | solution.py:17
  19.5 6.8 %collective-permute-start = (bf16[192,128]{1,0:T(8,128)(2,1)S(1)}, bf16[192,128]{1,0:T(8,128)(2,1)S(1)}, u32[]{:S(2)}, u32[]{:S(2)}) collective-permute-start(bf16[192,128]{1,0:T(8,128)(2,1)S(1)} %copy-done.2), channel_id=1, source_target_pairs={{0,4},{4,0},{8,12},{12,8},{16,20},{20,16},{24,28},{28,24},{1,5},{5... | collective-permute-start | bytes 147464 | tf_op jit(solution)/shard_map/ppermute | solution.py:17
  20.3 4.4 %collective-permute-start.4 = (bf16[192,64]{1,0:T(8,128)(2,1)S(1)}, bf16[192,64]{1,0:T(8,128)(2,1)S(1)}, u32[]{:S(2)}, u32[]{:S(2)}) collective-permute-start(bf16[192,64]{1,0:T(8,128)(2,1)S(1)} %maximum_select_fusion.4), channel_id=1, source_target_pairs={{0,8},{4,12},{8,0},{12,4},{16,24},{20,28},{24,16},{28,20},{1,9},{5... | collective-permute-start | bytes 73736 | tf_op jit(solution)/shard_map/ppermute | solution.py:17
  22.7 4.2 %collective-permute-start.2 = (bf16[192,128]{1,0:T(8,128)(2,1)S(1)}, bf16[192,128]{1,0:T(8,128)(2,1)S(1)}, u32[]{:S(2)}, u32[]{:S(2)}) collective-permute-start(bf16[192,128]{1,0:T(8,128)(2,1)S(1)} %maximum_select_fusion.3), channel_id=1, source_target_pairs={{0,8},{4,12},{8,0},{12,4},{16,24},{20,28},{24,16},{28,20},{1,9},{5... | collective-permute-start | bytes 147464 | tf_op jit(solution)/shard_map/ppermute | solution.py:17
  24.8 4.2 %collective-permute-start.5 = (bf16[192,128]{1,0:T(8,128)(2,1)S(1)}, bf16[192,128]{1,0:T(8,128)(2,1)S(1)}, u32[]{:S(2)}, u32[]{:S(2)}) collective-permute-start(bf16[192,128]{1,0:T(8,128)(2,1)S(1)} %maximum_select_fusion.5), channel_id=1, source_target_pairs={{0,16},{4,20},{8,24},{12,28},{16,0},{20,4},{24,8},{28,12},{1,17},{... | collective-permute-start | bytes 147464 | tf_op jit(solution)/shard_map/ppermute | solution.py:17
  37.9 9.7 %copy-start.1 = (bf16[192,8,512]{0,2,1:T(8,128)(2,1)}, bf16[192,8,512]{0,2,1:T(8,128)(2,1)S(1)}, u32[]{:S(2)}) copy-start(bf16[192,8,512]{0,2,1:T(8,128)(2,1)S(1)} %copy.60) | copy-start | bytes 4718596
  42.6 14.3 %copy-start.20 = (u32[32]{0:T(128)S(1)}, u32[32]{0:T(128)}, u32[]{:S(2)}) copy-start(u32[32]{0:T(128)} %constant.122) | copy-start | bytes 388
  49.4 31.4 %collective-permute-start.7 = (bf16[192,384]{0,1:T(8,128)(2,1)}, bf16[192,384]{0,1:T(8,128)(2,1)S(1)}, u32[]{:S(2)}, u32[]{:S(2)}) collective-permute-start(bf16[192,384]{0,1:T(8,128)(2,1)} %select_bitcast_fusion.3), channel_id=1, source_target_pairs={{0,24},{4,28},{8,0},{12,4},{16,8},{20,12},{24,16},{28,20},{1,25},{... | collective-permute-start | bytes 442376 | tf_op jit(solution)/shard_map/ppermute | solution.py:11
  53.7 21.7 %collective-permute-start.9 = (bf16[192,384]{0,1:T(8,128)(2,1)}, bf16[192,384]{0,1:T(8,128)(2,1)S(1)}, u32[]{:S(2)}, u32[]{:S(2)}) collective-permute-start(bf16[192,384]{0,1:T(8,128)(2,1)} %select_bitcast_fusion.2), channel_id=1, source_target_pairs={{0,28},{4,0},{8,4},{12,8},{16,12},{20,16},{24,20},{28,24},{1,29},{... | collective-permute-start | bytes 442376 | tf_op jit(solution)/shard_map/ppermute | solution.py:11
  55.4 14.4 %collective-permute-start.11 = (bf16[192,384]{0,1:T(8,128)(2,1)}, bf16[192,384]{0,1:T(8,128)(2,1)S(1)}, u32[]{:S(2)}, u32[]{:S(2)}) collective-permute-start(bf16[192,384]{0,1:T(8,128)(2,1)} %select_bitcast_fusion.1), channel_id=1, source_target_pairs={{0,4},{4,8},{8,12},{12,16},{16,20},{20,24},{24,28},{28,0},{1,5},{5... | collective-permute-start | bytes 442376 | tf_op jit(solution)/shard_map/ppermute | solution.py:11
  56.0 8.9 %collective-permute-start.13 = (bf16[192,384]{0,1:T(8,128)(2,1)S(1)}, bf16[192,384]{0,1:T(8,128)(2,1)S(1)}, u32[]{:S(2)}, u32[]{:S(2)}) collective-permute-start(bf16[192,384]{0,1:T(8,128)(2,1)S(1)} %select_bitcast_fusion), channel_id=1, source_target_pairs={{0,8},{4,12},{8,16},{12,20},{16,24},{20,28},{24,0},{28,4},{1,9},{5... | collective-permute-start | bytes 442376 | tf_op jit(solution)/shard_map/ppermute | solution.py:11
  80.7 5.5 %copy-start.12 = (pred[1536]{0:T(1024)(128)(4,1)S(1)}, pred[1536]{0:T(1024)(128)(4,1)}, u32[]{:S(2)}) copy-start(pred[1536]{0:T(1024)(128)(4,1)} %get-tuple-element.10) | copy-start | bytes 4612
  80.7 5.5 %copy-start.13 = (pred[1536]{0:T(1024)(128)(4,1)S(1)}, pred[1536]{0:T(1024)(128)(4,1)}, u32[]{:S(2)}) copy-start(pred[1536]{0:T(1024)(128)(4,1)} %get-tuple-element.29) | copy-start | bytes 4612
  86.2 7.4 %copy-start.19 = (f32[192]{0:T(256)S(1)}, f32[192]{0:T(256)}, u32[]{:S(2)}) copy-start(f32[192]{0:T(256)} %param.23) | copy-start | bytes 2308
  (11 other events, 53.4 us)
where the time goes:
time: 109 us; the launch traced here: 108 us
  local copies, waits for them, and re-layouts  44.4 us (41%)
  other arithmetic  20 us (18%)
  starting transfers between devices  13.6 us (12%)
  blocking collectives  11.9 us (11%)
  matrix products  11.3 us (10%)
  waiting for transfers between devices  4.83 us (4%)
  between operations  1.8 us (2%)
    gather x4, local copies, waits for them, and re-layouts, shards(): placed = jnp.take(returned, slot_ranks[number], axis=1)  21.1 us
    unnamed x1, blocking collectives  11.9 us
    gather x4, local copies, waits for them, and re-layouts, shards(): outgoing = jnp.take(displaced, wanted_lists[number], axis=1)  9.69 us
    ppermute x8, starting transfers between devices, passed_along(): lax.ppermute(shard, axis, [(i, (i + by) % peers) for i in range(peers)])  8.24 us
    select_n x1, other arithmetic, shards(): assembled = jnp.where((slot_offset == offset)[None, :], placed, assembled)  7.37 us
    dot_general x1, matrix products, shards(): jnp.einsum('amb,labr->mlr', ancestry, constraint_modes, preferred_element...  6.25 us
    gather x1, local copies, waits for them, and re-layouts, shards(): jnp.take(displaced, local_row, axis=1)  5.51 us
    ppermute x6, starting transfers between devices, from_partner(): return lax.ppermute(value, axis, pairs)  5.38 us
  transfers between devices with their start and end apart: 14, of which 4 were waited for; matrix products, arithmetic and copies ran while one was open for 30% of the time, Pallas kernels for 0%

commit v1 on v0

v1 whole, which is shorter than its diff:
```python
import jax
import jax.numpy as jnp
from jax import lax
from jax.experimental import pallas as pl
from jax.experimental.pallas import tpu as pltpu
from jax.sharding import PartitionSpec as P

VMEM = pltpu.VMEM
SMEM = pltpu.SMEM
OFFSETS = (-2, -1, 0, 1, 2)
REMOTE = (-2, -1, 1, 2)
F32 = jnp.float32
BF16 = jnp.bfloat16


def params(mib):
    return pltpu.CompilerParams(vmem_limit_bytes=mib * 1024 * 1024)


def cost(flops, nbytes):
    return pl.CostEstimate(flops=flops, bytes_accessed=nbytes, transcendentals=0)


def vmem_specs(count):
    return [pl.BlockSpec(memory_space=VMEM)] * count


def shift_by(value, axis, by):
    peers = lax.axis_size(axis)
    return lax.ppermute(value, axis, [(i, (i + by) % peers) for i in range(peers)])


def swap_with(value, axis, mask):
    return lax.ppermute(value, axis, [(i, i ^ mask) for i in range(lax.axis_size(axis))])


def pack_kernel(one_ref, two_ref, three_ref, out_ref):
    wide = one_ref.shape[1]
    mid = two_ref.shape[0]
    out_ref[:wide, :] = one_ref[...].astype(F32).T.astype(BF16)
    out_ref[wide : wide + mid, :] = two_ref[...]
    out_ref[wide + mid :, :] = three_ref[...]


def one_hot(target, first, rows):
    local = target - first
    local = jnp.where((local >= 0) & (local < rows), local, -1).astype(F32).astype(BF16)
    ids = lax.broadcasted_iota(jnp.int32, (rows, target.shape[1]), 0).astype(F32).astype(BF16)
    hit = ids == jnp.broadcast_to(local, ids.shape)
    return jnp.where(hit, jnp.ones((), BF16), jnp.zeros((), BF16))


def index_kernel(sub_count, dof_count, capacity, me_ref, rows_ref, key_ref, wanted_ref):
    clusters, width = rows_ref.shape
    row = rows_ref[...]
    source = lax.div(row, jnp.int32(dof_count))
    local = row - source * dof_count
    distance = source - me_ref[0]
    distance = jnp.where(distance < 0, distance + sub_count, distance)
    offset = jnp.where(distance > sub_count // 2, distance - sub_count, distance)
    before = lax.broadcasted_iota(jnp.int32, (width, width), 0)
    after = lax.broadcasted_iota(jnp.int32, (width, width), 1)
    upper = jnp.where(before <= after, 1.0, 0.0).astype(BF16)
    key = jnp.zeros((clusters, width), F32)
    for number, each in enumerate(OFFSETS):
        mask = jnp.where(offset == each, 1.0, 0.0)
        count = jnp.dot(mask.astype(BF16), upper, preferred_element_type=F32)
        carried = jnp.full((1, 1), float(number * capacity - 1), F32)
        placed = []
        for cluster in range(clusters):
            placed.append(count[cluster : cluster + 1, :] + carried)
            carried = carried + count[cluster : cluster + 1, width - 1 : width]
        key = key + mask * jnp.concatenate(placed, axis=0)
    key = key.astype(jnp.int32)
    key_ref[...] = key
    high = lax.div(local, jnp.int32(64))
    low = local - high * 64
    tile = 128
    for part in range(len(OFFSETS) * capacity // tile):
        total = jnp.zeros((2, tile), F32)
        for cluster in range(clusters):
            pick = one_hot(key[cluster : cluster + 1, :], part * tile, tile)
            values = jnp.concatenate(
                [high[cluster : cluster + 1, :], low[cluster : cluster + 1, :]], axis=0
            )
            total = total + lax.dot_general(
                values.astype(F32).astype(BF16),
                pick,
                (((1,), (1,)), ((), ())),
                preferred_element_type=F32,
            )
        answer = (total[0:1, :] * 64.0 + total[1:2, :]).astype(jnp.int32)
        wanted_ref[:, part * tile : (part + 1) * tile] = answer


def displace_kernel(
    me_ref,
    coords_ref,
    modes_ref,
    couple_ref,
    mine_ref,
    pair_ref,
    next_ref,
    far_ref,
    diag_ref,
    *rest,
):
    flows = len(rest) - 3 >> 1
    wanted = rest[:flows]
    outs = rest[flows : 2 * flows]
    anc_t, disp, total = rest[2 * flows :]
    leaves, modes, inner = coords_ref.shape
    width = modes_ref.shape[2]
    block = couple_ref.shape[2]
    me = me_ref[0]
    core = lax.rem(me, 2)
    chip = lax.rem(lax.div(me, 2), 4)
    half, quarter, eighth = block // 2, block // 4, block // 8

    def put(level, at, rows, value):
        anc_t[pl.ds(pl.multiple_of(level * block + at * rows, rows), rows), :] = value

    for which, ref in ((core, mine_ref), (1 - core, pair_ref)):
        put(0, which, half, ref[:half, :])
        put(1, 2 * lax.rem(chip, 2) + which, quarter, ref[half : half + quarter, :])
        put(2, 2 * chip + which, eighth, ref[half + quarter :, :])
    two = 2 * quarter
    near = chip + 1 - 2 * lax.rem(chip, 2)
    across = lax.rem(chip + 2, 4)
    diagonal = near + 2 - 4 * lax.div(near, 2)
    put(1, 1 - lax.rem(chip, 2), two, next_ref[:two, :])
    put(2, near, 2 * eighth, next_ref[two:, :])
    put(2, across, 2 * eighth, far_ref[...])
    put(2, diagonal, 2 * eighth, diag_ref[...])
    anc = anc_t[...].astype(F32).T.astype(BF16)
    for leaf in range(leaves):
        value = jnp.dot(coords_ref[leaf], modes_ref[leaf], preferred_element_type=F32)
        for level in range(couple_ref.shape[1]):
            value = value + jnp.dot(
                anc[:, level * block : (level + 1) * block],
                couple_ref[leaf, level],
                preferred_element_type=F32,
            )
        disp[:, leaf * width : (leaf + 1) * width] = value.astype(BF16)
    tile = 256
    for flow in range(flows):
        total[...] = jnp.zeros_like(total)
        want = wanted[flow][...]

        def step(part, carry, want=want):
            at = pl.multiple_of(part * tile, tile)
            total[...] += jnp.dot(
                disp[:, pl.ds(at, tile)], one_hot(want, at, tile), preferred_element_type=F32
            )
            return carry

        lax.fori_loop(0, leaves * width // tile, step, 0, unroll=4)
        outs[flow][...] = total[...].astype(BF16)


def permute_kernel(key_ref, operators_ref, out_ref):
    clusters, width, rows = operators_ref.shape
    tile = 128
    for part in range(out_ref.shape[0] // tile):
        for cluster in range(clusters):
            pick = one_hot(key_ref[cluster : cluster + 1, :], part * tile, tile)
            moved = jnp.dot(pick, operators_ref[cluster], preferred_element_type=F32)
            out_ref[
                part * tile : (part + 1) * tile, cluster * rows : (cluster + 1) * rows
            ] = moved.astype(BF16)


def stress_kernel(capacity, scale, weight_ref, compliance_ref, moved_ref, *rest):
    count = len(OFFSETS)
    arrived = rest[:count]
    stress_ref, energy_ref = rest[count:]
    clusters, modes, rows = stress_ref.shape
    points = energy_ref.shape[1]
    weight = weight_ref[...]
    for cluster in range(clusters):
        value = jnp.zeros((modes, rows), F32)
        for number in range(count):
            value = value + jnp.dot(
                arrived[number][...],
                moved_ref[
                    number * capacity : (number + 1) * capacity,
                    cluster * rows : (cluster + 1) * rows,
                ],
                preferred_element_type=F32,
            )
        stress_ref[cluster] = value
        square = jnp.sum(value * value * weight, axis=0, keepdims=True)
        square = square * compliance_ref[cluster : cluster + 1, :]
        term = square[:, :points]
        for part in range(1, rows // points):
            term = term + square[:, part * points : (part + 1) * points]
        energy_ref[cluster : cluster + 1, :] = term * scale


def shards(
    leaf_coords,
    leaf_modes,
    constraint_modes,
    sep_one,
    sep_two,
    sep_three,
    cluster_rows,
    operators,
    compliance,
    modal_weight,
):
    sub_count = lax.axis_size("sub")
    mode_count = lax.axis_size("mode")
    me = lax.axis_index("sub").astype(jnp.int32).reshape(1)
    leaves, modes, inner = leaf_coords.shape
    width = leaf_modes.shape[2]
    dof_count = leaves * width
    levels, block = constraint_modes.shape[1:3]
    clusters, slots = cluster_rows.shape
    rows = operators.shape[2]
    capacity = clusters * slots // 4
    count = len(OFFSETS)
    smem = pl.BlockSpec(memory_space=SMEM)
    vmem = pl.BlockSpec(memory_space=VMEM)

    held = sep_one.shape[1] + sep_two.shape[1] + sep_three.shape[1]
    mine = pl.pallas_call(
        pack_kernel,
        out_shape=jax.ShapeDtypeStruct((held, modes), BF16),
        in_specs=vmem_specs(3),
        out_specs=vmem,
        compiler_params=params(4),
        cost_estimate=cost(10000000, 300000),
        name="pack",
    )(sep_one, sep_two.T, sep_three.T)
    pair = swap_with(mine, "sub", 1)

    key, wanted = pl.pallas_call(
        lambda *refs: index_kernel(sub_count, dof_count, capacity, *refs),
        out_shape=(
            jax.ShapeDtypeStruct((clusters, slots), jnp.int32),
            jax.ShapeDtypeStruct((1, count * capacity), jnp.int32),
        ),
        in_specs=[smem, vmem],
        out_specs=(vmem, vmem),
        compiler_params=params(8),
        cost_estimate=cost(1500000000, 300000),
        name="index",
    )(me, cluster_rows)
    lists = []
    for number, offset in enumerate(OFFSETS):
        piece = wanted[:, number * capacity : (number + 1) * capacity]
        lists.append(shift_by(piece, "sub", offset) if offset else piece)

    odd = lax.rem(me[0], 2) == 1
    first = jnp.where(odd, pair, mine)
    second = jnp.where(odd, mine, pair)
    half, quarter = sep_one.shape[1], sep_two.shape[1]
    both = jnp.concatenate(
        [
            first[half : half + quarter],
            second[half : half + quarter],
            first[half + quarter :],
            second[half + quarter :],
        ],
        axis=0,
    )
    near = swap_with(both, "sub", 2)
    far = swap_with(both[2 * quarter :], "sub", 4)
    diag = swap_with(both[2 * quarter :], "sub", 6)

    picked = pl.pallas_call(
        displace_kernel,
        out_shape=(jax.ShapeDtypeStruct((modes, capacity), BF16),) * count,
        in_specs=[smem] + vmem_specs(8 + count),
        out_specs=(vmem,) * count,
        scratch_shapes=[
            VMEM((levels * block, modes), BF16),
            VMEM((modes, dof_count), BF16),
            VMEM((modes, capacity), F32),
        ],
        compiler_params=params(24),
        cost_estimate=cost(8000000000, 9000000),
        name="displace",
    )(me, leaf_coords, leaf_modes, constraint_modes, mine, pair, near, far, diag, *lists)

    arrived = [
        shift_by(piece, "sub", -offset) if offset else piece
        for piece, offset in zip(picked, OFFSETS)
    ]
    moved = pl.pallas_call(
        permute_kernel,
        out_shape=jax.ShapeDtypeStruct((count * capacity, clusters * rows), BF16),
        in_specs=vmem_specs(2),
        out_specs=vmem,
        compiler_params=params(16),
        cost_estimate=cost(6000000000, 6000000),
        name="permute",
    )(key, operators)

    points = rows // 6
    stresses, energy = pl.pallas_call(
        lambda *refs: stress_kernel(capacity, 0.5 / (modes * mode_count), *refs),
        out_shape=(
            jax.ShapeDtypeStruct((clusters, modes, rows), F32),
            jax.ShapeDtypeStruct((clusters, points), F32),
        ),
        in_specs=vmem_specs(3 + count),
        out_specs=(vmem, vmem),
        compiler_params=params(16),
        cost_estimate=cost(1000000000, 6000000),
        name="stress",
    )(modal_weight.reshape(modes, 1), compliance, moved, *arrived)

    total = energy
    for step in range(1, mode_count):
        total = total + shift_by(energy, "mode", step)
    share = clusters * points // mode_count
    strain_energy = lax.dynamic_slice(
        total.reshape(-1), (lax.axis_index("mode") * share,), (share,)
    )
    return (stresses, strain_energy)


def solution(mesh):
    return jax.shard_map(
        shards,
        mesh=mesh,
        in_specs=(
            P("sub", "mode", None),
            P("sub", None, None),
            P("sub", None, None, None),
            P("mode", "sub"),
            P("mode", "sub"),
            P("mode", "sub"),
            P("sub", None),
            P("sub", None, None),
            P("sub", None),
            P("mode"),
        ),
        out_specs=(P("sub", "mode", None), P(("sub", "mode"))),
        check_vma=False,
    )
```

time: 109 us -> 58.5 us (0.54)
  local copies, waits for them, and re-layouts: 44.4 us -> 9.44 us
  other arithmetic: 20 us -> 0.08 us
  Pallas kernels: 0 us -> 17.7 us
  blocking collectives: 11.9 us -> 0 us
  matrix products: 11.3 us -> 0 us
  waiting for transfers between devices: 4.83 us -> 13.5 us
  starting transfers between devices: 13.6 us -> 16.7 us
    gather x9 -> x0, local copies, waits for them, and re-layouts: 36.3 us -> none  [the longest x4 21.1 us: shards(): placed = jnp.take(returned, slot_ranks[number], axis=1)]
    pallas_call x0 -> x5, Pallas kernels: none -> 17.7 us  [the longest x1 9.6 us: shards(): pl.pallas_call(displace_kernel, out_shape=(jax.ShapeDtypeStruct((modes, c...]
    select_n x20 -> x1, other arithmetic: 13.1 us -> 0.05 us  [shards(): first = jnp.where(odd, pair, mine)]
    unnamed x1 -> x0, blocking collectives: 11.9 us -> none
    dot_general x3 -> x0, matrix products: 11.3 us -> none  [the longest x1 6.25 us: shards(): jnp.einsum('amb,labr->mlr', ancestry, constraint_modes, preferred_element...]
    ppermute x14 -> x15, waiting for transfers between devices: 4.83 us -> 13.5 us  [the longest x11 13.5 us: shift_by(): lax.ppermute(value, axis, [(i, (i + by) % peers) for i in range(peers)])]
    unnamed x47 -> x24, local copies, waits for them, and re-layouts: 2.91 us -> 8.64 us
    reshape x4 -> x2, local copies, waits for them, and re-layouts: 4.32 us -> 0.2 us  [the longest x1 0.12 us: shards(): modal_weight.reshape(modes, 1)]
  transfers between devices with their start and end apart: 14 -> 15, of which waited for: 4 -> 8; matrix products, arithmetic and copies ran while one was open for 30% -> 0% of each run, Pallas kernels for 0% -> 9%
where the time goes in v1:
time: 58.5 us; the launch traced here: 58.2 us
  Pallas kernels  17.7 us (30%)
  starting transfers between devices  16.7 us (29%)
  waiting for transfers between devices  13.5 us (23%)
  local copies, waits for them, and re-layouts  9.44 us (16%)
  between operations  0.8 us (1%)
    ppermute x11, waiting for transfers between devices, shift_by(): lax.ppermute(value, axis, [(i, (i + by) % peers) for i in range(peers)])  13.5 us
    ppermute x11, starting transfers between devices, shift_by(): lax.ppermute(value, axis, [(i, (i + by) % peers) for i in range(peers)])  11.9 us
    pallas_call x1, Pallas kernels, shards(): pl.pallas_call(displace_kernel, out_shape=(jax.ShapeDtypeStruct((modes, c...  9.6 us
    unnamed x24, local copies, waits for them, and re-layouts  8.64 us
    ppermute x4, starting transfers between devices, swap_with(): lax.ppermute(value, axis, [(i, i ^ mask) for i in range(lax.axis_size(axi...  4.79 us
    pallas_call x1, Pallas kernels, shards(): pl.pallas_call(permute_kernel, out_shape=jax.ShapeDtypeStruct((count * ca...  3.22 us
    pallas_call x1, Pallas kernels, shards(): pl.pallas_call(lambda *refs: stress_kernel(capacity, 0.5 / (modes * mode_...  2.44 us
    pallas_call x1, Pallas kernels, shards(): pl.pallas_call(lambda *refs: index_kernel(sub_count, dof_count, capacity,...  2.29 us
  transfers between devices with their start and end apart: 15, of which 8 were waited for; matrix products, arithmetic and copies ran while one was open for 0% of the time, Pallas kernels for 9%

profile of v1, /device:TPU:0, one launch (start us, length us, event | category | flops | bytes accessed | tf_op | source)
XLA Modules:
  0.0 58.2 jit_solution(16776548294383255527)
XLA Ops:
  0.6 0.8 %copy-done.2 = bf16[192,128]{1,0:T(8,128)(2,1)S(1)} copy-done((bf16[192,128]{1,0:T(8,128)(2,1)S(1)}, bf16[192,128]{1,0:T(8,128)(2,1)}, u32[]{:S(2)}) %copy-start.2) | copy-done | bytes 49176
  1.4 0.8 %copy-done.3 = bf16[192,64]{0,1:T(8,128)(2,1)S(1)} copy-done((bf16[192,64]{0,1:T(8,128)(2,1)S(1)}, bf16[192,64]{0,1:T(8,128)(2,1)}, u32[]{:S(2)}) %copy-start.3) | copy-done | bytes 24600
  2.2 0.7 %copy-done.4 = bf16[192,32]{0,1:T(8,128)(2,1)S(1)} copy-done((bf16[192,32]{0,1:T(8,128)(2,1)S(1)}, bf16[192,32]{0,1:T(8,128)(2,1)}, u32[]{:S(2)}) %copy-start.4) | copy-done | bytes 12312
  3.6 0.8 %copy-done.10 = s32[3,512]{1,0:T(4,128)S(1)} copy-done((s32[3,512]{1,0:T(4,128)S(1)}, s32[3,512]{1,0:T(4,128)}, u32[]{:S(2)}) %copy-start.10) | copy-done | bytes 6168
  4.4 2.3 %index.1 = (s32[3,512]{1,0:T(4,128)S(1)}, s32[1,1920]{1,0:T(1,128)S(1)}) custom-call(s32[1]{0:T(128)} %bitcast.1.refs_0_.me_ref, s32[3,512]{1,0:T(4,128)S(1)} %copy-done.10), custom_call_target="tpu_custom_call" | custom-call | flops 1500000000 | bytes 300000 | tf_op jit(solution)/shard_map/index/pallas_call | solution.py:238
  6.8 3.5 %collective-permute-start.3 = (bf16[64,192]{1,0:T(8,128)(2,1)S(1)}, bf16[64,192]{1,0:T(8,128)(2,1)S(1)}, u32[]{:S(2)}, u32[]{:S(2)}) collective-permute-start(bf16[64,192]{1,0:T(8,128)(2,1)S(1)} %pad_maximum_fusion.1), channel_id=1, source_target_pairs={{0,24},{4,28},{8,16},{12,20},{16,8},{20,12},{24,0},{28,4},{1,25},{... | collective-permute-start | bytes 73736 | tf_op jit(solution)/shard_map/ppermute | solution.py:34
  11.1 1.9 %collective-permute-start.7 = (s32[1,384]{1,0:T(1,128)S(1)}, s32[1,384]{1,0:T(1,128)S(1)}, u32[]{:S(2)}, u32[]{:S(2)}) collective-permute-start(s32[1,384]{1,0:T(1,128)S(1)} %get-tuple-element.22), channel_id=1, source_target_pairs={{0,8},{4,12},{8,16},{12,20},{16,24},{20,28},{24,0},{28,4},{1,9},{5... | collective-permute-start | bytes 4616 | tf_op jit(solution)/shard_map/ppermute | solution.py:30
  13.0 3.6 %collective-permute-done.7.rest_4_ = s32[1,384]{1,0:T(1,128)S(1)} collective-permute-done((s32[1,384]{1,0:T(1,128)S(1)}, s32[1,384]{1,0:T(1,128)S(1)}, u32[]{:S(2)}, u32[]{:S(2)}) %collective-permute-start.7) | collective-permute-done | bytes 1568 | tf_op jit(solution)/shard_map/ppermute | solution.py:30
  16.9 0.6 %collective-permute-start.4 = (s32[1,384]{1,0:T(1,128)S(1)}, s32[1,384]{1,0:T(1,128)S(1)}, u32[]{:S(2)}, u32[]{:S(2)}) collective-permute-start(s32[1,384]{1,0:T(1,128)S(1)} %get-tuple-element.26), channel_id=1, source_target_pairs={{0,24},{4,28},{8,0},{12,4},{16,8},{20,12},{24,16},{28,20},{1,25},{... | collective-permute-start | bytes 4616 | tf_op jit(solution)/shard_map/ppermute | solution.py:30
  17.9 2.6 %collective-permute-done.4.rest_0_ = s32[1,384]{1,0:T(1,128)S(1)} collective-permute-done((s32[1,384]{1,0:T(1,128)S(1)}, s32[1,384]{1,0:T(1,128)S(1)}, u32[]{:S(2)}, u32[]{:S(2)}) %collective-permute-start.4) | collective-permute-done | bytes 1568 | tf_op jit(solution)/shard_map/ppermute | solution.py:30
  20.5 1.2 %copy-done.8 = bf16[8,128,512]{2,1,0:T(8,128)(2,1)S(1)} copy-done((bf16[8,128,512]{2,1,0:T(8,128)(2,1)S(1)}, bf16[8,128,512]{2,1,0:T(8,128)(2,1)}, u32[]{:S(2)}) %copy-start.8) | copy-done | bytes 1048600
  21.7 9.6 %displace.1 = (bf16[192,384]{1,0:T(8,128)(2,1)S(1)}, bf16[192,384]{1,0:T(8,128)(2,1)S(1)}, bf16[192,384]{1,0:T(8,128)(2,1)S(1)}, bf16[192,384]{1,0:T(8,128)(2,1)S(1)}, bf16[192,384]{1,0:T(8,128)(2,1)S(1)}) custom-call(s32[1]{0:T(128)} %bitcast.1.refs_0_.me_ref, bf16[8,192,128]{2,1,0:T(8,128)(2,1)S(1)} %copy-done.9, bf16[8,128,512]{2,1,0:T(8,128)(2,1)S(1)} %copy-done.8, ...), custom_call_target="tpu_custom_call" | custom-call | flops 8000000000 | bytes 9000000 | tf_op jit(solution)/shard_map/displace/pallas_call | solution.py:272
  31.3 1.5 %collective-permute-start.8 = (bf16[192,384]{1,0:T(8,128)(2,1)S(1)}, bf16[192,384]{1,0:T(8,128)(2,1)S(1)}, u32[]{:S(2)}, u32[]{:S(2)}) collective-permute-start(bf16[192,384]{1,0:T(8,128)(2,1)S(1)} %get-tuple-element.13), channel_id=1, source_target_pairs={{0,8},{4,12},{8,16},{12,20},{16,24},{20,28},{24,0},{28,4},{1,9},{5... | collective-permute-start | bytes 442376 | tf_op jit(solution)/shard_map/ppermute | solution.py:30
  32.9 2.6 %collective-permute-start.10 = (bf16[192,384]{1,0:T(8,128)(2,1)S(1)}, bf16[192,384]{1,0:T(8,128)(2,1)S(1)}, u32[]{:S(2)}, u32[]{:S(2)}) collective-permute-start(bf16[192,384]{1,0:T(8,128)(2,1)S(1)} %get-tuple-element.16), channel_id=1, source_target_pairs={{0,28},{4,0},{8,4},{12,8},{16,12},{20,16},{24,20},{28,24},{1,29},{... | collective-permute-start | bytes 442376 | tf_op jit(solution)/shard_map/ppermute | solution.py:30
  36.1 3.2 %permute.1.refs_2_ = bf16[1920,1152]{1,0:T(8,128)(2,1)S(1)} custom-call(s32[3,512]{1,0:T(4,128)S(1)} %get-tuple-element.11.key_ref, bf16[3,512,384]{2,1,0:T(8,128)(2,1)S(1)} %copy-done.7), custom_call_target="tpu_custom_call" | custom-call | flops 6000000000 | bytes 6000000 | tf_op jit(solution)/shard_map/permute/pallas_call | solution.py:291
  39.3 2.0 %copy-done = bf16[1920,1152]{1,0:T(8,128)(2,1)} copy-done((bf16[1920,1152]{1,0:T(8,128)(2,1)}, bf16[1920,1152]{1,0:T(8,128)(2,1)S(1)}, u32[]{:S(2)}) %copy-start) | copy-done | bytes 4423704
  41.5 2.3 %collective-permute-done.11.refs_7_ = bf16[192,384]{1,0:T(8,128)(2,1)S(1)} collective-permute-done((bf16[192,384]{1,0:T(8,128)(2,1)S(1)}, bf16[192,384]{1,0:T(8,128)(2,1)S(1)}, u32[]{:S(2)}, u32[]{:S(2)}) %collective-permute-start.11) | collective-permute-done | bytes 147488 | tf_op jit(solution)/shard_map/ppermute | solution.py:30
  43.8 2.3 %copy-done.1 = bf16[1920,1152]{1,0:T(8,128)(2,1)S(1)} copy-done((bf16[1920,1152]{1,0:T(8,128)(2,1)S(1)}, bf16[1920,1152]{1,0:T(8,128)(2,1)}, u32[]{:S(2)}) %copy-start.1) | copy-done | bytes 4423704
  46.1 2.4 %stress.1 = (f32[3,192,384]{2,1,0:T(8,128)}, f32[3,64]{1,0:T(4,128)S(1)}) custom-call(f32[192,1]{1,0:T(8,128)S(1)} %copy.12.refs_0_, f32[3,384]{1,0:T(4,128)S(1)} %copy-done.5, bf16[1920,1152]{1,0:T(8,128)(2,1)S(1)} %copy-done.1, bf16[192,384]{1,0:T(8,128)(2,1)S(1)} %collective-permute-done.8.refs_3_, bf16[192,384]{1,0:T(8,128)(2,1)S(1)} %collective-permute-done.9.refs_4_, ...), custom_call_target="tpu_custom_call" | custom-call | flops 1000000000 | bytes 6000000 | tf_op jit(solution)/shard_map/stress/pallas_call | solution.py:302
  48.5 3.6 %collective-permute-start.14 = (f32[3,64]{1,0:T(4,128)S(1)}, f32[3,64]{1,0:T(4,128)S(1)}, u32[]{:S(2)}, u32[]{:S(2)}) collective-permute-start(f32[3,64]{1,0:T(4,128)S(1)} %get-tuple-element.19), channel_id=1, source_target_pairs={{0,3},{1,0},{2,1},{3,2},{4,7},{5,4},{6,5},{7,6},{8,11},{9,8},{10,9... | collective-permute-start | bytes 2312 | tf_op jit(solution)/shard_map/ppermute | solution.py:30
  52.1 1.0 %collective-permute-start.12 = (f32[3,64]{1,0:T(4,128)S(1)}, f32[3,64]{1,0:T(4,128)S(1)}, u32[]{:S(2)}, u32[]{:S(2)}) collective-permute-start(f32[3,64]{1,0:T(4,128)S(1)} %get-tuple-element.19), channel_id=1, source_target_pairs={{0,1},{1,2},{2,3},{3,0},{4,5},{5,6},{6,7},{7,4},{8,9},{9,10},{10,1... | collective-permute-start | bytes 2312 | tf_op jit(solution)/shard_map/ppermute | solution.py:30
  53.4 3.2 %collective-permute-done.13 = f32[3,64]{1,0:T(4,128)S(1)} collective-permute-done((f32[3,64]{1,0:T(4,128)S(1)}, f32[3,64]{1,0:T(4,128)S(1)}, u32[]{:S(2)}, u32[]{:S(2)}) %collective-permute-start.13) | collective-permute-done | bytes 800 | tf_op jit(solution)/shard_map/ppermute | solution.py:30
  56.6 0.9 %collective-permute-done.12 = f32[3,64]{1,0:T(4,128)S(1)} collective-permute-done((f32[3,64]{1,0:T(4,128)S(1)}, f32[3,64]{1,0:T(4,128)S(1)}, u32[]{:S(2)}, u32[]{:S(2)}) %collective-permute-start.12) | collective-permute-done | bytes 800 | tf_op jit(solution)/shard_map/ppermute | solution.py:30
  57.6 0.6 %dynamic_slice.3 = f32[48]{0:T(128)} dynamic-slice(f32[192]{0:T(256)S(1)} %reshape.15, s32[]{:T(128)S(6)} %select_n.18), dynamic_slice_sizes={48} | dynamic-slice | bytes 388 | tf_op jit(solution)/shard_map/dynamic_slice | solution.py:319
  (47 shorter events, 3.2 us)
Async XLA Ops:
  2.9 17.6 %copy-start.9 = (bf16[8,192,128]{2,1,0:T(8,128)(2,1)S(1)}, bf16[8,192,128]{2,1,0:T(8,128)(2,1)}, u32[]{:S(2)}) copy-start(bf16[8,192,128]{2,1,0:T(8,128)(2,1)} %coords_ref.1) | copy-start | bytes 1179652
  3.0 3.7 %collective-permute-start = (bf16[224,192]{1,0:T(8,128)(2,1)S(1)}, bf16[224,192]{1,0:T(8,128)(2,1)S(1)}, u32[]{:S(2)}, u32[]{:S(2)}) collective-permute-start(bf16[224,192]{1,0:T(8,128)(2,1)S(1)} %pack.1.mine_ref), channel_id=1, source_target_pairs={{0,4},{4,0},{8,12},{12,8},{16,20},{20,16},{24,28},{28,24},{1,5},{5... | collective-permute-start | bytes 258056 | tf_op jit(solution)/shard_map/ppermute | solution.py:34
  3.6 16.9 %copy-start.6 = (bf16[8,3,256,512]{3,2,1,0:T(8,128)(2,1)S(1)}, bf16[8,3,256,512]{3,2,1,0:T(8,128)(2,1)}, u32[]{:S(2)}) copy-start(bf16[8,3,256,512]{3,2,1,0:T(8,128)(2,1)} %couple_ref.1) | copy-start | bytes 18874372
  3.6 0.8 %copy-start.10 = (s32[3,512]{1,0:T(4,128)S(1)}, s32[3,512]{1,0:T(4,128)}, u32[]{:S(2)}) copy-start(s32[3,512]{1,0:T(4,128)} %refs_1_.2) | copy-start | bytes 18436
  6.8 13.6 %collective-permute-start.3 = (bf16[64,192]{1,0:T(8,128)(2,1)S(1)}, bf16[64,192]{1,0:T(8,128)(2,1)S(1)}, u32[]{:S(2)}, u32[]{:S(2)}) collective-permute-start(bf16[64,192]{1,0:T(8,128)(2,1)S(1)} %pad_maximum_fusion.1), channel_id=1, source_target_pairs={{0,24},{4,28},{8,16},{12,20},{16,8},{20,12},{24,0},{28,4},{1,25},{... | collective-permute-start | bytes 73736 | tf_op jit(solution)/shard_map/ppermute | solution.py:34
  10.4 10.1 %collective-permute-start.2 = (bf16[64,192]{1,0:T(8,128)(2,1)S(1)}, bf16[64,192]{1,0:T(8,128)(2,1)S(1)}, u32[]{:S(2)}, u32[]{:S(2)}) collective-permute-start(bf16[64,192]{1,0:T(8,128)(2,1)S(1)} %pad_maximum_fusion.1), channel_id=1, source_target_pairs={{0,16},{4,20},{8,24},{12,28},{16,0},{20,4},{24,8},{28,12},{1,17},{... | collective-permute-start | bytes 73736 | tf_op jit(solution)/shard_map/ppermute | solution.py:34
  10.9 9.6 %collective-permute-start.1 = (bf16[192,192]{1,0:T(8,128)(2,1)S(1)}, bf16[192,192]{1,0:T(8,128)(2,1)S(1)}, u32[]{:S(2)}, u32[]{:S(2)}) collective-permute-start(bf16[192,192]{1,0:T(8,128)(2,1)S(1)} %pad_maximum_fusion), channel_id=1, source_target_pairs={{0,8},{4,12},{8,0},{12,4},{16,24},{20,28},{24,16},{28,20},{1,9},{5... | collective-permute-start | bytes 221192 | tf_op jit(solution)/shard_map/ppermute | solution.py:34
  11.1 5.5 %collective-permute-start.7 = (s32[1,384]{1,0:T(1,128)S(1)}, s32[1,384]{1,0:T(1,128)S(1)}, u32[]{:S(2)}, u32[]{:S(2)}) collective-permute-start(s32[1,384]{1,0:T(1,128)S(1)} %get-tuple-element.22), channel_id=1, source_target_pairs={{0,8},{4,12},{8,16},{12,20},{16,24},{20,28},{24,0},{28,4},{1,9},{5... | collective-permute-start | bytes 4616 | tf_op jit(solution)/shard_map/ppermute | solution.py:30
  13.0 3.9 %collective-permute-start.6 = (s32[1,384]{1,0:T(1,128)S(1)}, s32[1,384]{1,0:T(1,128)S(1)}, u32[]{:S(2)}, u32[]{:S(2)}) collective-permute-start(s32[1,384]{1,0:T(1,128)S(1)} %get-tuple-element.23), channel_id=1, source_target_pairs={{0,4},{4,8},{8,12},{12,16},{16,20},{20,24},{24,28},{28,0},{1,5},{5... | collective-permute-start | bytes 4616 | tf_op jit(solution)/shard_map/ppermute | solution.py:30
  16.6 1.3 %collective-permute-start.5 = (s32[1,384]{1,0:T(1,128)S(1)}, s32[1,384]{1,0:T(1,128)S(1)}, u32[]{:S(2)}, u32[]{:S(2)}) collective-permute-start(s32[1,384]{1,0:T(1,128)S(1)} %get-tuple-element.25), channel_id=1, source_target_pairs={{0,28},{4,0},{8,4},{12,8},{16,12},{20,16},{24,20},{28,24},{1,29},{... | collective-permute-start | bytes 4616 | tf_op jit(solution)/shard_map/ppermute | solution.py:30
  16.9 3.6 %collective-permute-start.4 = (s32[1,384]{1,0:T(1,128)S(1)}, s32[1,384]{1,0:T(1,128)S(1)}, u32[]{:S(2)}, u32[]{:S(2)}) collective-permute-start(s32[1,384]{1,0:T(1,128)S(1)} %get-tuple-element.26), channel_id=1, source_target_pairs={{0,24},{4,28},{8,0},{12,4},{16,8},{20,12},{24,16},{28,20},{1,25},{... | collective-permute-start | bytes 4616 | tf_op jit(solution)/shard_map/ppermute | solution.py:30
  20.5 1.2 %copy-start.8 = (bf16[8,128,512]{2,1,0:T(8,128)(2,1)S(1)}, bf16[8,128,512]{2,1,0:T(8,128)(2,1)}, u32[]{:S(2)}) copy-start(bf16[8,128,512]{2,1,0:T(8,128)(2,1)} %modes_ref.1) | copy-start | bytes 3145732
  21.7 14.3 %copy-start.7 = (bf16[3,512,384]{2,1,0:T(8,128)(2,1)S(1)}, bf16[3,512,384]{2,1,0:T(8,128)(2,1)}, u32[]{:S(2)}) copy-start(bf16[3,512,384]{2,1,0:T(8,128)(2,1)} %operators_ref.1) | copy-start | bytes 3538948
  31.3 10.1 %collective-permute-start.8 = (bf16[192,384]{1,0:T(8,128)(2,1)S(1)}, bf16[192,384]{1,0:T(8,128)(2,1)S(1)}, u32[]{:S(2)}, u32[]{:S(2)}) collective-permute-start(bf16[192,384]{1,0:T(8,128)(2,1)S(1)} %get-tuple-element.13), channel_id=1, source_target_pairs={{0,8},{4,12},{8,16},{12,20},{16,24},{20,28},{24,0},{28,4},{1,9},{5... | collective-permute-start | bytes 442376 | tf_op jit(solution)/shard_map/ppermute | solution.py:30
  32.9 8.6 %collective-permute-start.9 = (bf16[192,384]{1,0:T(8,128)(2,1)S(1)}, bf16[192,384]{1,0:T(8,128)(2,1)S(1)}, u32[]{:S(2)}, u32[]{:S(2)}) collective-permute-start(bf16[192,384]{1,0:T(8,128)(2,1)S(1)} %get-tuple-element.14), channel_id=1, source_target_pairs={{0,4},{4,8},{8,12},{12,16},{16,20},{20,24},{24,28},{28,0},{1,5},{5... | collective-permute-start | bytes 442376 | tf_op jit(solution)/shard_map/ppermute | solution.py:30
  32.9 8.6 %collective-permute-start.10 = (bf16[192,384]{1,0:T(8,128)(2,1)S(1)}, bf16[192,384]{1,0:T(8,128)(2,1)S(1)}, u32[]{:S(2)}, u32[]{:S(2)}) collective-permute-start(bf16[192,384]{1,0:T(8,128)(2,1)S(1)} %get-tuple-element.16), channel_id=1, source_target_pairs={{0,28},{4,0},{8,4},{12,8},{16,12},{20,16},{24,20},{28,24},{1,29},{... | collective-permute-start | bytes 442376 | tf_op jit(solution)/shard_map/ppermute | solution.py:30
  35.5 8.3 %collective-permute-start.11 = (bf16[192,384]{1,0:T(8,128)(2,1)S(1)}, bf16[192,384]{1,0:T(8,128)(2,1)S(1)}, u32[]{:S(2)}, u32[]{:S(2)}) collective-permute-start(bf16[192,384]{1,0:T(8,128)(2,1)S(1)} %get-tuple-element.17), channel_id=1, source_target_pairs={{0,24},{4,28},{8,0},{12,4},{16,8},{20,12},{24,16},{28,20},{1,25},{... | collective-permute-start | bytes 442376 | tf_op jit(solution)/shard_map/ppermute | solution.py:30
  36.1 5.3 %copy-start.11 = (f32[192]{0:T(256)S(1)}, f32[192]{0:T(256)}, u32[]{:S(2)}) copy-start(f32[192]{0:T(256)} %param.19) | copy-start | bytes 2308
  36.1 7.7 %copy-start.5 = (f32[3,384]{1,0:T(4,128)S(1)}, f32[3,384]{1,0:T(4,128)}, u32[]{:S(2)}) copy-start(f32[3,384]{1,0:T(4,128)} %refs_1_.3) | copy-start | bytes 13828
  39.3 2.0 %copy-start = (bf16[1920,1152]{1,0:T(8,128)(2,1)}, bf16[1920,1152]{1,0:T(8,128)(2,1)S(1)}, u32[]{:S(2)}) copy-start(bf16[1920,1152]{1,0:T(8,128)(2,1)S(1)} %permute.1.refs_2_) | copy-start | bytes 13271044
  43.8 2.3 %copy-start.1 = (bf16[1920,1152]{1,0:T(8,128)(2,1)S(1)}, bf16[1920,1152]{1,0:T(8,128)(2,1)}, u32[]{:S(2)}) copy-start(bf16[1920,1152]{1,0:T(8,128)(2,1)} %copy-done) | copy-start | bytes 13271044
  48.5 4.9 %collective-permute-start.14 = (f32[3,64]{1,0:T(4,128)S(1)}, f32[3,64]{1,0:T(4,128)S(1)}, u32[]{:S(2)}, u32[]{:S(2)}) collective-permute-start(f32[3,64]{1,0:T(4,128)S(1)} %get-tuple-element.19), channel_id=1, source_target_pairs={{0,3},{1,0},{2,1},{3,2},{4,7},{5,4},{6,5},{7,6},{8,11},{9,8},{10,9... | collective-permute-start | bytes 2312 | tf_op jit(solution)/shard_map/ppermute | solution.py:30
  52.1 4.5 %collective-permute-start.13 = (f32[3,64]{1,0:T(4,128)S(1)}, f32[3,64]{1,0:T(4,128)S(1)}, u32[]{:S(2)}, u32[]{:S(2)}) collective-permute-start(f32[3,64]{1,0:T(4,128)S(1)} %get-tuple-element.19), channel_id=1, source_target_pairs={{0,2},{1,3},{2,0},{3,1},{4,6},{5,7},{6,4},{7,5},{8,10},{9,11},{10,... | collective-permute-start | bytes 2312 | tf_op jit(solution)/shard_map/ppermute | solution.py:30
  52.1 5.4 %collective-permute-start.12 = (f32[3,64]{1,0:T(4,128)S(1)}, f32[3,64]{1,0:T(4,128)S(1)}, u32[]{:S(2)}, u32[]{:S(2)}) collective-permute-start(f32[3,64]{1,0:T(4,128)S(1)} %get-tuple-element.19), channel_id=1, source_target_pairs={{0,1},{1,2},{2,3},{3,0},{4,5},{5,6},{6,7},{7,4},{8,9},{9,10},{10,1... | collective-permute-start | bytes 2312 | tf_op jit(solution)/shard_map/ppermute | solution.py:30
  (3 other events, 2.3 us)

commit v2 on v0

v2 whole, which is shorter than its diff:
```python
import jax
import jax.numpy as jnp
from jax import lax
from jax.experimental import pallas as pl
from jax.experimental.pallas import tpu as pltpu
from jax.sharding import PartitionSpec as P

VMEM = pltpu.VMEM
F32 = jnp.float32
BF16 = jnp.bfloat16
I32 = jnp.int32
BASE = 64
GROUP = 4

PLUS, MINUS, PAIR, OWN, CROSS = range(5)


def shift_by(value, axis, by):
    peers = lax.axis_size(axis)
    return lax.ppermute(value, axis, [(i, (i + by) % peers) for i in range(peers)])


def swap_with(value, axis, mask):
    return lax.ppermute(value, axis, [(i, i ^ mask) for i in range(lax.axis_size(axis))])


def swap_across(value, axis):
    peers = lax.axis_size(axis)
    return lax.ppermute(
        value, axis, [(i, (i + 2 * (i % 2) - 1) % peers) for i in range(peers)]
    )


def call(kernel, name, inputs, outputs, mib, flops, specs=None, scratch=()):
    vmem = pl.BlockSpec(memory_space=VMEM)
    many = isinstance(outputs, tuple)
    nbytes = sum(x.size * x.dtype.itemsize for x in inputs)
    return pl.pallas_call(
        kernel,
        out_shape=outputs,
        in_specs=specs or [vmem] * len(inputs),
        out_specs=(vmem,) * len(outputs) if many else vmem,
        scratch_shapes=list(scratch),
        compiler_params=pltpu.CompilerParams(vmem_limit_bytes=mib * 1024 * 1024),
        cost_estimate=pl.CostEstimate(flops=flops, bytes_accessed=nbytes, transcendentals=0),
        name=name,
    )(*inputs)


def one_hot(target, first, rows):
    local = target - first
    local = jnp.where((local >= 0) & (local < rows), local, -1).astype(F32).astype(BF16)
    ids = lax.broadcasted_iota(I32, (rows, target.shape[1]), 0).astype(F32).astype(BF16)
    hit = ids == jnp.broadcast_to(local, ids.shape)
    return jnp.where(hit, jnp.ones((), BF16), jnp.zeros((), BF16))


def list_rows(key, digits, group, capacity):
    clusters = len(digits)
    parts = []
    tile = 128
    for part in range(capacity // tile):
        total = jnp.zeros((2, tile), F32)
        for cluster in range(clusters):
            pick = one_hot(key[cluster : cluster + 1, :], group * capacity + part * tile, tile)
            total = total + lax.dot_general(
                digits[cluster], pick, (((1,), (1,)), ((), ())), preferred_element_type=F32
            )
        parts.append(total)
    return [part[0:1, :] for part in parts] + [part[1:2, :] for part in parts]


def digit_rows(local, clusters):
    high = lax.div(local, jnp.int32(BASE))
    low = local - high * BASE
    return [
        jnp.concatenate([high[c : c + 1, :], low[c : c + 1, :]], axis=0).astype(F32).astype(BF16)
        for c in range(clusters)
    ]


def filled(rows, count):
    lanes = rows[0].shape[1]
    rest = count - sum(row.shape[0] for row in rows)
    return jnp.concatenate(rows + [jnp.zeros((rest, lanes), F32)], axis=0)


def unpacked(block, start, capacity):
    parts = capacity // 128
    block = block.astype(F32)
    high = [block[start + i : start + i + 1, :] for i in range(parts)]
    low = [block[start + parts + i : start + parts + i + 1, :] for i in range(parts)]
    wanted = jnp.concatenate(high, axis=1) * float(BASE) + jnp.concatenate(low, axis=1)
    return wanted.astype(I32)


def list_height(capacity, lists):
    return (2 * capacity // 128 * lists + 15) // 16 * 16


def prep_kernel(
    sub_count,
    dof_count,
    capacity,
    me_ref,
    one_hbm,
    two_hbm,
    three_hbm,
    rows_hbm,
    out_ref,
    key_ref,
    local_ref,
    one_ref,
    two_ref,
    three_ref,
    rows_ref,
    sems,
):
    moves = [
        pltpu.make_async_copy(source, target, sems.at[number])
        for number, (source, target) in enumerate(
            (
                (rows_hbm, rows_ref),
                (one_hbm, one_ref),
                (two_hbm, two_ref),
                (three_hbm, three_ref),
            )
        )
    ]
    for move in moves:
        move.start()
    clusters, width = rows_ref.shape
    before = lax.broadcasted_iota(I32, (width, width), 0)
    after = lax.broadcasted_iota(I32, (width, width), 1)
    upper = jnp.where(before <= after, 1.0, 0.0).astype(BF16)
    moves[0].wait()
    row = rows_ref[...]
    me = me_ref[0]
    odd = lax.rem(me, 2)
    source = lax.div(row, jnp.int32(dof_count))
    local = row - source * dof_count
    distance = source - me
    distance = jnp.where(distance < 0, distance + sub_count, distance)
    offset = jnp.where(distance > sub_count // 2, distance - sub_count, distance)
    cross = 2 * odd - 1
    masks = [
        jnp.where(offset == each, 1.0, 0.0) for each in (2, -2, -cross, 0, cross)
    ]
    key = jnp.zeros((clusters, width), F32)
    for number, mask in enumerate(masks):
        count = jnp.dot(mask.astype(BF16), upper, preferred_element_type=F32)
        carried = jnp.full((1, 1), float(number * capacity - 1), F32)
        placed = []
        for cluster in range(clusters):
            placed.append(count[cluster : cluster + 1, :] + carried)
            carried = carried + count[cluster : cluster + 1, width - 1 : width]
        key = key + mask * jnp.concatenate(placed, axis=0)
    key = key.astype(I32)
    key_ref[...] = key
    local_ref[...] = local
    digits = digit_rows(local, clusters)
    rows = list_rows(key, digits, PAIR, capacity) + list_rows(key, digits, CROSS, capacity)
    wide, mid, small = one_ref.shape[1], two_ref.shape[0], three_ref.shape[0]
    head = wide + mid + small
    tail = list_height(capacity, 2)
    out_ref[head : head + tail, :] = jnp.zeros((tail, out_ref.shape[1]), BF16)
    out_ref[head : head + tail, :128] = filled(rows, tail).astype(BF16)
    for move in moves[1:]:
        move.wait()
    out_ref[:wide, :] = one_ref[...].astype(F32).T.astype(BF16)
    out_ref[wide : wide + mid, :] = two_ref[...]
    out_ref[wide + mid : head, :] = three_ref[...]


def lists_kernel(capacity, key_ref, local_ref, out_ref):
    clusters = key_ref.shape[0]
    key = key_ref[...]
    digits = digit_rows(local_ref[...], clusters)
    height = list_height(capacity, 1)
    for number, group in enumerate((PLUS, MINUS, OWN)):
        rows = list_rows(key, digits, group, capacity)
        out_ref[number * height : (number + 1) * height, :] = filled(rows, height).astype(BF16)


def relay_kernel(
    capacity, half, quarter, eighth, me_ref, mine_ref, pair_ref, lists_ref, up_ref, down_ref, far_ref
):
    odd = lax.rem(me_ref[0], 2)
    two = half
    three = half + quarter
    head = three + eighth
    tall = 2 * capacity // 128

    def put(ref, at, rows, which, value):
        ref[pl.ds(pl.multiple_of(at + which * rows, rows), rows), :] = value

    for which, ref in ((odd, mine_ref), (1 - odd, pair_ref)):
        for target in (up_ref, down_ref):
            put(target, 0, quarter, which, ref[two:three, :])
            put(target, 2 * quarter, eighth, which, ref[three:head, :])
        put(far_ref, 0, eighth, which, ref[three:head, :])
    base = 2 * (quarter + eighth)
    tail = up_ref.shape[0] - base
    relayed = pair_ref[head : head + list_height(capacity, 2), :128].astype(F32)
    relayed = relayed[tall : 2 * tall, :]
    height = list_height(capacity, 1)
    for target, number in ((up_ref, 0), (down_ref, 1)):
        own = lists_ref[number * height : (number + 1) * height, :].astype(F32)[:tall, :]
        target[base:, :] = jnp.zeros((tail, target.shape[1]), BF16)
        target[base:, :128] = filled([own, relayed], tail).astype(BF16)


def direct_kernel(coords_ref, modes_ref, out_ref):
    leaves = coords_ref.shape[0]
    width = modes_ref.shape[2]
    for leaf in range(leaves):
        out_ref[:, leaf * width : (leaf + 1) * width] = jnp.dot(
            coords_ref[leaf], modes_ref[leaf], preferred_element_type=F32
        )


def gathered(disp_ref, wanted):
    depth = 256
    total = None
    for at in range(0, disp_ref.shape[1], depth):
        part = jnp.dot(
            disp_ref[:, at : at + depth], one_hot(wanted, at, depth), preferred_element_type=F32
        )
        total = part if total is None else total + part
    return total.astype(BF16)


def displace_kernel(
    capacity,
    shifts,
    wraps,
    me_ref,
    direct_ref,
    couple_ref,
    mine_ref,
    pair_ref,
    lists_ref,
    *rest,
):
    arrays = rest[: len(shifts)]
    disp_ref, wanted_ref, cross_ref, anc_t = rest[len(shifts) :]
    leaves, levels, block, width = couple_ref.shape
    me = me_ref[0]
    odd = lax.rem(me, 2)
    chip = lax.rem(lax.div(me, 2), GROUP)
    half, quarter, eighth = block // 2, block // 4, block // 8

    def put(level, at, rows, value):
        anc_t[pl.ds(pl.multiple_of(level * block + at * rows, rows), rows), :] = value

    for which, ref in ((odd, mine_ref), (1 - odd, pair_ref)):
        put(0, which, half, ref[:half, :])
        put(1, 2 * lax.rem(chip, 2) + which, quarter, ref[half : half + quarter, :])
        put(2, 2 * chip + which, eighth, ref[half + quarter : half + quarter + eighth, :])
    two = 2 * quarter
    up, down = arrays[0], arrays[1]
    beside = 1 - lax.rem(chip, 2)
    low = lax.rem(chip, 2) == 0
    put(1, beside, two, jnp.where(low, down[:two, :], up[:two, :]))
    for shift, ref in zip(shifts, arrays):
        at = two if ref.shape[0] > 2 * eighth else 0
        place = chip - shift
        if wraps:
            put(2, lax.rem(place + GROUP, GROUP), 2 * eighth, ref[at : at + 2 * eighth, :])
        else:

            @pl.when((place >= 0) & (place < GROUP))
            def _(place=place, ref=ref, at=at):
                put(2, place, 2 * eighth, ref[at : at + 2 * eighth, :])

    anc = anc_t[...].astype(F32).T.astype(BF16)
    for leaf in range(leaves):
        value = direct_ref[:, leaf * width : (leaf + 1) * width]
        for level in range(levels):
            value = value + jnp.dot(
                anc[:, level * block : (level + 1) * block],
                couple_ref[leaf, level],
                preferred_element_type=F32,
            )
        disp_ref[:, leaf * width : (leaf + 1) * width] = value.astype(BF16)

    tall = 2 * capacity // 128
    height = list_height(capacity, 1)
    base = two + 2 * eighth
    up_lists, down_lists = up[base:, :128], down[base:, :128]
    head = half + quarter + eighth
    pair_lists = pair_ref[head : head + list_height(capacity, 2), :128]
    wanted_ref[:, :capacity] = unpacked(up_lists, 0, capacity)
    wanted_ref[:, capacity : 2 * capacity] = unpacked(down_lists, 0, capacity)
    wanted_ref[:, 2 * capacity : 3 * capacity] = unpacked(pair_lists, 0, capacity)
    wanted_ref[:, 3 * capacity :] = unpacked(
        lists_ref[2 * height : 3 * height, :], 0, capacity
    )
    across = jnp.where(
        odd == 1, unpacked(down_lists, tall, capacity), unpacked(up_lists, tall, capacity)
    )
    cross_ref[...] = gathered(disp_ref, across)


def gather_kernel(capacity, first, disp_ref, wanted_ref, left_ref, right_ref):
    both = gathered(
        disp_ref, wanted_ref[:, first * capacity : (first + 2) * capacity]
    )
    left_ref[...] = both[:, :capacity]
    right_ref[...] = both[:, capacity:]


def permute_kernel(first, key_ref, operators_ref, out_ref):
    clusters, width, rows = operators_ref.shape
    tile = 384
    for part in range(out_ref.shape[0] // tile):
        for cluster in range(clusters):
            for at in range(0, tile, 128):
                pick = one_hot(
                    key_ref[cluster : cluster + 1, :], first + part * tile + at, 128
                )
                moved = jnp.dot(pick, operators_ref[cluster], preferred_element_type=F32)
                start = part * tile + at
                out_ref[start : start + 128, cluster * rows : (cluster + 1) * rows] = (
                    moved.astype(BF16)
                )


def early_kernel(capacity, moved_ref, pair_ref, own_ref, cross_ref, out_ref):
    clusters, modes, rows = out_ref.shape
    for cluster in range(clusters):
        value = None
        for number, ref in enumerate((pair_ref, own_ref, cross_ref)):
            part = jnp.dot(
                ref[...],
                moved_ref[
                    number * capacity : (number + 1) * capacity,
                    cluster * rows : (cluster + 1) * rows,
                ],
                preferred_element_type=F32,
            )
            value = part if value is None else value + part
        out_ref[cluster] = value


def late_kernel(
    capacity,
    scale,
    weight_ref,
    compliance_ref,
    early_ref,
    moved_ref,
    plus_ref,
    minus_ref,
    stress_ref,
    energy_ref,
):
    clusters, modes, rows = stress_ref.shape
    points = energy_ref.shape[1]
    weight = weight_ref[...]
    for cluster in range(clusters):
        value = early_ref[cluster]
        for number, ref in enumerate((plus_ref, minus_ref)):
            value = value + jnp.dot(
                ref[...],
                moved_ref[
                    number * capacity : (number + 1) * capacity,
                    cluster * rows : (cluster + 1) * rows,
                ],
                preferred_element_type=F32,
            )
        stress_ref[cluster] = value
        square = jnp.sum(value * value * weight, axis=0, keepdims=True)
        square = square * compliance_ref[cluster : cluster + 1, :]
        term = square[:, :points]
        for part in range(1, rows // points):
            term = term + square[:, part * points : (part + 1) * points]
        energy_ref[cluster : cluster + 1, :] = term * scale


def store_kernel(source_ref, target_hbm, sem):
    move = pltpu.make_async_copy(source_ref, target_hbm, sem)
    move.start()
    move.wait()


def share_kernel(at_ref, mine_ref, other_ref, out_ref):
    clusters, points = mine_ref.shape
    total = mine_ref[...] + other_ref[...]
    row = [total[c : c + 1, :] for c in range(clusters)]
    lanes = (clusters * points + 127) // 128 * 128
    if lanes > clusters * points:
        row.append(jnp.zeros((1, lanes - clusters * points), F32))
    flat = jnp.broadcast_to(jnp.concatenate(row, axis=1), (8, lanes))
    share = out_ref.shape[1]
    moved = pltpu.roll(flat, lanes - at_ref[0] * share, 1)
    out_ref[...] = moved[0:1, :share]


def shards(
    leaf_coords,
    leaf_modes,
    constraint_modes,
    sep_one,
    sep_two,
    sep_three,
    cluster_rows,
    operators,
    compliance,
    modal_weight,
):
    sub_count = lax.axis_size("sub")
    mode_count = lax.axis_size("mode")
    me = lax.axis_index("sub").astype(I32).reshape(1)
    leaves, modes, inner = leaf_coords.shape
    width = leaf_modes.shape[2]
    dof_count = leaves * width
    levels, block = constraint_modes.shape[1:3]
    clusters, slots = cluster_rows.shape
    rows = operators.shape[2]
    points = rows // 6
    capacity = clusters * slots // 4
    smem = pl.BlockSpec(memory_space=pltpu.SMEM)
    vmem = pl.BlockSpec(memory_space=VMEM)
    hbm = pl.BlockSpec(memory_space=pltpu.HBM)
    array = jax.ShapeDtypeStruct
    half, quarter, eighth = sep_one.shape[1], sep_two.shape[1], sep_three.shape[1]

    held = half + quarter + eighth + list_height(capacity, 2)
    mine, key, local = call(
        lambda *refs: prep_kernel(sub_count, dof_count, capacity, *refs),
        "prep",
        (me, sep_one, sep_two.T, sep_three.T, cluster_rows),
        (
            array((held, modes), BF16),
            array((clusters, slots), I32),
            array((clusters, slots), I32),
        ),
        8,
        1000000000,
        [smem, hbm, hbm, hbm, hbm],
        [
            VMEM((modes, half), BF16),
            VMEM((quarter, modes), BF16),
            VMEM((eighth, modes), BF16),
            VMEM((clusters, slots), I32),
            pltpu.SemaphoreType.DMA((4,)),
        ],
    )
    pair = swap_with(mine, "sub", 1)
    lists = call(
        lambda *refs: lists_kernel(capacity, *refs),
        "lists",
        (key, local),
        array((3 * list_height(capacity, 1), 128), BF16),
        8,
        1000000000,
    )
    sent = 2 * (quarter + eighth)
    up, down, far = call(
        lambda *refs: relay_kernel(capacity, half, quarter, eighth, *refs),
        "relay",
        (me, mine, pair, lists),
        (
            array((sent + list_height(capacity, 2), modes), BF16),
            array((sent + list_height(capacity, 2), modes), BF16),
            array((2 * eighth, modes), BF16),
        ),
        4,
        10000000,
        [smem, vmem, vmem, vmem],
    )
    wraps = sub_count == 2 * GROUP
    shifts = (1, -1, 2) if wraps else (1, -1, 2, -2, 3, -3)
    arrays = [
        shift_by({1: up, -1: down}.get(shift, far), "sub", 2 * shift) for shift in shifts
    ]
    direct = call(
        direct_kernel,
        "direct",
        (leaf_coords, leaf_modes),
        array((modes, dof_count), F32),
        4,
        1500000000,
    )
    disp, wanted, cross = call(
        lambda *refs: displace_kernel(capacity, shifts, wraps, *refs),
        "displace",
        (me, direct, constraint_modes, mine, pair, lists, *arrays),
        (
            array((modes, dof_count), BF16),
            array((1, 4 * capacity), I32),
            array((modes, capacity), BF16),
        ),
        12,
        3000000000,
        [smem] + [vmem] * (5 + len(arrays)),
        [VMEM((levels * block, modes), BF16)],
    )
    cross = swap_across(cross, "sub")
    flow = array((modes, capacity), BF16)
    plus, minus = call(
        lambda *refs: gather_kernel(capacity, 0, *refs),
        "gather_far",
        (disp, wanted),
        (flow, flow),
        12,
        2000000000,
    )
    plus = shift_by(plus, "sub", -2)
    minus = shift_by(minus, "sub", 2)
    other, own = call(
        lambda *refs: gather_kernel(capacity, 2, *refs),
        "gather_near",
        (disp, wanted),
        (flow, flow),
        12,
        2000000000,
    )
    other = swap_with(other, "sub", 1)
    moved_near = call(
        lambda *refs: permute_kernel(2 * capacity, *refs),
        "permute_near",
        (key, operators),
        array((3 * capacity, clusters * rows), BF16),
        8,
        3000000000,
    )
    moved_far = call(
        lambda *refs: permute_kernel(0, *refs),
        "permute_far",
        (key, operators),
        array((2 * capacity, clusters * rows), BF16),
        8,
        2000000000,
    )
    early = call(
        lambda *refs: early_kernel(capacity, *refs),
        "stress_early",
        (moved_near, other, own, cross),
        array((clusters, modes, rows), F32),
        8,
        500000000,
    )
    stresses, energy = call(
        lambda *refs: late_kernel(capacity, 0.5 / (modes * mode_count), *refs),
        "stress_late",
        (modal_weight.reshape(modes, 1), compliance, early, moved_far, plus, minus),
        (array((clusters, modes, rows), F32), array((clusters, points), F32)),
        8,
        500000000,
    )
    mask = 1
    while 2 * mask < mode_count:
        energy = energy + swap_with(energy, "mode", mask)
        mask *= 2
    arrived = swap_with(energy, "mode", mask)
    stresses = pl.pallas_call(
        store_kernel,
        out_shape=array((clusters, modes, rows), F32),
        in_specs=[vmem],
        out_specs=hbm,
        scratch_shapes=[pltpu.SemaphoreType.DMA],
        compiler_params=pltpu.CompilerParams(vmem_limit_bytes=4 * 1024 * 1024),
        cost_estimate=pl.CostEstimate(
            flops=500000000, bytes_accessed=2000000, transcendentals=0
        ),
        name="store",
    )(stresses)
    at = lax.axis_index("mode").astype(I32).reshape(1)
    share = clusters * points // mode_count
    strain_energy = call(
        share_kernel,
        "share",
        (at, energy, arrived),
        array((1, share), F32),
        4,
        1000,
        [smem, vmem, vmem],
    )
    return (stresses, strain_energy.reshape(share))


def solution(mesh):
    return jax.shard_map(
        shards,
        mesh=mesh,
        in_specs=(
            P("sub", "mode", None),
            P("sub", None, None),
            P("sub", None, None, None),
            P("mode", "sub"),
            P("mode", "sub"),
            P("mode", "sub"),
            P("sub", None),
            P("sub", None, None),
            P("sub", None),
            P("mode"),
        ),
        out_specs=(P("sub", "mode", None), P(("sub", "mode"))),
        check_vma=False,
    )
```

time: 109 us -> 50.1 us (0.46)
  local copies, waits for them, and re-layouts: 44.4 us -> 9.51 us
  other arithmetic: 20 us -> 0.01 us
  Pallas kernels: 0 us -> 15 us
  blocking collectives: 11.9 us -> 0 us
  matrix products: 11.3 us -> 0 us
  waiting for transfers between devices: 4.83 us -> 9.36 us
  starting transfers between devices: 13.6 us -> 15 us
    gather x9 -> x0, local copies, waits for them, and re-layouts: 36.3 us -> none  [the longest x4 21.1 us: shards(): placed = jnp.take(returned, slot_ranks[number], axis=1)]
    pallas_call x0 -> x13, Pallas kernels: none -> 15 us  [the longest x12 14.1 us: call(): pl.pallas_call(kernel, out_shape=outputs, in_specs=specs or [vmem] * len(...]
    select_n x20 -> x0, other arithmetic: 13.1 us -> none  [the longest x1 7.37 us: shards(): assembled = jnp.where((slot_offset == offset)[None, :], placed, assembled)]
    unnamed x1 -> x0, blocking collectives: 11.9 us -> none
    dot_general x3 -> x0, matrix products: 11.3 us -> none  [the longest x1 6.25 us: shards(): jnp.einsum('amb,labr->mlr', ancestry, constraint_modes, preferred_element...]
    unnamed x47 -> x26, local copies, waits for them, and re-layouts: 2.91 us -> 9.4 us
    ppermute x14 -> x10, waiting for transfers between devices: 4.83 us -> 9.36 us  [the longest x1 4.55 us: swap_across(): lax.ppermute(value, axis, [(i, (i + 2 * (i % 2) - 1) % peers) for i in ra...]
    reshape x4 -> x1, local copies, waits for them, and re-layouts: 4.32 us -> 0.12 us  [shards(): modal_weight.reshape(modes, 1)]
  transfers between devices with their start and end apart: 14 -> 10, of which waited for: 4 -> 4; matrix products, arithmetic and copies ran while one was open for 30% -> 0% of each run, Pallas kernels for 0% -> 14%
where the time goes in v2:
time: 50.1 us; the launch traced here: 49.8 us
  Pallas kernels  15 us (30%)
  starting transfers between devices  15 us (30%)
  local copies, waits for them, and re-layouts  9.51 us (19%)
  waiting for transfers between devices  9.36 us (19%)
  between operations  0.84 us (2%)
    pallas_call x12, Pallas kernels, call(): pl.pallas_call(kernel, out_shape=outputs, in_specs=specs or [vmem] * len(...  14.1 us
    unnamed x26, local copies, waits for them, and re-layouts  9.4 us
    ppermute x5, starting transfers between devices, shift_by(): lax.ppermute(value, axis, [(i, (i + by) % peers) for i in range(peers)])  7.58 us
    ppermute x4, starting transfers between devices, swap_with(): lax.ppermute(value, axis, [(i, i ^ mask) for i in range(lax.axis_size(axi...  4.74 us
    ppermute x1, waiting for transfers between devices, swap_across(): lax.ppermute(value, axis, [(i, (i + 2 * (i % 2) - 1) % peers) for i in ra...  4.55 us
    ppermute x4, waiting for transfers between devices, swap_with(): lax.ppermute(value, axis, [(i, i ^ mask) for i in range(lax.axis_size(axi...  2.99 us
    ppermute x1, starting transfers between devices, swap_across(): lax.ppermute(value, axis, [(i, (i + 2 * (i % 2) - 1) % peers) for i in ra...  2.71 us
    ppermute x5, waiting for transfers between devices, shift_by(): lax.ppermute(value, axis, [(i, (i + by) % peers) for i in range(peers)])  1.82 us
  transfers between devices with their start and end apart: 10, of which 4 were waited for; matrix products, arithmetic and copies ran while one was open for 0% of the time, Pallas kernels for 14%

profile of v2, /device:TPU:0, one launch (start us, length us, event | category | flops | bytes accessed | tf_op | source)
XLA Modules:
  0.0 49.8 jit_solution(11951879920322380314)
XLA Ops:
  0.7 0.9 %copy-done.6 = bf16[192,128]{1,0:T(8,128)(2,1)S(1)} copy-done((bf16[192,128]{1,0:T(8,128)(2,1)S(1)}, bf16[192,128]{1,0:T(8,128)(2,1)}, u32[]{:S(2)}) %copy-start.6) | copy-done | bytes 49176
  3.7 1.5 %prep.1 = (bf16[240,192]{1,0:T(8,128)(2,1)S(1)}, s32[3,512]{1,0:T(4,128)S(1)}, s32[3,512]{1,0:T(4,128)S(1)}) custom-call(s32[1]{0:T(128)} %bitcast.1.refs_0_, bf16[192,128]{1,0:T(8,128)(2,1)S(1)} %copy-done.6, bf16[64,192]{1,0:T(8,128)(2,1)S(1)} %bitcast.6, bf16[32,192]{1,0:T(8,128)(2,1)S(1)} %bitcast.7, s32[3,512]{1,0:T(4,128)S(1)} %copy-done.9), custom_call_target="tpu_custom_call" | custom-call | flops 1000000000 | bytes 92164 | tf_op jit(solution)/shard_map/prep/pallas_call | solution.py:38
  5.8 2.0 %permute_near.1.refs_0_ = bf16[1152,1152]{1,0:T(8,128)(2,1)S(1)} custom-call(s32[3,512]{1,0:T(4,128)S(1)} %get-tuple-element.17.refs_0_, bf16[3,512,384]{2,1,0:T(8,128)(2,1)S(1)} %copy-done.2), custom_call_target="tpu_custom_call" | custom-call | flops 3000000000 | bytes 1185792 | tf_op jit(solution)/shard_map/permute_near/pallas_call | solution.py:38
  7.8 1.0 %lists.1.refs_3_.refs_5_ = bf16[48,128]{1,0:T(8,128)(2,1)S(1)} custom-call(s32[3,512]{1,0:T(4,128)S(1)} %get-tuple-element.17.refs_0_, s32[3,512]{1,0:T(4,128)S(1)} %get-tuple-element.19.refs_1_), custom_call_target="tpu_custom_call" | custom-call | flops 1000000000 | bytes 12288 | tf_op jit(solution)/shard_map/lists/pallas_call | solution.py:38
  8.9 2.5 %collective-permute-start.1 = (bf16[208,192]{1,0:T(8,128)(2,1)S(1)}, bf16[208,192]{1,0:T(8,128)(2,1)S(1)}, u32[]{:S(2)}, u32[]{:S(2)}) collective-permute-start(bf16[208,192]{1,0:T(8,128)(2,1)S(1)} %get-tuple-element.20), channel_id=1, source_target_pairs={{0,8},{4,12},{8,16},{12,20},{16,24},{20,28},{24,0},{28,4},{1,9},{5... | collective-permute-start | bytes 239624 | tf_op jit(solution)/shard_map/ppermute | solution.py:20
  11.4 1.0 %collective-permute-start.2 = (bf16[208,192]{1,0:T(8,128)(2,1)S(1)}, bf16[208,192]{1,0:T(8,128)(2,1)S(1)}, u32[]{:S(2)}, u32[]{:S(2)}) collective-permute-start(bf16[208,192]{1,0:T(8,128)(2,1)S(1)} %get-tuple-element.21), channel_id=1, source_target_pairs={{0,24},{4,28},{8,0},{12,4},{16,8},{20,12},{24,16},{28,20},{1,25},{... | collective-permute-start | bytes 239624 | tf_op jit(solution)/shard_map/ppermute | solution.py:20
  12.5 1.9 %collective-permute-start.3 = (bf16[64,192]{1,0:T(8,128)(2,1)S(1)}, bf16[64,192]{1,0:T(8,128)(2,1)S(1)}, u32[]{:S(2)}, u32[]{:S(2)}) collective-permute-start(bf16[64,192]{1,0:T(8,128)(2,1)S(1)} %get-tuple-element.22), channel_id=1, source_target_pairs={{0,16},{4,20},{8,24},{12,28},{16,0},{20,4},{24,8},{28,12},{1,17},{... | collective-permute-start | bytes 73736 | tf_op jit(solution)/shard_map/ppermute | solution.py:20
  15.0 1.6 %copy-done.10 = f32[192,4096]{1,0:T(8,128)} copy-done((f32[192,4096]{1,0:T(8,128)}, f32[192,4096]{1,0:T(8,128)S(1)}, u32[]{:S(2)}) %copy-start.10) | copy-done | bytes 3145752
  16.7 1.8 %collective-permute-done.2.refs_7_ = bf16[208,192]{1,0:T(8,128)(2,1)S(1)} collective-permute-done((bf16[208,192]{1,0:T(8,128)(2,1)S(1)}, bf16[208,192]{1,0:T(8,128)(2,1)S(1)}, u32[]{:S(2)}, u32[]{:S(2)}) %collective-permute-start.2) | collective-permute-done | bytes 79904 | tf_op jit(solution)/shard_map/ppermute | solution.py:20
  18.6 2.8 %copy-done.1 = bf16[8,3,256,512]{3,2,1,0:T(8,128)(2,1)S(1)} copy-done((bf16[8,3,256,512]{3,2,1,0:T(8,128)(2,1)S(1)}, bf16[8,3,256,512]{3,2,1,0:T(8,128)(2,1)}, u32[]{:S(2)}) %copy-start.1) | copy-done | bytes 6291480
  21.3 1.9 %copy-done.11 = f32[192,4096]{1,0:T(8,128)S(1)} copy-done((f32[192,4096]{1,0:T(8,128)S(1)}, f32[192,4096]{1,0:T(8,128)}, u32[]{:S(2)}) %copy-start.11) | copy-done | bytes 3145752
  23.2 2.4 %displace.1 = (bf16[192,4096]{1,0:T(8,128)(2,1)S(1)}, s32[1,1536]{1,0:T(1,128)S(1)}, bf16[192,384]{1,0:T(8,128)(2,1)S(1)}) custom-call(s32[1]{0:T(128)} %bitcast.1.refs_0_, f32[192,4096]{1,0:T(8,128)S(1)} %copy-done.11, bf16[8,3,256,512]{3,2,1,0:T(8,128)(2,1)S(1)} %copy-done.1, bf16[240,192]{1,0:T(8,128)(2,1)S(1)} %get-tuple-element.18.refs_1_.refs_3_, ...), custom_call_target="tpu_custom_call" | custom-call | flops 3000000000 | bytes 9818116 | tf_op jit(solution)/shard_map/displace/pallas_call | solution.py:38
  25.6 1.4 %gather_far.1 = (bf16[192,384]{1,0:T(8,128)(2,1)S(1)}, bf16[192,384]{1,0:T(8,128)(2,1)S(1)}) custom-call(bf16[192,4096]{1,0:T(8,128)(2,1)S(1)} %get-tuple-element.23.refs_0_, s32[1,1536]{1,0:T(1,128)S(1)} %get-tuple-element.24.refs_1_), custom_call_target="tpu_custom_call" | custom-call | flops 2000000000 | bytes 1579008 | tf_op jit(solution)/shard_map/gather_far/pallas_call | solution.py:38
  27.0 1.4 %gather_near.1 = (bf16[192,384]{1,0:T(8,128)(2,1)S(1)}, bf16[192,384]{1,0:T(8,128)(2,1)S(1)}) custom-call(bf16[192,4096]{1,0:T(8,128)(2,1)S(1)} %get-tuple-element.23.refs_0_, s32[1,1536]{1,0:T(1,128)S(1)} %get-tuple-element.24.refs_1_), custom_call_target="tpu_custom_call" | custom-call | flops 2000000000 | bytes 1579008 | tf_op jit(solution)/shard_map/gather_near/pallas_call | solution.py:38
  28.4 1.8 %collective-permute-start.6 = (bf16[192,384]{1,0:T(8,128)(2,1)S(1)}, bf16[192,384]{1,0:T(8,128)(2,1)S(1)}, u32[]{:S(2)}, u32[]{:S(2)}) collective-permute-start(bf16[192,384]{1,0:T(8,128)(2,1)S(1)} %get-tuple-element.28), channel_id=1, source_target_pairs={{0,24},{4,28},{8,0},{12,4},{16,8},{20,12},{24,16},{28,20},{1,25},{... | collective-permute-start | bytes 442376 | tf_op jit(solution)/shard_map/ppermute | solution.py:20
  30.5 2.7 %collective-permute-start.5 = (bf16[192,384]{1,0:T(8,128)(2,1)S(1)}, bf16[192,384]{1,0:T(8,128)(2,1)S(1)}, u32[]{:S(2)}, u32[]{:S(2)}) collective-permute-start(bf16[192,384]{1,0:T(8,128)(2,1)S(1)} %get-tuple-element.27), channel_id=1, source_target_pairs={{0,28},{4,8},{8,4},{12,16},{16,12},{20,24},{24,20},{28,0},{1,29},{... | collective-permute-start | bytes 442376 | tf_op jit(solution)/shard_map/ppermute | solution.py:29
  33.2 1.4 %permute_far.1.refs_3_ = bf16[768,1152]{1,0:T(8,128)(2,1)S(1)} custom-call(s32[3,512]{1,0:T(4,128)S(1)} %get-tuple-element.17.refs_0_, bf16[3,512,384]{2,1,0:T(8,128)(2,1)S(1)} %copy-done.3), custom_call_target="tpu_custom_call" | custom-call | flops 2000000000 | bytes 1185792 | tf_op jit(solution)/shard_map/permute_far/pallas_call | solution.py:38
  34.6 4.5 %collective-permute-done.5.refs_3_ = bf16[192,384]{1,0:T(8,128)(2,1)S(1)} collective-permute-done((bf16[192,384]{1,0:T(8,128)(2,1)S(1)}, bf16[192,384]{1,0:T(8,128)(2,1)S(1)}, u32[]{:S(2)}, u32[]{:S(2)}) %collective-permute-start.5) | collective-permute-done | bytes 147488 | tf_op jit(solution)/shard_map/ppermute | solution.py:29
  39.2 1.0 %stress_early.1.refs_2_ = f32[3,192,384]{2,1,0:T(8,128)S(1)} custom-call(bf16[1152,1152]{1,0:T(8,128)(2,1)S(1)} %permute_near.1.refs_0_, bf16[192,384]{1,0:T(8,128)(2,1)S(1)} %collective-permute-done.4.refs_1_, bf16[192,384]{1,0:T(8,128)(2,1)S(1)} %get-tuple-element.26.refs_2_, bf16[192,384]{1,0:T(8,128)(2,1)S(1)} %collective-permute-done.5.refs_3_), custom_call_target="tpu_custom_call" | custom-call | flops 500000000 | bytes 3096576 | tf_op jit(solution)/shard_map/stress_early/pallas_call | solution.py:38
  41.0 1.6 %collective-permute-start.8 = (f32[3,64]{1,0:T(4,128)S(1)}, f32[3,64]{1,0:T(4,128)S(1)}, u32[]{:S(2)}, u32[]{:S(2)}) collective-permute-start(f32[3,64]{1,0:T(4,128)S(1)} %get-tuple-element.31), channel_id=1, source_target_pairs={{0,1},{1,0},{2,3},{3,2},{4,5},{5,4},{6,7},{7,6},{8,9},{9,8},{10,11... | collective-permute-start | bytes 2312 | tf_op jit(solution)/shard_map/ppermute | solution.py:24
  42.6 2.0 %collective-permute-done.8 = f32[3,64]{1,0:T(4,128)S(1)} collective-permute-done((f32[3,64]{1,0:T(4,128)S(1)}, f32[3,64]{1,0:T(4,128)S(1)}, u32[]{:S(2)}, u32[]{:S(2)}) %collective-permute-start.8) | collective-permute-done | bytes 800 | tf_op jit(solution)/shard_map/ppermute | solution.py:24
  44.6 2.6 %collective-permute-start.9 = (f32[3,64]{1,0:T(4,128)S(1)}, f32[3,64]{1,0:T(4,128)S(1)}, u32[]{:S(2)}, u32[]{:S(2)}) collective-permute-start(f32[3,64]{1,0:T(4,128)S(1)} %add.3.mine_ref), channel_id=1, source_target_pairs={{0,2},{1,3},{2,0},{3,1},{4,6},{5,7},{6,4},{7,5},{8,10},{9,11},{10,... | collective-permute-start | bytes 2312 | tf_op jit(solution)/shard_map/ppermute | solution.py:24
  47.2 0.9 %store.1 = f32[3,192,384]{2,1,0:T(8,128)} custom-call(f32[3,192,384]{2,1,0:T(8,128)S(1)} %get-tuple-element.30.source_ref), custom_call_target="tpu_custom_call" | custom-call | flops 500000000 | bytes 2000000 | tf_op jit(solution)/shard_map/store/pallas_call | solution.py:558
  48.1 1.0 %collective-permute-done.9.other_ref = f32[3,64]{1,0:T(4,128)S(1)} collective-permute-done((f32[3,64]{1,0:T(4,128)S(1)}, f32[3,64]{1,0:T(4,128)S(1)}, u32[]{:S(2)}, u32[]{:S(2)}) %collective-permute-start.9) | collective-permute-done | bytes 800 | tf_op jit(solution)/shard_map/ppermute | solution.py:24
  (37 shorter events, 5.3 us)
Async XLA Ops:
  0.6 5.1 %copy-start.2 = (bf16[3,512,384]{2,1,0:T(8,128)(2,1)S(1)}, bf16[3,512,384]{2,1,0:T(8,128)(2,1)}, u32[]{:S(2)}) copy-start(bf16[3,512,384]{2,1,0:T(8,128)(2,1)} %refs_1_.6) | copy-start | bytes 3538948
  0.6 0.9 %copy-start.6 = (bf16[192,128]{1,0:T(8,128)(2,1)S(1)}, bf16[192,128]{1,0:T(8,128)(2,1)}, u32[]{:S(2)}) copy-start(bf16[192,128]{1,0:T(8,128)(2,1)} %refs_1_.4) | copy-start | bytes 147460
  1.5 0.8 %copy-start.7 = (bf16[192,64]{0,1:T(8,128)(2,1)S(1)}, bf16[192,64]{0,1:T(8,128)(2,1)}, u32[]{:S(2)}) copy-start(bf16[192,64]{0,1:T(8,128)(2,1)} %param.14) | copy-start | bytes 73732
  2.3 0.7 %copy-start.8 = (bf16[192,32]{0,1:T(8,128)(2,1)S(1)}, bf16[192,32]{0,1:T(8,128)(2,1)}, u32[]{:S(2)}) copy-start(bf16[192,32]{0,1:T(8,128)(2,1)} %param.15) | copy-start | bytes 36868
  3.0 0.7 %copy-start.9 = (s32[3,512]{1,0:T(4,128)S(1)}, s32[3,512]{1,0:T(4,128)}, u32[]{:S(2)}) copy-start(s32[3,512]{1,0:T(4,128)} %refs_4_.1) | copy-start | bytes 18436
  5.2 3.6 %collective-permute-start = (bf16[240,192]{1,0:T(8,128)(2,1)S(1)}, bf16[240,192]{1,0:T(8,128)(2,1)S(1)}, u32[]{:S(2)}, u32[]{:S(2)}) collective-permute-start(bf16[240,192]{1,0:T(8,128)(2,1)S(1)} %get-tuple-element.18.refs_1_.refs_3_), channel_id=1, source_target_pairs={{0,4},{4,0},{8,12},{12,8},{16,20},{20,16},{24,28},{28,24},{1,5},{5... | collective-permute-start | bytes 276488 | tf_op jit(solution)/shard_map/ppermute | solution.py:24
  7.8 6.6 %copy-start.4 = (bf16[8,128,512]{2,1,0:T(8,128)(2,1)S(1)}, bf16[8,128,512]{2,1,0:T(8,128)(2,1)}, u32[]{:S(2)}) copy-start(bf16[8,128,512]{2,1,0:T(8,128)(2,1)} %modes_ref.1) | copy-start | bytes 3145732
  7.8 6.6 %copy-start.5 = (bf16[8,192,128]{2,1,0:T(8,128)(2,1)S(1)}, bf16[8,192,128]{2,1,0:T(8,128)(2,1)}, u32[]{:S(2)}) copy-start(bf16[8,192,128]{2,1,0:T(8,128)(2,1)} %coords_ref.1) | copy-start | bytes 1179652
  8.9 7.8 %collective-permute-start.1 = (bf16[208,192]{1,0:T(8,128)(2,1)S(1)}, bf16[208,192]{1,0:T(8,128)(2,1)S(1)}, u32[]{:S(2)}, u32[]{:S(2)}) collective-permute-start(bf16[208,192]{1,0:T(8,128)(2,1)S(1)} %get-tuple-element.20), channel_id=1, source_target_pairs={{0,8},{4,12},{8,16},{12,20},{16,24},{20,28},{24,0},{28,4},{1,9},{5... | collective-permute-start | bytes 239624 | tf_op jit(solution)/shard_map/ppermute | solution.py:20
  11.4 7.1 %collective-permute-start.2 = (bf16[208,192]{1,0:T(8,128)(2,1)S(1)}, bf16[208,192]{1,0:T(8,128)(2,1)S(1)}, u32[]{:S(2)}, u32[]{:S(2)}) collective-permute-start(bf16[208,192]{1,0:T(8,128)(2,1)S(1)} %get-tuple-element.21), channel_id=1, source_target_pairs={{0,24},{4,28},{8,0},{12,4},{16,8},{20,12},{24,16},{28,20},{1,25},{... | collective-permute-start | bytes 239624 | tf_op jit(solution)/shard_map/ppermute | solution.py:20
  12.5 4.1 %copy-start.12 = (f32[192]{0:T(256)S(1)}, f32[192]{0:T(256)}, u32[]{:S(2)}) copy-start(f32[192]{0:T(256)} %param.19) | copy-start | bytes 2308
  12.5 4.3 %collective-permute-start.3 = (bf16[64,192]{1,0:T(8,128)(2,1)S(1)}, bf16[64,192]{1,0:T(8,128)(2,1)S(1)}, u32[]{:S(2)}, u32[]{:S(2)}) collective-permute-start(bf16[64,192]{1,0:T(8,128)(2,1)S(1)} %get-tuple-element.22), channel_id=1, source_target_pairs={{0,16},{4,20},{8,24},{12,28},{16,0},{20,4},{24,8},{28,12},{1,17},{... | collective-permute-start | bytes 73736 | tf_op jit(solution)/shard_map/ppermute | solution.py:20
  14.9 1.6 %copy-start.10 = (f32[192,4096]{1,0:T(8,128)}, f32[192,4096]{1,0:T(8,128)S(1)}, u32[]{:S(2)}) copy-start(f32[192,4096]{1,0:T(8,128)S(1)} %direct.1.refs_1_) | copy-start | bytes 9437188
  18.5 2.8 %copy-start.1 = (bf16[8,3,256,512]{3,2,1,0:T(8,128)(2,1)S(1)}, bf16[8,3,256,512]{3,2,1,0:T(8,128)(2,1)}, u32[]{:S(2)}) copy-start(bf16[8,3,256,512]{3,2,1,0:T(8,128)(2,1)} %refs_2_.1) | copy-start | bytes 18874372
  21.3 1.9 %copy-start.11 = (f32[192,4096]{1,0:T(8,128)S(1)}, f32[192,4096]{1,0:T(8,128)}, u32[]{:S(2)}) copy-start(f32[192,4096]{1,0:T(8,128)} %copy-done.10) | copy-start | bytes 9437188
  27.0 6.2 %copy-start.3 = (bf16[3,512,384]{2,1,0:T(8,128)(2,1)S(1)}, bf16[3,512,384]{2,1,0:T(8,128)(2,1)}, u32[]{:S(2)}) copy-start(bf16[3,512,384]{2,1,0:T(8,128)(2,1)} %refs_1_.6) | copy-start | bytes 3538948
  28.4 11.8 %collective-permute-start.6 = (bf16[192,384]{1,0:T(8,128)(2,1)S(1)}, bf16[192,384]{1,0:T(8,128)(2,1)S(1)}, u32[]{:S(2)}, u32[]{:S(2)}) collective-permute-start(bf16[192,384]{1,0:T(8,128)(2,1)S(1)} %get-tuple-element.28), channel_id=1, source_target_pairs={{0,24},{4,28},{8,0},{12,4},{16,8},{20,12},{24,16},{28,20},{1,25},{... | collective-permute-start | bytes 442376 | tf_op jit(solution)/shard_map/ppermute | solution.py:20
  30.2 10.0 %collective-permute-start.7 = (bf16[192,384]{1,0:T(8,128)(2,1)S(1)}, bf16[192,384]{1,0:T(8,128)(2,1)S(1)}, u32[]{:S(2)}, u32[]{:S(2)}) collective-permute-start(bf16[192,384]{1,0:T(8,128)(2,1)S(1)} %get-tuple-element.29), channel_id=1, source_target_pairs={{0,8},{4,12},{8,16},{12,20},{16,24},{20,28},{24,0},{28,4},{1,9},{5... | collective-permute-start | bytes 442376 | tf_op jit(solution)/shard_map/ppermute | solution.py:20
  30.5 4.1 %collective-permute-start.4 = (bf16[192,384]{1,0:T(8,128)(2,1)S(1)}, bf16[192,384]{1,0:T(8,128)(2,1)S(1)}, u32[]{:S(2)}, u32[]{:S(2)}) collective-permute-start(bf16[192,384]{1,0:T(8,128)(2,1)S(1)} %get-tuple-element.25), channel_id=1, source_target_pairs={{0,4},{4,0},{8,12},{12,8},{16,20},{20,16},{24,28},{28,24},{1,5},{5... | collective-permute-start | bytes 442376 | tf_op jit(solution)/shard_map/ppermute | solution.py:24
  30.5 8.7 %collective-permute-start.5 = (bf16[192,384]{1,0:T(8,128)(2,1)S(1)}, bf16[192,384]{1,0:T(8,128)(2,1)S(1)}, u32[]{:S(2)}, u32[]{:S(2)}) collective-permute-start(bf16[192,384]{1,0:T(8,128)(2,1)S(1)} %get-tuple-element.27), channel_id=1, source_target_pairs={{0,28},{4,8},{8,4},{12,16},{16,12},{20,24},{24,20},{28,0},{1,29},{... | collective-permute-start | bytes 442376 | tf_op jit(solution)/shard_map/ppermute | solution.py:29
  34.6 5.6 %copy-start = (f32[3,384]{1,0:T(4,128)S(1)}, f32[3,384]{1,0:T(4,128)}, u32[]{:S(2)}) copy-start(f32[3,384]{1,0:T(4,128)} %refs_1_.7) | copy-start | bytes 13828
  41.0 3.6 %collective-permute-start.8 = (f32[3,64]{1,0:T(4,128)S(1)}, f32[3,64]{1,0:T(4,128)S(1)}, u32[]{:S(2)}, u32[]{:S(2)}) collective-permute-start(f32[3,64]{1,0:T(4,128)S(1)} %get-tuple-element.31), channel_id=1, source_target_pairs={{0,1},{1,0},{2,3},{3,2},{4,5},{5,4},{6,7},{7,6},{8,9},{9,8},{10,11... | collective-permute-start | bytes 2312 | tf_op jit(solution)/shard_map/ppermute | solution.py:24
  44.6 4.5 %collective-permute-start.9 = (f32[3,64]{1,0:T(4,128)S(1)}, f32[3,64]{1,0:T(4,128)S(1)}, u32[]{:S(2)}, u32[]{:S(2)}) collective-permute-start(f32[3,64]{1,0:T(4,128)S(1)} %add.3.mine_ref), channel_id=1, source_target_pairs={{0,2},{1,3},{2,0},{3,1},{4,6},{5,7},{6,4},{7,5},{8,10},{9,11},{10,... | collective-permute-start | bytes 2312 | tf_op jit(solution)/shard_map/ppermute | solution.py:24

commit v3 on v2

v3 whole, which is shorter than its diff:
```python
import jax
import jax.numpy as jnp
from jax import lax
from jax.experimental import pallas as pl
from jax.experimental.pallas import tpu as pltpu
from jax.sharding import PartitionSpec as P


VMEM = pltpu.VMEM
F32 = jnp.float32
BF16 = jnp.bfloat16
I32 = jnp.int32
BASE = 64
GROUP = 4

PLUS, MINUS, PAIR, OWN, CROSS = range(5)


def shift_by(value, axis, by):
    peers = lax.axis_size(axis)
    return lax.ppermute(value, axis, [(i, (i + by) % peers) for i in range(peers)])


def swap_with(value, axis, mask):
    return lax.ppermute(value, axis, [(i, i ^ mask) for i in range(lax.axis_size(axis))])


def swap_across(value, axis):
    peers = lax.axis_size(axis)
    return lax.ppermute(
        value, axis, [(i, (i + 2 * (i % 2) - 1) % peers) for i in range(peers)]
    )


def call(kernel, inputs, outputs, mib, flops, specs=None, scratch=()):
    vmem = pl.BlockSpec(memory_space=VMEM)
    many = isinstance(outputs, tuple)
    nbytes = sum(x.size * x.dtype.itemsize for x in inputs)
    return pl.pallas_call(
        kernel,
        out_shape=outputs,
        in_specs=specs or [vmem] * len(inputs),
        out_specs=(vmem,) * len(outputs) if many else vmem,
        scratch_shapes=list(scratch),
        compiler_params=pltpu.CompilerParams(vmem_limit_bytes=mib * 1024 * 1024),
        cost_estimate=pl.CostEstimate(flops=flops, bytes_accessed=nbytes, transcendentals=0),
    )(*inputs)


def one_hot(target, first, rows):
    local = target - first
    local = jnp.where((local >= 0) & (local < rows), local, -1).astype(F32).astype(BF16)
    ids = lax.broadcasted_iota(I32, (rows, target.shape[1]), 0).astype(F32).astype(BF16)
    hit = ids == jnp.broadcast_to(local, ids.shape)
    return jnp.where(hit, jnp.ones((), BF16), jnp.zeros((), BF16))


def list_rows(key, digits, group, capacity):
    total = None
    for cluster, values in enumerate(digits):
        pick = jnp.concatenate(
            [
                one_hot(key[cluster : cluster + 1, :], group * capacity + at, 128)
                for at in range(0, capacity, 128)
            ],
            axis=0,
        )
        part = lax.dot_general(
            values, pick, (((1,), (1,)), ((), ())), preferred_element_type=F32
        )
        total = part if total is None else total + part
    return [
        total[digit : digit + 1, at : at + 128]
        for digit in (0, 1)
        for at in range(0, capacity, 128)
    ]


def digit_rows(local, clusters):
    high = lax.div(local, jnp.int32(BASE))
    low = local - high * BASE
    return [
        jnp.concatenate([high[c : c + 1, :], low[c : c + 1, :]], axis=0).astype(F32).astype(BF16)
        for c in range(clusters)
    ]


def filled(rows, count):
    lanes = rows[0].shape[1]
    rest = count - sum(row.shape[0] for row in rows)
    return jnp.concatenate(rows + [jnp.zeros((rest, lanes), F32)], axis=0)


def unpacked(block, start, capacity):
    parts = capacity // 128
    block = block.astype(F32)
    high = [block[start + i : start + i + 1, :] for i in range(parts)]
    low = [block[start + parts + i : start + parts + i + 1, :] for i in range(parts)]
    wanted = jnp.concatenate(high, axis=1) * float(BASE) + jnp.concatenate(low, axis=1)
    return wanted.astype(I32)


def list_height(capacity, lists):
    return (2 * capacity // 128 * lists + 15) // 16 * 16


def index_kernel(sub_count, dof_count, capacity, me_ref, rows_ref, key_ref, local_ref, lists_ref):
    clusters, width = rows_ref.shape
    high = (clusters + 7) // 8 * 8
    row = jnp.concatenate(
        [rows_ref[...], jnp.full((high - clusters, width), -1, I32)], axis=0
    )
    before = lax.broadcasted_iota(I32, (width, width), 0)
    after = lax.broadcasted_iota(I32, (width, width), 1)
    upper = jnp.where(before <= after, 1.0, 0.0).astype(BF16)
    me = me_ref[0]
    odd = lax.rem(me, 2)
    source = lax.div(row, jnp.int32(dof_count))
    local = row - source * dof_count
    distance = source - me
    distance = jnp.where(distance < 0, distance + sub_count, distance)
    offset = jnp.where(distance > sub_count // 2, distance - sub_count, distance)
    cross = 2 * odd - 1
    classes = (2, -2, -cross, 0, cross)
    masks = jnp.concatenate(
        [jnp.where((offset == each) & (row >= 0), 1.0, 0.0) for each in classes], axis=0
    )
    counts = jnp.dot(masks.astype(BF16), upper, preferred_element_type=F32)
    key = jnp.zeros((clusters, width), F32)
    for number in range(len(classes)):
        at = number * high
        carried = jnp.full((1, 1), float(number * capacity - 1), F32)
        placed = []
        for cluster in range(clusters):
            count = counts[at + cluster : at + cluster + 1, :]
            placed.append(count + carried)
            carried = carried + count[:, width - 1 : width]
        key = key + masks[at : at + clusters, :] * jnp.concatenate(placed, axis=0)
    key = key.astype(I32)
    local = local[:clusters, :]
    key_ref[...] = key
    local_ref[...] = local
    digits = digit_rows(local, clusters)
    height = list_height(capacity, 1)
    for number, group in enumerate((PLUS, MINUS, CROSS)):
        lists_ref[number * height : (number + 1) * height, :] = filled(
            list_rows(key, digits, group, capacity), height
        )


def pack_kernel(
    capacity,
    rides,
    me_ref,
    one_ref,
    two_ref,
    three_ref,
    lists_ref,
    near_ref,
    diag_ref,
    far_ref,
    one_t_ref,
    *rest,
):
    quarter, eighth = two_ref.shape[0], three_ref.shape[0]
    tall = 2 * capacity // 128
    height = list_height(capacity, 1)
    tail = list_height(capacity, 2)
    plus, minus, relay = [
        lists_ref[number * height : number * height + tall, :] for number in range(3)
    ]
    up = filled([plus, relay], tail)
    down = filled([minus, relay], tail)
    near_ref[:quarter, :] = two_ref[...]
    near_ref[quarter : quarter + eighth, :] = three_ref[...]
    diag_ref[:eighth, :] = three_ref[...]
    far_ref[...] = three_ref[...]
    lanes = near_ref.shape[1]
    if rides:
        low = lax.rem(lax.div(me_ref[0], 2), 2) == 0
        slots = (
            (near_ref, quarter + eighth, jnp.where(low, up, down)),
            (diag_ref, eighth, jnp.where(low, down, up)),
        )
    else:
        slots = ((rest[0], 0, up), (rest[1], 0, down))
    for ref, at, value in slots:
        ref[at : at + tail, :] = jnp.zeros((tail, lanes), BF16)
        ref[at : at + tail, :128] = value.astype(BF16)
    one_t_ref[...] = one_ref[...].astype(F32).T.astype(BF16)


def lists_kernel(capacity, key_ref, local_ref, out_ref):
    clusters = key_ref.shape[0]
    key = key_ref[...]
    digits = digit_rows(local_ref[...], clusters)
    height = list_height(capacity, 1)
    for number, group in enumerate((PAIR, OWN)):
        rows = list_rows(key, digits, group, capacity)
        out_ref[number * height : (number + 1) * height, :] = filled(rows, height)


def relay_kernel(
    capacity,
    rides,
    me_ref,
    one_ref,
    two_ref,
    three_ref,
    near_ref,
    diag_ref,
    far_ref,
    lists_ref,
    *rest,
):
    wants_ref, bag_ref = rest[-1], rest[-2]
    quarter, eighth = two_ref.shape[0], three_ref.shape[0]
    tall = 2 * capacity // 128
    tail = list_height(capacity, 2)
    at = 0
    for value in (
        one_ref[...],
        two_ref[...],
        three_ref[...],
        near_ref[: quarter + eighth, :],
        diag_ref[:eighth, :],
        far_ref[...],
    ):
        bag_ref[at : at + value.shape[0], :] = value
        at += value.shape[0]
    if rides:
        beside = near_ref[quarter + eighth :, :128].astype(F32)
        opposite = diag_ref[eighth:, :128].astype(F32)
        low = lax.rem(lax.div(me_ref[0], 2), 2) == 0
        from_behind = jnp.where(low, opposite, beside)
        from_ahead = jnp.where(low, beside, opposite)
    else:
        from_behind = rest[0][:, :128].astype(F32)
        from_ahead = rest[1][:, :128].astype(F32)
    odd = lax.rem(me_ref[0], 2) == 1
    relayed = jnp.where(odd, from_behind, from_ahead)[tall : 2 * tall, :]
    bag_ref[at : at + tail, :] = jnp.zeros((tail, bag_ref.shape[1]), BF16)
    bag_ref[at : at + tail, :128] = filled([lists_ref[:tall, :], relayed], tail).astype(BF16)
    wants_ref[...] = filled([from_behind[:tall, :], from_ahead[:tall, :]], tail)


def direct_kernel(coords_ref, modes_ref, out_ref):
    leaves = coords_ref.shape[0]
    width = modes_ref.shape[2]
    for leaf in range(leaves):
        out_ref[:, leaf * width : (leaf + 1) * width] = jnp.dot(
            coords_ref[leaf], modes_ref[leaf], preferred_element_type=F32
        )


def gathered(disp_ref, wanted):
    depth = 256
    total = None
    for at in range(0, disp_ref.shape[1], depth):
        part = jnp.dot(
            disp_ref[:, at : at + depth], one_hot(wanted, at, depth), preferred_element_type=F32
        )
        total = part if total is None else total + part
    return total.astype(BF16)


def displace_kernel(
    capacity,
    me_ref,
    direct_ref,
    couple_ref,
    mine_ref,
    pair_ref,
    wants_ref,
    lists_ref,
    disp_ref,
    wanted_ref,
    cross_ref,
    anc_t,
):
    leaves, levels, block, width = couple_ref.shape
    me = me_ref[0]
    odd = lax.rem(me, 2)
    chip = lax.rem(lax.div(me, 2), GROUP)
    near = chip + 1 - 2 * lax.rem(chip, 2)
    far = lax.rem(chip + 2, GROUP)
    diag = lax.rem(near + 2, GROUP)
    half, quarter, eighth = block // 2, block // 4, block // 8

    def put(level, at, rows, value):
        anc_t[pl.ds(pl.multiple_of(level * block + at * rows, rows), rows), :] = value

    for core, ref in ((odd, mine_ref), (1 - odd, pair_ref)):
        pieces = (
            (0, core, half),
            (1, 2 * lax.rem(chip, 2) + core, quarter),
            (2, 2 * chip + core, eighth),
            (1, 2 * lax.rem(near, 2) + core, quarter),
            (2, 2 * near + core, eighth),
            (2, 2 * diag + core, eighth),
            (2, 2 * far + core, eighth),
        )
        start = 0
        for level, at, rows in pieces:
            put(level, at, rows, ref[start : start + rows, :])
            start += rows

    anc = anc_t[...].astype(F32).T.astype(BF16)
    for leaf in range(leaves):
        value = direct_ref[:, leaf * width : (leaf + 1) * width]
        for level in range(levels):
            value = value + jnp.dot(
                anc[:, level * block : (level + 1) * block],
                couple_ref[leaf, level],
                preferred_element_type=F32,
            )
        disp_ref[:, leaf * width : (leaf + 1) * width] = value.astype(BF16)

    tall = 2 * capacity // 128
    height = list_height(capacity, 1)
    tail = list_height(capacity, 2)
    ours = pair_ref[start : start + tail, :128]
    wants = wants_ref[...]
    wanted_ref[:, :capacity] = unpacked(wants, 0, capacity)
    wanted_ref[:, capacity : 2 * capacity] = unpacked(wants, tall, capacity)
    wanted_ref[:, 2 * capacity : 3 * capacity] = unpacked(ours, 0, capacity)
    wanted_ref[:, 3 * capacity :] = unpacked(lists_ref[height : 2 * height, :], 0, capacity)
    cross_ref[...] = gathered(disp_ref, unpacked(ours, tall, capacity))


def gather_kernel(capacity, first, disp_ref, wanted_ref, left_ref, right_ref):
    both = gathered(
        disp_ref, wanted_ref[:, first * capacity : (first + 2) * capacity]
    )
    left_ref[...] = both[:, :capacity]
    right_ref[...] = both[:, capacity:]


def permute_kernel(first, key_ref, operators_ref, out_ref):
    clusters, _, rows = operators_ref.shape
    tile = 384
    for part in range(out_ref.shape[0] // tile):
        for cluster in range(clusters):
            for at in range(0, tile, 128):
                pick = one_hot(
                    key_ref[cluster : cluster + 1, :], first + part * tile + at, 128
                )
                moved = jnp.dot(pick, operators_ref[cluster], preferred_element_type=F32)
                start = part * tile + at
                out_ref[start : start + 128, cluster * rows : (cluster + 1) * rows] = (
                    moved.astype(BF16)
                )


def early_kernel(capacity, moved_ref, pair_ref, own_ref, cross_ref, out_ref):
    clusters, _, rows = out_ref.shape
    for cluster in range(clusters):
        value = None
        for number, ref in enumerate((pair_ref, own_ref, cross_ref)):
            part = jnp.dot(
                ref[...],
                moved_ref[
                    number * capacity : (number + 1) * capacity,
                    cluster * rows : (cluster + 1) * rows,
                ],
                preferred_element_type=F32,
            )
            value = part if value is None else value + part
        out_ref[cluster] = value


def late_kernel(
    capacity,
    scale,
    weight_ref,
    compliance_ref,
    early_ref,
    moved_ref,
    plus_ref,
    minus_ref,
    stress_ref,
    energy_ref,
):
    clusters, modes, rows = stress_ref.shape
    points = energy_ref.shape[1]
    weight = jnp.broadcast_to(weight_ref[...], (8, modes)).T[:, :1]
    for cluster in range(clusters):
        value = early_ref[cluster]
        for number, ref in enumerate((plus_ref, minus_ref)):
            value = value + jnp.dot(
                ref[...],
                moved_ref[
                    number * capacity : (number + 1) * capacity,
                    cluster * rows : (cluster + 1) * rows,
                ],
                preferred_element_type=F32,
            )
        stress_ref[cluster] = value
        square = jnp.sum(value * value * weight, axis=0, keepdims=True)
        square = square * compliance_ref[cluster : cluster + 1, :]
        term = square[:, :points]
        for part in range(1, rows // points):
            term = term + square[:, part * points : (part + 1) * points]
        energy_ref[cluster : cluster + 1, :] = term * scale


def store_kernel(source_ref, target_hbm, sem):
    move = pltpu.make_async_copy(source_ref, target_hbm, sem)
    move.start()
    move.wait()


def share_kernel(at_ref, mine_ref, other_ref, out_ref):
    clusters, points = mine_ref.shape
    total = mine_ref[...] + other_ref[...]
    row = [total[c : c + 1, :] for c in range(clusters)]
    lanes = (clusters * points + 127) // 128 * 128
    if lanes > clusters * points:
        row.append(jnp.zeros((1, lanes - clusters * points), F32))
    flat = jnp.broadcast_to(jnp.concatenate(row, axis=1), (8, lanes))
    share = out_ref.shape[1]
    moved = pltpu.roll(flat, lanes - at_ref[0] * share, 1)
    out_ref[...] = moved[0:1, :share]


def shards(
    leaf_coords,
    leaf_modes,
    constraint_modes,
    sep_one,
    sep_two,
    sep_three,
    cluster_rows,
    operators,
    compliance,
    modal_weight,
):
    sub_count = lax.axis_size("sub")
    mode_count = lax.axis_size("mode")
    me = lax.axis_index("sub").astype(I32).reshape(1)
    leaves, modes, _ = leaf_coords.shape
    width = leaf_modes.shape[2]
    dof_count = leaves * width
    levels, block = constraint_modes.shape[1:3]
    clusters, slots = cluster_rows.shape
    rows = operators.shape[2]
    points = rows // 6
    capacity = clusters * slots // 4
    smem = pl.BlockSpec(memory_space=pltpu.SMEM)
    vmem = pl.BlockSpec(memory_space=VMEM)
    hbm = pl.BlockSpec(memory_space=pltpu.HBM)
    array = jax.ShapeDtypeStruct
    half, quarter, eighth = sep_one.shape[1], sep_two.shape[1], sep_three.shape[1]

    height = list_height(capacity, 1)
    tail = list_height(capacity, 2)
    rides = sub_count == 2 * GROUP
    two_t, three_t = sep_two.T, sep_three.T

    key, local, leaving = call(
        lambda *refs: index_kernel(sub_count, dof_count, capacity, *refs),
        (me, cluster_rows),
        (
            array((clusters, slots), I32),
            array((clusters, slots), I32),
            array((3 * height, 128), F32),
        ),
        8,
        1000000000,
        [smem, vmem],
    )
    extra = tail if rides else 0
    spare = () if rides else (array((tail, modes), BF16),) * 2
    near, diag, far, one_t, *loose = call(
        lambda *refs: pack_kernel(capacity, rides, *refs),
        (me, sep_one, two_t, three_t, leaving),
        (
            array((quarter + eighth + extra, modes), BF16),
            array((eighth + extra, modes), BF16),
            array((eighth, modes), BF16),
            array((half, modes), BF16),
        )
        + spare,
        4,
        10000000,
        [smem, vmem, vmem, vmem, vmem],
    )
    diag = swap_with(diag, "sub", 6)
    near = swap_with(near, "sub", 2)
    far = swap_with(far, "sub", 4)
    if loose:
        loose = [shift_by(loose[0], "sub", 2), shift_by(loose[1], "sub", -2)]
    lists = call(
        lambda *refs: lists_kernel(capacity, *refs),
        (key, local),
        array((2 * height, 128), F32),
        8,
        1000000000,
    )
    direct = call(
        direct_kernel,
        (leaf_coords, leaf_modes),
        array((modes, dof_count), F32),
        4,
        1500000000,
    )
    moved_near = call(
        lambda *refs: permute_kernel(2 * capacity, *refs),
        (key, operators),
        array((3 * capacity, clusters * rows), BF16),
        8,
        3000000000,
    )
    held = half + 2 * quarter + 4 * eighth + tail
    bag, wants = call(
        lambda *refs: relay_kernel(capacity, rides, *refs),
        (me, one_t, two_t, three_t, near, diag, far, lists, *loose),
        (array((held, modes), BF16), array((tail, 128), F32)),
        4,
        10000000,
        [smem] + [vmem] * (7 + len(loose)),
    )
    pair = swap_with(bag, "sub", 1)
    disp, wanted, cross = call(
        lambda *refs: displace_kernel(capacity, *refs),
        (me, direct, constraint_modes, bag, pair, wants, lists),
        (
            array((modes, dof_count), BF16),
            array((1, 4 * capacity), I32),
            array((modes, capacity), BF16),
        ),
        12,
        3000000000,
        [smem] + [vmem] * 6,
        [VMEM((levels * block, modes), BF16)],
    )
    cross = swap_across(cross, "sub")
    flow = array((modes, capacity), BF16)
    plus, minus = call(
        lambda *refs: gather_kernel(capacity, 0, *refs),
        (disp, wanted),
        (flow, flow),
        12,
        2000000000,
    )
    plus = shift_by(plus, "sub", -2)
    minus = shift_by(minus, "sub", 2)
    other, own = call(
        lambda *refs: gather_kernel(capacity, 2, *refs),
        (disp, wanted),
        (flow, flow),
        12,
        2000000000,
    )
    other = swap_with(other, "sub", 1)
    moved_far = call(
        lambda *refs: permute_kernel(0, *refs),
        (key, operators),
        array((2 * capacity, clusters * rows), BF16),
        8,
        2000000000,
    )
    early = call(
        lambda *refs: early_kernel(capacity, *refs),
        (moved_near, other, own, cross),
        array((clusters, modes, rows), F32),
        8,
        500000000,
    )
    stresses, energy = call(
        lambda *refs: late_kernel(capacity, 0.5 / (modes * mode_count), *refs),
        (modal_weight.reshape(1, modes), compliance, early, moved_far, plus, minus),
        (array((clusters, modes, rows), F32), array((clusters, points), F32)),
        8,
        500000000,
    )
    mask = 1
    while 2 * mask < mode_count:
        energy = energy + swap_with(energy, "mode", mask)
        mask *= 2
    arrived = swap_with(energy, "mode", mask)
    stresses = pl.pallas_call(
        store_kernel,
        out_shape=array((clusters, modes, rows), F32),
        in_specs=[vmem],
        out_specs=hbm,
        scratch_shapes=[pltpu.SemaphoreType.DMA],
        compiler_params=pltpu.CompilerParams(vmem_limit_bytes=4 * 1024 * 1024),
        cost_estimate=pl.CostEstimate(
            flops=500000000, bytes_accessed=2000000, transcendentals=0
        ),
        name="store",
    )(stresses)
    at = lax.axis_index("mode").astype(I32).reshape(1)
    share = clusters * points // mode_count
    strain_energy = call(
        share_kernel,
        (at, energy, arrived),
        array((1, share), F32),
        4,
        1000,
        [smem, vmem, vmem],
    )
    return (stresses, strain_energy.reshape(share))


def solution(mesh):
    return jax.shard_map(
        shards,
        mesh=mesh,
        in_specs=(
            P("sub", "mode", None),
            P("sub", None, None),
            P("sub", None, None, None),
            P("mode", "sub"),
            P("mode", "sub"),
            P("mode", "sub"),
            P("sub", None),
            P("sub", None, None),
            P("sub", None),
            P("mode"),
        ),
        out_specs=(P("sub", "mode", None), P(("sub", "mode"))),
        check_vma=False,
    )
```

time: 50.1 us -> 42.5 us (0.85)
  local copies, waits for them, and re-layouts: 9.51 us -> 0.76 us
  waiting for transfers between devices: 9.36 us -> 12.6 us
  starting transfers between devices: 15 us -> 13.3 us
    unnamed x26 -> x22, local copies, waits for them, and re-layouts: 9.4 us -> 0.76 us
    ppermute x5 -> x2, starting transfers between devices: 7.58 us -> 2.08 us  [shift_by(): lax.ppermute(value, axis, [(i, (i + by) % peers) for i in range(peers)])]
    ppermute x4 -> x7, starting transfers between devices: 4.74 us -> 8.8 us  [swap_with(): lax.ppermute(value, axis, [(i, i ^ mask) for i in range(lax.axis_size(axi...]
    ppermute x4 -> x7, waiting for transfers between devices: 2.99 us -> 6.02 us  [swap_with(): lax.ppermute(value, axis, [(i, i ^ mask) for i in range(lax.axis_size(axi...]
    ppermute x1, waiting for transfers between devices: 4.55 us -> 6.62 us  [swap_across(): lax.ppermute(value, axis, [(i, (i + 2 * (i % 2) - 1) % peers) for i in ra...]
    ppermute x5 -> x2, waiting for transfers between devices: 1.82 us -> 0.01 us  [shift_by(): lax.ppermute(value, axis, [(i, (i + by) % peers) for i in range(peers)])]
    pallas_call x12 -> x13, Pallas kernels: 14.1 us -> 13.7 us  [call(): pl.pallas_call(kernel, out_shape=outputs, in_specs=specs or [vmem] * len(...]
  transfers between devices with their start and end apart: 10 -> 10, of which waited for: 4 -> 4; matrix products, arithmetic and copies ran while one was open for 0% -> 0% of each run, Pallas kernels for 14% -> 15%
where the time goes in v3:
time: 42.5 us; the launch traced here: 42.3 us
  Pallas kernels  14.6 us (34%)
  starting transfers between devices  13.3 us (31%)
  waiting for transfers between devices  12.6 us (30%)
  between operations  0.92 us (2%)
  local copies, waits for them, and re-layouts  0.76 us (2%)
    pallas_call x13, Pallas kernels, call(): pl.pallas_call(kernel, out_shape=outputs, in_specs=specs or [vmem] * len(...  13.7 us
    ppermute x7, starting transfers between devices, swap_with(): lax.ppermute(value, axis, [(i, i ^ mask) for i in range(lax.axis_size(axi...  8.8 us
    ppermute x1, waiting for transfers between devices, swap_across(): lax.ppermute(value, axis, [(i, (i + 2 * (i % 2) - 1) % peers) for i in ra...  6.62 us
    ppermute x7, waiting for transfers between devices, swap_with(): lax.ppermute(value, axis, [(i, i ^ mask) for i in range(lax.axis_size(axi...  6.02 us
    ppermute x1, starting transfers between devices, swap_across(): lax.ppermute(value, axis, [(i, (i + 2 * (i % 2) - 1) % peers) for i in ra...  2.45 us
    ppermute x2, starting transfers between devices, shift_by(): lax.ppermute(value, axis, [(i, (i + by) % peers) for i in range(peers)])  2.08 us
    pallas_call x1, Pallas kernels, shards(): pl.pallas_call(store_kernel, out_shape=array((clusters, modes, rows), F32...  0.92 us
  transfers between devices with their start and end apart: 10, of which 4 were waited for; matrix products, arithmetic and copies ran while one was open for 0% of the time, Pallas kernels for 15%

profile of v3, /device:TPU:0, one launch (start us, length us, event | category | flops | bytes accessed | tf_op | source)
XLA Modules:
  0.0 42.3 jit_solution(15571964799990658431)
XLA Ops:
  0.7 0.7 %copy-done.8 = s32[3,512]{1,0:T(4,128)S(1)} copy-done((s32[3,512]{1,0:T(4,128)S(1)}, s32[3,512]{1,0:T(4,128)}, u32[]{:S(2)}) %copy-start.8) | copy-done | bytes 6168
  1.4 1.4 %shard_map.113 = (s32[3,512]{1,0:T(4,128)S(1)}, s32[3,512]{1,0:T(4,128)S(1)}, f32[48,128]{1,0:T(8,128)S(1)}) custom-call(s32[1]{0:T(128)} %bitcast.1.refs_0_, s32[3,512]{1,0:T(4,128)S(1)} %copy-done.8), custom_call_target="tpu_custom_call" | custom-call | flops 1000000000 | bytes 6148 | tf_op jit(solution)/shard_map/pallas_call | solution.py:39
  2.9 3.0 %collective-permute-start = (bf16[112,192]{1,0:T(8,128)(2,1)S(1)}, bf16[112,192]{1,0:T(8,128)(2,1)S(1)}, u32[]{:S(2)}, u32[]{:S(2)}) collective-permute-start(bf16[112,192]{1,0:T(8,128)(2,1)S(1)} %get-tuple-element.23), channel_id=1, source_target_pairs={{0,8},{4,12},{8,0},{12,4},{16,24},{20,28},{24,16},{28,20},{1,9},{5... | collective-permute-start | bytes 129032 | tf_op jit(solution)/shard_map/ppermute | solution.py:25
  5.9 1.5 %collective-permute-start.1 = (bf16[48,192]{1,0:T(8,128)(2,1)S(1)}, bf16[48,192]{1,0:T(8,128)(2,1)S(1)}, u32[]{:S(2)}, u32[]{:S(2)}) collective-permute-start(bf16[48,192]{1,0:T(8,128)(2,1)S(1)} %get-tuple-element.24), channel_id=1, source_target_pairs={{0,24},{4,28},{8,16},{12,20},{16,8},{20,12},{24,0},{28,4},{1,25},{... | collective-permute-start | bytes 55304 | tf_op jit(solution)/shard_map/ppermute | solution.py:25
  7.5 0.7 %shard_map.117.refs_7_.refs_6_ = f32[32,128]{1,0:T(8,128)S(1)} custom-call(s32[3,512]{1,0:T(4,128)S(1)} %get-tuple-element.20.refs_0_, s32[3,512]{1,0:T(4,128)S(1)} %get-tuple-element.26.refs_1_), custom_call_target="tpu_custom_call" | custom-call | flops 1000000000 | bytes 12288 | tf_op jit(solution)/shard_map/pallas_call | solution.py:39
  8.2 3.0 %collective-permute-done.2.refs_6_ = bf16[32,192]{1,0:T(8,128)(2,1)S(1)} collective-permute-done((bf16[32,192]{1,0:T(8,128)(2,1)S(1)}, bf16[32,192]{1,0:T(8,128)(2,1)S(1)}, u32[]{:S(2)}, u32[]{:S(2)}) %collective-permute-start.2) | collective-permute-done | bytes 12320 | tf_op jit(solution)/shard_map/ppermute | solution.py:25
  11.3 2.0 %shard_map.114.refs_0_ = bf16[1152,1152]{1,0:T(8,128)(2,1)S(1)} custom-call(s32[3,512]{1,0:T(4,128)S(1)} %get-tuple-element.20.refs_0_, bf16[3,512,384]{2,1,0:T(8,128)(2,1)S(1)} %copy-done.5), custom_call_target="tpu_custom_call" | custom-call | flops 3000000000 | bytes 1185792 | tf_op jit(solution)/shard_map/pallas_call | solution.py:39
  13.3 0.5 %shard_map.115.refs_1_ = f32[192,4096]{1,0:T(8,128)S(1)} custom-call(bf16[8,192,128]{2,1,0:T(8,128)(2,1)S(1)} %copy-done.7, bf16[8,128,512]{2,1,0:T(8,128)(2,1)S(1)} %copy-done.6), custom_call_target="tpu_custom_call" | custom-call | flops 1500000000 | bytes 1441792 | tf_op jit(solution)/shard_map/pallas_call | solution.py:39
  13.9 2.4 %shard_map.119 = (bf16[192,4096]{1,0:T(8,128)(2,1)S(1)}, s32[1,1536]{1,0:T(1,128)S(1)}, bf16[192,384]{1,0:T(8,128)(2,1)S(1)}) custom-call(s32[1]{0:T(128)} %bitcast.1.refs_0_, f32[192,4096]{1,0:T(8,128)S(1)} %shard_map.115.refs_1_, bf16[8,3,256,512]{3,2,1,0:T(8,128)(2,1)S(1)} %bitcast.12, bf16[400,192]{1,0:T(8,128)(2,1)S(1)} %get-tuple-element.27.refs_3_, ...), custom_call_target="tpu_custom_call" | custom-call | flops 3000000000 | bytes 9768964 | tf_op jit(solution)/shard_map/pallas_call | solution.py:39
  16.3 1.4 %shard_map.123 = (bf16[192,384]{1,0:T(8,128)(2,1)S(1)}, bf16[192,384]{1,0:T(8,128)(2,1)S(1)}) custom-call(bf16[192,4096]{1,0:T(8,128)(2,1)S(1)} %get-tuple-element.29.refs_0_, s32[1,1536]{1,0:T(1,128)S(1)} %get-tuple-element.30.refs_1_), custom_call_target="tpu_custom_call" | custom-call | flops 2000000000 | bytes 1579008 | tf_op jit(solution)/shard_map/pallas_call | solution.py:39
  17.7 1.4 %shard_map.120 = (bf16[192,384]{1,0:T(8,128)(2,1)S(1)}, bf16[192,384]{1,0:T(8,128)(2,1)S(1)}) custom-call(bf16[192,4096]{1,0:T(8,128)(2,1)S(1)} %get-tuple-element.29.refs_0_, s32[1,1536]{1,0:T(1,128)S(1)} %get-tuple-element.30.refs_1_), custom_call_target="tpu_custom_call" | custom-call | flops 2000000000 | bytes 1579008 | tf_op jit(solution)/shard_map/pallas_call | solution.py:39
  19.1 1.5 %collective-permute-start.6 = (bf16[192,384]{1,0:T(8,128)(2,1)S(1)}, bf16[192,384]{1,0:T(8,128)(2,1)S(1)}, u32[]{:S(2)}, u32[]{:S(2)}) collective-permute-start(bf16[192,384]{1,0:T(8,128)(2,1)S(1)} %get-tuple-element.34), channel_id=1, source_target_pairs={{0,24},{4,28},{8,0},{12,4},{16,8},{20,12},{24,16},{28,20},{1,25},{... | collective-permute-start | bytes 442376 | tf_op jit(solution)/shard_map/ppermute | solution.py:21
  20.6 0.6 %collective-permute-start.7 = (bf16[192,384]{1,0:T(8,128)(2,1)S(1)}, bf16[192,384]{1,0:T(8,128)(2,1)S(1)}, u32[]{:S(2)}, u32[]{:S(2)}) collective-permute-start(bf16[192,384]{1,0:T(8,128)(2,1)S(1)} %get-tuple-element.35), channel_id=1, source_target_pairs={{0,8},{4,12},{8,16},{12,20},{16,24},{20,28},{24,0},{28,4},{1,9},{5... | collective-permute-start | bytes 442376 | tf_op jit(solution)/shard_map/ppermute | solution.py:21
  21.2 2.5 %collective-permute-start.5 = (bf16[192,384]{1,0:T(8,128)(2,1)S(1)}, bf16[192,384]{1,0:T(8,128)(2,1)S(1)}, u32[]{:S(2)}, u32[]{:S(2)}) collective-permute-start(bf16[192,384]{1,0:T(8,128)(2,1)S(1)} %get-tuple-element.33), channel_id=1, source_target_pairs={{0,28},{4,8},{8,4},{12,16},{16,12},{20,24},{24,20},{28,0},{1,29},{... | collective-permute-start | bytes 442376 | tf_op jit(solution)/shard_map/ppermute | solution.py:30
  23.7 1.4 %shard_map.122.refs_3_ = bf16[768,1152]{1,0:T(8,128)(2,1)S(1)} custom-call(s32[3,512]{1,0:T(4,128)S(1)} %get-tuple-element.20.refs_0_, bf16[3,512,384]{2,1,0:T(8,128)(2,1)S(1)} %copy-done.5), custom_call_target="tpu_custom_call" | custom-call | flops 2000000000 | bytes 1185792 | tf_op jit(solution)/shard_map/pallas_call | solution.py:39
  25.1 6.6 %collective-permute-done.5.refs_3_ = bf16[192,384]{1,0:T(8,128)(2,1)S(1)} collective-permute-done((bf16[192,384]{1,0:T(8,128)(2,1)S(1)}, bf16[192,384]{1,0:T(8,128)(2,1)S(1)}, u32[]{:S(2)}, u32[]{:S(2)}) %collective-permute-start.5) | collective-permute-done | bytes 147488 | tf_op jit(solution)/shard_map/ppermute | solution.py:30
  31.7 1.0 %shard_map.121.refs_2_ = f32[3,192,384]{2,1,0:T(8,128)S(1)} custom-call(bf16[1152,1152]{1,0:T(8,128)(2,1)S(1)} %shard_map.114.refs_0_, bf16[192,384]{1,0:T(8,128)(2,1)S(1)} %collective-permute-done.4.refs_1_, bf16[192,384]{1,0:T(8,128)(2,1)S(1)} %get-tuple-element.32.refs_2_, bf16[192,384]{1,0:T(8,128)(2,1)S(1)} %collective-permute-done.5.refs_3_), custom_call_target="tpu_custom_call" | custom-call | flops 500000000 | bytes 3096576 | tf_op jit(solution)/shard_map/pallas_call | solution.py:39
  32.8 0.8 %shard_map.124 = (f32[3,192,384]{2,1,0:T(8,128)S(1)}, f32[3,64]{1,0:T(4,128)S(1)}) custom-call(f32[1,192]{1,0:T(1,128)S(1)} %bitcast.10, f32[3,384]{1,0:T(4,128)S(1)} %copy-done.3, f32[3,192,384]{2,1,0:T(8,128)S(1)} %shard_map.121.refs_2_, bf16[768,1152]{1,0:T(8,128)(2,1)S(1)} %shard_map.122.refs_3_, bf16[192,384]{1,0:T(8,128)(2,1)S(1)} %collective-permute-done.6.refs_4_, ...), custom_call_target="tpu_custom_call" | custom-call | flops 500000000 | bytes 2954496 | tf_op jit(solution)/shard_map/pallas_call | solution.py:39
  33.6 1.6 %collective-permute-start.8 = (f32[3,64]{1,0:T(4,128)S(1)}, f32[3,64]{1,0:T(4,128)S(1)}, u32[]{:S(2)}, u32[]{:S(2)}) collective-permute-start(f32[3,64]{1,0:T(4,128)S(1)} %get-tuple-element.37), channel_id=1, source_target_pairs={{0,1},{1,0},{2,3},{3,2},{4,5},{5,4},{6,7},{7,6},{8,9},{9,8},{10,11... | collective-permute-start | bytes 2312 | tf_op jit(solution)/shard_map/ppermute | solution.py:25
  35.2 2.0 %collective-permute-done.8 = f32[3,64]{1,0:T(4,128)S(1)} collective-permute-done((f32[3,64]{1,0:T(4,128)S(1)}, f32[3,64]{1,0:T(4,128)S(1)}, u32[]{:S(2)}, u32[]{:S(2)}) %collective-permute-start.8) | collective-permute-done | bytes 800 | tf_op jit(solution)/shard_map/ppermute | solution.py:25
  37.2 2.6 %collective-permute-start.9 = (f32[3,64]{1,0:T(4,128)S(1)}, f32[3,64]{1,0:T(4,128)S(1)}, u32[]{:S(2)}, u32[]{:S(2)}) collective-permute-start(f32[3,64]{1,0:T(4,128)S(1)} %add.3.mine_ref), channel_id=1, source_target_pairs={{0,2},{1,3},{2,0},{3,1},{4,6},{5,7},{6,4},{7,5},{8,10},{9,11},{10,... | collective-permute-start | bytes 2312 | tf_op jit(solution)/shard_map/ppermute | solution.py:25
  39.7 0.9 %store.1 = f32[3,192,384]{2,1,0:T(8,128)} custom-call(f32[3,192,384]{2,1,0:T(8,128)S(1)} %get-tuple-element.36.source_ref), custom_call_target="tpu_custom_call" | custom-call | flops 500000000 | bytes 2000000 | tf_op jit(solution)/shard_map/store/pallas_call | solution.py:582
  40.7 1.0 %collective-permute-done.9.other_ref = f32[3,64]{1,0:T(4,128)S(1)} collective-permute-done((f32[3,64]{1,0:T(4,128)S(1)}, f32[3,64]{1,0:T(4,128)S(1)}, u32[]{:S(2)}, u32[]{:S(2)}) %collective-permute-start.9) | collective-permute-done | bytes 800 | tf_op jit(solution)/shard_map/ppermute | solution.py:25
  41.7 0.7 %shard_map.125 = f32[1,48]{1,0:T(1,128)} custom-call(s32[1]{0:T(128)} %bitcast.4.at_ref, f32[3,64]{1,0:T(4,128)S(1)} %add.3.mine_ref, f32[3,64]{1,0:T(4,128)S(1)} %collective-permute-done.9.other_ref), custom_call_target="tpu_custom_call" | custom-call | flops 1000 | bytes 1540 | tf_op jit(solution)/shard_map/pallas_call | solution.py:39
  (34 shorter events, 0.3 us)
Async XLA Ops:
  0.6 2.1 %copy-start = (bf16[192,64]{0,1:T(8,128)(2,1)S(1)}, bf16[192,64]{0,1:T(8,128)(2,1)}, u32[]{:S(2)}) copy-start(bf16[192,64]{0,1:T(8,128)(2,1)} %param.14) | copy-start | bytes 73732
  0.6 2.1 %copy-start.1 = (bf16[192,32]{0,1:T(8,128)(2,1)S(1)}, bf16[192,32]{0,1:T(8,128)(2,1)}, u32[]{:S(2)}) copy-start(bf16[192,32]{0,1:T(8,128)(2,1)} %param.15) | copy-start | bytes 36868
  0.7 2.1 %copy-start.2 = (bf16[192,128]{1,0:T(8,128)(2,1)S(1)}, bf16[192,128]{1,0:T(8,128)(2,1)}, u32[]{:S(2)}) copy-start(bf16[192,128]{1,0:T(8,128)(2,1)} %refs_1_.7) | copy-start | bytes 147460
  0.7 0.7 %copy-start.8 = (s32[3,512]{1,0:T(4,128)S(1)}, s32[3,512]{1,0:T(4,128)}, u32[]{:S(2)}) copy-start(s32[3,512]{1,0:T(4,128)} %refs_1_.5) | copy-start | bytes 18436
  2.7 8.6 %copy-start.5 = (bf16[3,512,384]{2,1,0:T(8,128)(2,1)S(1)}, bf16[3,512,384]{2,1,0:T(8,128)(2,1)}, u32[]{:S(2)}) copy-start(bf16[3,512,384]{2,1,0:T(8,128)(2,1)} %refs_1_.8) | copy-start | bytes 3538948
  2.9 8.3 %collective-permute-start = (bf16[112,192]{1,0:T(8,128)(2,1)S(1)}, bf16[112,192]{1,0:T(8,128)(2,1)S(1)}, u32[]{:S(2)}, u32[]{:S(2)}) collective-permute-start(bf16[112,192]{1,0:T(8,128)(2,1)S(1)} %get-tuple-element.23), channel_id=1, source_target_pairs={{0,8},{4,12},{8,0},{12,4},{16,24},{20,28},{24,16},{28,20},{1,9},{5... | collective-permute-start | bytes 129032 | tf_op jit(solution)/shard_map/ppermute | solution.py:25
  5.9 5.2 %collective-permute-start.1 = (bf16[48,192]{1,0:T(8,128)(2,1)S(1)}, bf16[48,192]{1,0:T(8,128)(2,1)S(1)}, u32[]{:S(2)}, u32[]{:S(2)}) collective-permute-start(bf16[48,192]{1,0:T(8,128)(2,1)S(1)} %get-tuple-element.24), channel_id=1, source_target_pairs={{0,24},{4,28},{8,16},{12,20},{16,8},{20,12},{24,0},{28,4},{1,25},{... | collective-permute-start | bytes 55304 | tf_op jit(solution)/shard_map/ppermute | solution.py:25
  7.4 3.7 %collective-permute-start.2 = (bf16[32,192]{1,0:T(8,128)(2,1)S(1)}, bf16[32,192]{1,0:T(8,128)(2,1)S(1)}, u32[]{:S(2)}, u32[]{:S(2)}) collective-permute-start(bf16[32,192]{1,0:T(8,128)(2,1)S(1)} %get-tuple-element.25), channel_id=1, source_target_pairs={{0,16},{4,20},{8,24},{12,28},{16,0},{20,4},{24,8},{28,12},{1,17},{... | collective-permute-start | bytes 36872 | tf_op jit(solution)/shard_map/ppermute | solution.py:25
  7.5 6.4 %slice-start = ((s8[6291456]{0:T(1024)(128)(4,1)}), s8[4194304]{0:T(1024)(128)(4,1)S(1)}, s32[]{:S(2)}) async-start(s8[6291456]{0:T(1024)(128)(4,1)} %bitcast.11), calls=%async_computation | async-start | bytes 8388608
  11.2 2.1 %copy-start.6 = (bf16[8,128,512]{2,1,0:T(8,128)(2,1)S(1)}, bf16[8,128,512]{2,1,0:T(8,128)(2,1)}, u32[]{:S(2)}) copy-start(bf16[8,128,512]{2,1,0:T(8,128)(2,1)} %modes_ref.1) | copy-start | bytes 3145732
  11.2 2.1 %copy-start.7 = (bf16[8,192,128]{2,1,0:T(8,128)(2,1)S(1)}, bf16[8,192,128]{2,1,0:T(8,128)(2,1)}, u32[]{:S(2)}) copy-start(bf16[8,192,128]{2,1,0:T(8,128)(2,1)} %coords_ref.1) | copy-start | bytes 1179652
  11.2 2.7 %slice-start.1 = ((s8[6291456]{0:T(1024)(128)(4,1)}), s8[2097152]{0:T(1024)(128)(4,1)S(1)}, s32[]{:S(2)}) async-start(s8[6291456]{0:T(1024)(128)(4,1)} %bitcast.11), calls=%async_computation.1 | async-start | bytes 4194304
  11.2 2.7 %collective-permute-start.3 = (bf16[400,192]{1,0:T(8,128)(2,1)S(1)}, bf16[400,192]{1,0:T(8,128)(2,1)S(1)}, u32[]{:S(2)}, u32[]{:S(2)}) collective-permute-start(bf16[400,192]{1,0:T(8,128)(2,1)S(1)} %get-tuple-element.27.refs_3_), channel_id=1, source_target_pairs={{0,4},{4,0},{8,12},{12,8},{16,20},{20,16},{24,28},{28,24},{1,5},{5... | collective-permute-start | bytes 460808 | tf_op jit(solution)/shard_map/ppermute | solution.py:25
  19.1 13.6 %collective-permute-start.6 = (bf16[192,384]{1,0:T(8,128)(2,1)S(1)}, bf16[192,384]{1,0:T(8,128)(2,1)S(1)}, u32[]{:S(2)}, u32[]{:S(2)}) collective-permute-start(bf16[192,384]{1,0:T(8,128)(2,1)S(1)} %get-tuple-element.34), channel_id=1, source_target_pairs={{0,24},{4,28},{8,0},{12,4},{16,8},{20,12},{24,16},{28,20},{1,25},{... | collective-permute-start | bytes 442376 | tf_op jit(solution)/shard_map/ppermute | solution.py:21
  20.6 12.1 %collective-permute-start.7 = (bf16[192,384]{1,0:T(8,128)(2,1)S(1)}, bf16[192,384]{1,0:T(8,128)(2,1)S(1)}, u32[]{:S(2)}, u32[]{:S(2)}) collective-permute-start(bf16[192,384]{1,0:T(8,128)(2,1)S(1)} %get-tuple-element.35), channel_id=1, source_target_pairs={{0,8},{4,12},{8,16},{12,20},{16,24},{20,28},{24,0},{28,4},{1,9},{5... | collective-permute-start | bytes 442376 | tf_op jit(solution)/shard_map/ppermute | solution.py:21
  21.2 3.9 %collective-permute-start.4 = (bf16[192,384]{1,0:T(8,128)(2,1)S(1)}, bf16[192,384]{1,0:T(8,128)(2,1)S(1)}, u32[]{:S(2)}, u32[]{:S(2)}) collective-permute-start(bf16[192,384]{1,0:T(8,128)(2,1)S(1)} %get-tuple-element.31), channel_id=1, source_target_pairs={{0,4},{4,0},{8,12},{12,8},{16,20},{20,16},{24,28},{28,24},{1,5},{5... | collective-permute-start | bytes 442376 | tf_op jit(solution)/shard_map/ppermute | solution.py:25
  21.2 10.5 %collective-permute-start.5 = (bf16[192,384]{1,0:T(8,128)(2,1)S(1)}, bf16[192,384]{1,0:T(8,128)(2,1)S(1)}, u32[]{:S(2)}, u32[]{:S(2)}) collective-permute-start(bf16[192,384]{1,0:T(8,128)(2,1)S(1)} %get-tuple-element.33), channel_id=1, source_target_pairs={{0,28},{4,8},{8,4},{12,16},{16,12},{20,24},{24,20},{28,0},{1,29},{... | collective-permute-start | bytes 442376 | tf_op jit(solution)/shard_map/ppermute | solution.py:30
  25.0 7.7 %copy-start.3 = (f32[3,384]{1,0:T(4,128)S(1)}, f32[3,384]{1,0:T(4,128)}, u32[]{:S(2)}) copy-start(f32[3,384]{1,0:T(4,128)} %refs_1_.9) | copy-start | bytes 13828
  25.1 7.7 %copy-start.4 = (f32[192]{0:T(256)S(1)}, f32[192]{0:T(256)}, u32[]{:S(2)}) copy-start(f32[192]{0:T(256)} %param.19) | copy-start | bytes 2308
  33.6 3.6 %collective-permute-start.8 = (f32[3,64]{1,0:T(4,128)S(1)}, f32[3,64]{1,0:T(4,128)S(1)}, u32[]{:S(2)}, u32[]{:S(2)}) collective-permute-start(f32[3,64]{1,0:T(4,128)S(1)} %get-tuple-element.37), channel_id=1, source_target_pairs={{0,1},{1,0},{2,3},{3,2},{4,5},{5,4},{6,7},{7,6},{8,9},{9,8},{10,11... | collective-permute-start | bytes 2312 | tf_op jit(solution)/shard_map/ppermute | solution.py:25
  37.2 4.5 %collective-permute-start.9 = (f32[3,64]{1,0:T(4,128)S(1)}, f32[3,64]{1,0:T(4,128)S(1)}, u32[]{:S(2)}, u32[]{:S(2)}) collective-permute-start(f32[3,64]{1,0:T(4,128)S(1)} %add.3.mine_ref), channel_id=1, source_target_pairs={{0,2},{1,3},{2,0},{3,1},{4,6},{5,7},{6,4},{7,5},{8,10},{9,11},{10,... | collective-permute-start | bytes 2312 | tf_op jit(solution)/shard_map/ppermute | solution.py:25

commit v4 on v3

--- a/solution.py
+++ b/solution.py
@@ -55,34 +55,10 @@
     return jnp.where(hit, jnp.ones((), BF16), jnp.zeros((), BF16))
 
 
-def list_rows(key, digits, group, capacity):
-    total = None
-    for cluster, values in enumerate(digits):
-        pick = jnp.concatenate(
-            [
-                one_hot(key[cluster : cluster + 1, :], group * capacity + at, 128)
-                for at in range(0, capacity, 128)
-            ],
-            axis=0,
-        )
-        part = lax.dot_general(
-            values, pick, (((1,), (1,)), ((), ())), preferred_element_type=F32
-        )
-        total = part if total is None else total + part
-    return [
-        total[digit : digit + 1, at : at + 128]
-        for digit in (0, 1)
-        for at in range(0, capacity, 128)
-    ]
-
-
-def digit_rows(local, clusters):
-    high = lax.div(local, jnp.int32(BASE))
-    low = local - high * BASE
-    return [
-        jnp.concatenate([high[c : c + 1, :], low[c : c + 1, :]], axis=0).astype(F32).astype(BF16)
-        for c in range(clusters)
-    ]
+def list_rows(lists, group, capacity):
+    parts = capacity // 128
+    low = lists.shape[0] // 2 + group * parts
+    return [lists[group * parts : (group + 1) * parts, :], lists[low : low + parts, :]]
 
 
 def filled(rows, count):
@@ -104,7 +80,7 @@
     return (2 * capacity // 128 * lists + 15) // 16 * 16
 
 
-def index_kernel(sub_count, dof_count, capacity, me_ref, rows_ref, key_ref, local_ref, lists_ref):
+def index_kernel(sub_count, dof_count, capacity, me_ref, rows_ref, key_ref, lists_ref):
     clusters, width = rows_ref.shape
     high = (clusters + 7) // 8 * 8
     row = jnp.concatenate(
@@ -137,15 +113,27 @@
             carried = carried + count[:, width - 1 : width]
         key = key + masks[at : at + clusters, :] * jnp.concatenate(placed, axis=0)
     key = key.astype(I32)
-    local = local[:clusters, :]
     key_ref[...] = key
-    local_ref[...] = local
-    digits = digit_rows(local, clusters)
-    height = list_height(capacity, 1)
-    for number, group in enumerate((PLUS, MINUS, CROSS)):
-        lists_ref[number * height : (number + 1) * height, :] = filled(
-            list_rows(key, digits, group, capacity), height
+    tall = lists_ref.shape[0] // 2
+    rank_high = lax.div(key, jnp.int32(128))
+    rank_low = key - rank_high * 128
+    digit_high = lax.div(local, jnp.int32(BASE))
+    digits = (digit_high.astype(F32), (local - digit_high * BASE).astype(F32))
+    ids = lax.broadcasted_iota(I32, (tall, width), 0)
+    values, picks = [], []
+    for cluster in range(clusters):
+        at = slice(cluster, cluster + 1)
+        hit = ids == rank_high[at, :]
+        values.append(
+            jnp.concatenate([jnp.where(hit, digit[at, :], 0.0) for digit in digits], axis=0)
         )
+        picks.append(one_hot(rank_low[at, :], 0, 128))
+    lists_ref[...] = lax.dot_general(
+        jnp.concatenate(values, axis=1).astype(BF16),
+        jnp.concatenate(picks, axis=1),
+        (((1,), (1,)), ((), ())),
+        preferred_element_type=F32,
+    )
 
 
 def pack_kernel(
@@ -163,14 +151,11 @@
     *rest,
 ):
     quarter, eighth = two_ref.shape[0], three_ref.shape[0]
-    tall = 2 * capacity // 128
-    height = list_height(capacity, 1)
     tail = list_height(capacity, 2)
-    plus, minus, relay = [
-        lists_ref[number * height : number * height + tall, :] for number in range(3)
-    ]
-    up = filled([plus, relay], tail)
-    down = filled([minus, relay], tail)
+    lists = lists_ref[...]
+    relay = list_rows(lists, CROSS, capacity)
+    up = filled(list_rows(lists, PLUS, capacity) + relay, tail)
+    down = filled(list_rows(lists, MINUS, capacity) + relay, tail)
     near_ref[:quarter, :] = two_ref[...]
     near_ref[quarter : quarter + eighth, :] = three_ref[...]
     diag_ref[:eighth, :] = three_ref[...]
@@ -188,16 +173,6 @@
         ref[at : at + tail, :] = jnp.zeros((tail, lanes), BF16)
         ref[at : at + tail, :128] = value.astype(BF16)
     one_t_ref[...] = one_ref[...].astype(F32).T.astype(BF16)
-
-
-def lists_kernel(capacity, key_ref, local_ref, out_ref):
-    clusters = key_ref.shape[0]
-    key = key_ref[...]
-    digits = digit_rows(local_ref[...], clusters)
-    height = list_height(capacity, 1)
-    for number, group in enumerate((PAIR, OWN)):
-        rows = list_rows(key, digits, group, capacity)
-        out_ref[number * height : (number + 1) * height, :] = filled(rows, height)
 
 
 def relay_kernel(
@@ -240,7 +215,9 @@
     odd = lax.rem(me_ref[0], 2) == 1
     relayed = jnp.where(odd, from_behind, from_ahead)[tall : 2 * tall, :]
     bag_ref[at : at + tail, :] = jnp.zeros((tail, bag_ref.shape[1]), BF16)
-    bag_ref[at : at + tail, :128] = filled([lists_ref[:tall, :], relayed], tail).astype(BF16)
+    bag_ref[at : at + tail, :128] = filled(
+        list_rows(lists_ref[...], PAIR, capacity) + [relayed], tail
+    ).astype(BF16)
     wants_ref[...] = filled([from_behind[:tall, :], from_ahead[:tall, :]], tail)
 
 
@@ -264,67 +241,67 @@
     return total.astype(BF16)
 
 
+def coupled(me, core, couple_ref, bag_ref):
+    leaves, _, block, width = couple_ref.shape
+    chip = lax.rem(lax.div(me, 2), GROUP)
+    near = chip + 1 - 2 * lax.rem(chip, 2)
+    far = lax.rem(chip + 2, GROUP)
+    diag = lax.rem(near + 2, GROUP)
+    half, quarter, eighth = block // 2, block // 4, block // 8
+    pieces = (
+        (0, core, half),
+        (1, 2 * lax.rem(chip, 2) + core, quarter),
+        (2, 2 * chip + core, eighth),
+        (1, 2 * lax.rem(near, 2) + core, quarter),
+        (2, 2 * near + core, eighth),
+        (2, 2 * diag + core, eighth),
+        (2, 2 * far + core, eighth),
+    )
+    held = sum(rows for level, at, rows in pieces)
+    anc = bag_ref[:held, :].astype(F32).T.astype(BF16)
+    for leaf in range(leaves):
+        weights = jnp.concatenate(
+            [
+                couple_ref[leaf, level, pl.ds(pl.multiple_of(at * rows, rows), rows), :]
+                for level, at, rows in pieces
+            ],
+            axis=0,
+        )
+        columns = slice(leaf * width, (leaf + 1) * width)
+        yield columns, jnp.dot(anc, weights, preferred_element_type=F32)
+
+
+def partial_kernel(me_ref, direct_ref, couple_ref, bag_ref, out_ref):
+    me = me_ref[0]
+    for columns, value in coupled(me, lax.rem(me, 2), couple_ref, bag_ref):
+        out_ref[:, columns] = direct_ref[:, columns] + value
+
+
 def displace_kernel(
     capacity,
     me_ref,
-    direct_ref,
+    partial_ref,
     couple_ref,
-    mine_ref,
     pair_ref,
     wants_ref,
     lists_ref,
     disp_ref,
     wanted_ref,
     cross_ref,
-    anc_t,
 ):
-    leaves, levels, block, width = couple_ref.shape
     me = me_ref[0]
-    odd = lax.rem(me, 2)
-    chip = lax.rem(lax.div(me, 2), GROUP)
-    near = chip + 1 - 2 * lax.rem(chip, 2)
-    far = lax.rem(chip + 2, GROUP)
-    diag = lax.rem(near + 2, GROUP)
-    half, quarter, eighth = block // 2, block // 4, block // 8
-
-    def put(level, at, rows, value):
-        anc_t[pl.ds(pl.multiple_of(level * block + at * rows, rows), rows), :] = value
-
-    for core, ref in ((odd, mine_ref), (1 - odd, pair_ref)):
-        pieces = (
-            (0, core, half),
-            (1, 2 * lax.rem(chip, 2) + core, quarter),
-            (2, 2 * chip + core, eighth),
-            (1, 2 * lax.rem(near, 2) + core, quarter),
-            (2, 2 * near + core, eighth),
-            (2, 2 * diag + core, eighth),
-            (2, 2 * far + core, eighth),
-        )
-        start = 0
-        for level, at, rows in pieces:
-            put(level, at, rows, ref[start : start + rows, :])
-            start += rows
-
-    anc = anc_t[...].astype(F32).T.astype(BF16)
-    for leaf in range(leaves):
-        value = direct_ref[:, leaf * width : (leaf + 1) * width]
-        for level in range(levels):
-            value = value + jnp.dot(
-                anc[:, level * block : (level + 1) * block],
-                couple_ref[leaf, level],
-                preferred_element_type=F32,
-            )
-        disp_ref[:, leaf * width : (leaf + 1) * width] = value.astype(BF16)
-
+    for columns, value in coupled(me, 1 - lax.rem(me, 2), couple_ref, pair_ref):
+        disp_ref[:, columns] = (partial_ref[:, columns] + value).astype(BF16)
     tall = 2 * capacity // 128
-    height = list_height(capacity, 1)
     tail = list_height(capacity, 2)
-    ours = pair_ref[start : start + tail, :128]
+    ours = pair_ref[pair_ref.shape[0] - tail :, :128]
     wants = wants_ref[...]
     wanted_ref[:, :capacity] = unpacked(wants, 0, capacity)
     wanted_ref[:, capacity : 2 * capacity] = unpacked(wants, tall, capacity)
     wanted_ref[:, 2 * capacity : 3 * capacity] = unpacked(ours, 0, capacity)
-    wanted_ref[:, 3 * capacity :] = unpacked(lists_ref[height : 2 * height, :], 0, capacity)
+    wanted_ref[:, 3 * capacity :] = unpacked(
+        filled(list_rows(lists_ref[...], OWN, capacity), tail), 0, capacity
+    )
     cross_ref[...] = gathered(disp_ref, unpacked(ours, tall, capacity))
 
 
@@ -370,7 +347,6 @@
 
 
 def late_kernel(
-    capacity,
     scale,
     weight_ref,
     compliance_ref,
@@ -384,17 +360,10 @@
     clusters, modes, rows = stress_ref.shape
     points = energy_ref.shape[1]
     weight = jnp.broadcast_to(weight_ref[...], (8, modes)).T[:, :1]
+    arrived = jnp.concatenate([plus_ref[...], minus_ref[...]], axis=1)
+    late = jnp.dot(arrived, moved_ref[...], preferred_element_type=F32)
     for cluster in range(clusters):
-        value = early_ref[cluster]
-        for number, ref in enumerate((plus_ref, minus_ref)):
-            value = value + jnp.dot(
-                ref[...],
-                moved_ref[
-                    number * capacity : (number + 1) * capacity,
-                    cluster * rows : (cluster + 1) * rows,
-                ],
-                preferred_element_type=F32,
-            )
+        value = early_ref[cluster] + late[:, cluster * rows : (cluster + 1) * rows]
         stress_ref[cluster] = value
         square = jnp.sum(value * value * weight, axis=0, keepdims=True)
         square = square * compliance_ref[cluster : cluster + 1, :]
@@ -441,7 +410,6 @@
     leaves, modes, _ = leaf_coords.shape
     width = leaf_modes.shape[2]
     dof_count = leaves * width
-    levels, block = constraint_modes.shape[1:3]
     clusters, slots = cluster_rows.shape
     rows = operators.shape[2]
     points = rows // 6
@@ -452,19 +420,15 @@
     array = jax.ShapeDtypeStruct
     half, quarter, eighth = sep_one.shape[1], sep_two.shape[1], sep_three.shape[1]
 
-    height = list_height(capacity, 1)
     tail = list_height(capacity, 2)
     rides = sub_count == 2 * GROUP
     two_t, three_t = sep_two.T, sep_three.T
 
-    key, local, leaving = call(
+    tall = (5 * capacity // 128 + 7) // 8 * 8
+    key, lists = call(
         lambda *refs: index_kernel(sub_count, dof_count, capacity, *refs),
         (me, cluster_rows),
-        (
-            array((clusters, slots), I32),
-            array((clusters, slots), I32),
-            array((3 * height, 128), F32),
-        ),
+        (array((clusters, slots), I32), array((2 * tall, 128), F32)),
         8,
         1000000000,
         [smem, vmem],
@@ -473,7 +437,7 @@
     spare = () if rides else (array((tail, modes), BF16),) * 2
     near, diag, far, one_t, *loose = call(
         lambda *refs: pack_kernel(capacity, rides, *refs),
-        (me, sep_one, two_t, three_t, leaving),
+        (me, sep_one, two_t, three_t, lists),
         (
             array((quarter + eighth + extra, modes), BF16),
             array((eighth + extra, modes), BF16),
@@ -490,13 +454,6 @@
     far = swap_with(far, "sub", 4)
     if loose:
         loose = [shift_by(loose[0], "sub", 2), shift_by(loose[1], "sub", -2)]
-    lists = call(
-        lambda *refs: lists_kernel(capacity, *refs),
-        (key, local),
-        array((2 * height, 128), F32),
-        8,
-        1000000000,
-    )
     direct = call(
         direct_kernel,
         (leaf_coords, leaf_modes),
@@ -521,9 +478,17 @@
         [smem] + [vmem] * (7 + len(loose)),
     )
     pair = swap_with(bag, "sub", 1)
+    partial = call(
+        partial_kernel,
+        (me, direct, constraint_modes, bag),
+        array((modes, dof_count), F32),
+        8,
+        1000000000,
+        [smem] + [vmem] * 3,
+    )
     disp, wanted, cross = call(
         lambda *refs: displace_kernel(capacity, *refs),
-        (me, direct, constraint_modes, bag, pair, wants, lists),
+        (me, partial, constraint_modes, pair, wants, lists),
         (
             array((modes, dof_count), BF16),
             array((1, 4 * capacity), I32),
@@ -531,8 +496,7 @@
         ),
         12,
         3000000000,
-        [smem] + [vmem] * 6,
-        [VMEM((levels * block, modes), BF16)],
+        [smem] + [vmem] * 5,
     )
     cross = swap_across(cross, "sub")
     flow = array((modes, capacity), BF16)
@@ -568,7 +532,7 @@
         500000000,
     )
     stresses, energy = call(
-        lambda *refs: late_kernel(capacity, 0.5 / (modes * mode_count), *refs),
+        lambda *refs: late_kernel(0.5 / (modes * mode_count), *refs),
         (modal_weight.reshape(1, modes), compliance, early, moved_far, plus, minus),
         (array((clusters, modes, rows), F32), array((clusters, points), F32)),
         8,

time: 42.5 us -> 40.1 us (0.944)
  waiting for transfers between devices: 12.6 us -> 11.3 us
  Pallas kernels: 14.6 us -> 13.6 us
    ppermute x7, waiting for transfers between devices: 6.02 us -> 4.65 us  [swap_with(): lax.ppermute(value, axis, [(i, i ^ mask) for i in range(lax.axis_size(axi...]
    pallas_call x13, Pallas kernels: 13.7 us -> 12.6 us  [call(): pl.pallas_call(kernel, out_shape=outputs, in_specs=specs or [vmem] * len(...]
  transfers between devices with their start and end apart: 10 -> 10, of which waited for: 4 -> 4; matrix products, arithmetic and copies ran while one was open for 0% -> 0% of each run, Pallas kernels for 15% -> 17%
where the time goes in v4:
time: 40.1 us; the launch traced here: 39.9 us
  Pallas kernels  13.6 us (34%)
  starting transfers between devices  13.3 us (33%)
  waiting for transfers between devices  11.3 us (28%)
  between operations  0.89 us (2%)
  local copies, waits for them, and re-layouts  0.85 us (2%)
    pallas_call x13, Pallas kernels, call(): pl.pallas_call(kernel, out_shape=outputs, in_specs=specs or [vmem] * len(...  12.6 us
    ppermute x7, starting transfers between devices, swap_with(): lax.ppermute(value, axis, [(i, i ^ mask) for i in range(lax.axis_size(axi...  8.83 us
    ppermute x1, waiting for transfers between devices, swap_across(): lax.ppermute(value, axis, [(i, (i + 2 * (i % 2) - 1) % peers) for i in ra...  6.61 us
    ppermute x7, waiting for transfers between devices, swap_with(): lax.ppermute(value, axis, [(i, i ^ mask) for i in range(lax.axis_size(axi...  4.65 us
    ppermute x1, starting transfers between devices, swap_across(): lax.ppermute(value, axis, [(i, (i + 2 * (i % 2) - 1) % peers) for i in ra...  2.44 us
    ppermute x2, starting transfers between devices, shift_by(): lax.ppermute(value, axis, [(i, (i + by) % peers) for i in range(peers)])  2.08 us
    pallas_call x1, Pallas kernels, shards(): pl.pallas_call(store_kernel, out_shape=array((clusters, modes, rows), F32...  0.92 us
    unnamed x22, local copies, waits for them, and re-layouts  0.85 us
  transfers between devices with their start and end apart: 10, of which 4 were waited for; matrix products, arithmetic and copies ran while one was open for 0% of the time, Pallas kernels for 17%

profile of v4, /device:TPU:0, one launch (start us, length us, event | category | flops | bytes accessed | tf_op | source)
XLA Modules:
  0.0 39.9 jit_solution(7434147227400561123)
XLA Ops:
  0.7 0.8 %copy-done.8 = s32[3,512]{1,0:T(4,128)S(1)} copy-done((s32[3,512]{1,0:T(4,128)S(1)}, s32[3,512]{1,0:T(4,128)}, u32[]{:S(2)}) %copy-start.8) | copy-done | bytes 6168
  1.5 0.6 %shard_map.113 = (s32[3,512]{1,0:T(4,128)S(1)}, f32[32,128]{1,0:T(8,128)S(1)}) custom-call(s32[1]{0:T(128)} %bitcast.1.refs_0_.me_ref, s32[3,512]{1,0:T(4,128)S(1)} %copy-done.8), custom_call_target="tpu_custom_call" | custom-call | flops 1000000000 | bytes 6148 | tf_op jit(solution)/shard_map/pallas_call | solution.py:39
  2.2 3.0 %collective-permute-start = (bf16[112,192]{1,0:T(8,128)(2,1)S(1)}, bf16[112,192]{1,0:T(8,128)(2,1)S(1)}, u32[]{:S(2)}, u32[]{:S(2)}) collective-permute-start(bf16[112,192]{1,0:T(8,128)(2,1)S(1)} %get-tuple-element.22), channel_id=1, source_target_pairs={{0,8},{4,12},{8,0},{12,4},{16,24},{20,28},{24,16},{28,20},{1,9},{5... | collective-permute-start | bytes 129032 | tf_op jit(solution)/shard_map/ppermute | solution.py:25
  5.3 1.5 %collective-permute-start.1 = (bf16[48,192]{1,0:T(8,128)(2,1)S(1)}, bf16[48,192]{1,0:T(8,128)(2,1)S(1)}, u32[]{:S(2)}, u32[]{:S(2)}) collective-permute-start(bf16[48,192]{1,0:T(8,128)(2,1)S(1)} %get-tuple-element.23), channel_id=1, source_target_pairs={{0,24},{4,28},{8,16},{12,20},{16,8},{20,12},{24,0},{28,4},{1,25},{... | collective-permute-start | bytes 55304 | tf_op jit(solution)/shard_map/ppermute | solution.py:25
  6.8 2.0 %shard_map.114.refs_0_ = bf16[1152,1152]{1,0:T(8,128)(2,1)S(1)} custom-call(s32[3,512]{1,0:T(4,128)S(1)} %get-tuple-element.19.refs_0_, bf16[3,512,384]{2,1,0:T(8,128)(2,1)S(1)} %copy-done.5), custom_call_target="tpu_custom_call" | custom-call | flops 3000000000 | bytes 1185792 | tf_op jit(solution)/shard_map/pallas_call | solution.py:39
  8.8 1.7 %collective-permute-done.2.refs_6_ = bf16[32,192]{1,0:T(8,128)(2,1)S(1)} collective-permute-done((bf16[32,192]{1,0:T(8,128)(2,1)S(1)}, bf16[32,192]{1,0:T(8,128)(2,1)S(1)}, u32[]{:S(2)}, u32[]{:S(2)}) %collective-permute-start.2) | collective-permute-done | bytes 12320 | tf_op jit(solution)/shard_map/ppermute | solution.py:25
  10.6 0.6 %shard_map.115.direct_ref = f32[192,4096]{1,0:T(8,128)S(1)} custom-call(bf16[8,192,128]{2,1,0:T(8,128)(2,1)S(1)} %copy-done.7, bf16[8,128,512]{2,1,0:T(8,128)(2,1)S(1)} %copy-done.6), custom_call_target="tpu_custom_call" | custom-call | flops 1500000000 | bytes 1441792 | tf_op jit(solution)/shard_map/pallas_call | solution.py:39
  11.2 1.0 %shard_map.118.refs_1_ = f32[192,4096]{1,0:T(8,128)S(1)} custom-call(s32[1]{0:T(128)} %bitcast.1.refs_0_.me_ref, f32[192,4096]{1,0:T(8,128)S(1)} %shard_map.115.direct_ref, bf16[8,3,256,512]{3,2,1,0:T(8,128)(2,1)S(1)} %bitcast.7, bf16[400,192]{1,0:T(8,128)(2,1)S(1)} %get-tuple-element.25.bag_ref), custom_call_target="tpu_custom_call" | custom-call | flops 1000000000 | bytes 9590788 | tf_op jit(solution)/shard_map/pallas_call | solution.py:39
  12.2 1.9 %shard_map.119 = (bf16[192,4096]{1,0:T(8,128)(2,1)S(1)}, s32[1,1536]{1,0:T(1,128)S(1)}, bf16[192,384]{1,0:T(8,128)(2,1)S(1)}) custom-call(s32[1]{0:T(128)} %bitcast.1.refs_0_.me_ref, f32[192,4096]{1,0:T(8,128)S(1)} %shard_map.118.refs_1_, bf16[8,3,256,512]{3,2,1,0:T(8,128)(2,1)S(1)} %bitcast.7, bf16[400,192]{1,0:T(8,128)(2,1)S(1)} %collective-permute-done.3.refs_3_, ...), custom_call_target="tpu_custom_call" | custom-call | flops 3000000000 | bytes 9615364 | tf_op jit(solution)/shard_map/pallas_call | solution.py:39
  14.1 1.4 %shard_map.123 = (bf16[192,384]{1,0:T(8,128)(2,1)S(1)}, bf16[192,384]{1,0:T(8,128)(2,1)S(1)}) custom-call(bf16[192,4096]{1,0:T(8,128)(2,1)S(1)} %get-tuple-element.27.refs_0_, s32[1,1536]{1,0:T(1,128)S(1)} %get-tuple-element.28.refs_1_), custom_call_target="tpu_custom_call" | custom-call | flops 2000000000 | bytes 1579008 | tf_op jit(solution)/shard_map/pallas_call | solution.py:39
  15.5 1.4 %shard_map.120 = (bf16[192,384]{1,0:T(8,128)(2,1)S(1)}, bf16[192,384]{1,0:T(8,128)(2,1)S(1)}) custom-call(bf16[192,4096]{1,0:T(8,128)(2,1)S(1)} %get-tuple-element.27.refs_0_, s32[1,1536]{1,0:T(1,128)S(1)} %get-tuple-element.28.refs_1_), custom_call_target="tpu_custom_call" | custom-call | flops 2000000000 | bytes 1579008 | tf_op jit(solution)/shard_map/pallas_call | solution.py:39
  16.9 1.5 %collective-permute-start.6 = (bf16[192,384]{1,0:T(8,128)(2,1)S(1)}, bf16[192,384]{1,0:T(8,128)(2,1)S(1)}, u32[]{:S(2)}, u32[]{:S(2)}) collective-permute-start(bf16[192,384]{1,0:T(8,128)(2,1)S(1)} %get-tuple-element.32), channel_id=1, source_target_pairs={{0,24},{4,28},{8,0},{12,4},{16,8},{20,12},{24,16},{28,20},{1,25},{... | collective-permute-start | bytes 442376 | tf_op jit(solution)/shard_map/ppermute | solution.py:21
  18.4 0.6 %collective-permute-start.7 = (bf16[192,384]{1,0:T(8,128)(2,1)S(1)}, bf16[192,384]{1,0:T(8,128)(2,1)S(1)}, u32[]{:S(2)}, u32[]{:S(2)}) collective-permute-start(bf16[192,384]{1,0:T(8,128)(2,1)S(1)} %get-tuple-element.33), channel_id=1, source_target_pairs={{0,8},{4,12},{8,16},{12,20},{16,24},{20,28},{24,0},{28,4},{1,9},{5... | collective-permute-start | bytes 442376 | tf_op jit(solution)/shard_map/ppermute | solution.py:21
  19.0 2.4 %collective-permute-start.5 = (bf16[192,384]{1,0:T(8,128)(2,1)S(1)}, bf16[192,384]{1,0:T(8,128)(2,1)S(1)}, u32[]{:S(2)}, u32[]{:S(2)}) collective-permute-start(bf16[192,384]{1,0:T(8,128)(2,1)S(1)} %get-tuple-element.31), channel_id=1, source_target_pairs={{0,28},{4,8},{8,4},{12,16},{16,12},{20,24},{24,20},{28,0},{1,29},{... | collective-permute-start | bytes 442376 | tf_op jit(solution)/shard_map/ppermute | solution.py:30
  21.5 1.4 %shard_map.122.refs_3_ = bf16[768,1152]{1,0:T(8,128)(2,1)S(1)} custom-call(s32[3,512]{1,0:T(4,128)S(1)} %get-tuple-element.19.refs_0_, bf16[3,512,384]{2,1,0:T(8,128)(2,1)S(1)} %copy-done.5), custom_call_target="tpu_custom_call" | custom-call | flops 2000000000 | bytes 1185792 | tf_op jit(solution)/shard_map/pallas_call | solution.py:39
  22.9 6.6 %collective-permute-done.5.refs_3_ = bf16[192,384]{1,0:T(8,128)(2,1)S(1)} collective-permute-done((bf16[192,384]{1,0:T(8,128)(2,1)S(1)}, bf16[192,384]{1,0:T(8,128)(2,1)S(1)}, u32[]{:S(2)}, u32[]{:S(2)}) %collective-permute-start.5) | collective-permute-done | bytes 147488 | tf_op jit(solution)/shard_map/ppermute | solution.py:30
  29.5 1.0 %shard_map.121.refs_2_ = f32[3,192,384]{2,1,0:T(8,128)S(1)} custom-call(bf16[1152,1152]{1,0:T(8,128)(2,1)S(1)} %shard_map.114.refs_0_, bf16[192,384]{1,0:T(8,128)(2,1)S(1)} %collective-permute-done.4.refs_1_, bf16[192,384]{1,0:T(8,128)(2,1)S(1)} %get-tuple-element.30.refs_2_, bf16[192,384]{1,0:T(8,128)(2,1)S(1)} %collective-permute-done.5.refs_3_), custom_call_target="tpu_custom_call" | custom-call | flops 500000000 | bytes 3096576 | tf_op jit(solution)/shard_map/pallas_call | solution.py:39
  30.5 0.6 %shard_map.124 = (f32[3,192,384]{2,1,0:T(8,128)S(1)}, f32[3,64]{1,0:T(4,128)S(1)}) custom-call(f32[1,192]{1,0:T(1,128)S(1)} %bitcast.12, f32[3,384]{1,0:T(4,128)S(1)} %copy-done.3, f32[3,192,384]{2,1,0:T(8,128)S(1)} %shard_map.121.refs_2_, bf16[768,1152]{1,0:T(8,128)(2,1)S(1)} %shard_map.122.refs_3_, bf16[192,384]{1,0:T(8,128)(2,1)S(1)} %collective-permute-done.6.refs_4_, ...), custom_call_target="tpu_custom_call" | custom-call | flops 500000000 | bytes 2954496 | tf_op jit(solution)/shard_map/pallas_call | solution.py:39
  31.2 1.6 %collective-permute-start.8 = (f32[3,64]{1,0:T(4,128)S(1)}, f32[3,64]{1,0:T(4,128)S(1)}, u32[]{:S(2)}, u32[]{:S(2)}) collective-permute-start(f32[3,64]{1,0:T(4,128)S(1)} %get-tuple-element.35), channel_id=1, source_target_pairs={{0,1},{1,0},{2,3},{3,2},{4,5},{5,4},{6,7},{7,6},{8,9},{9,8},{10,11... | collective-permute-start | bytes 2312 | tf_op jit(solution)/shard_map/ppermute | solution.py:25
  32.8 2.0 %collective-permute-done.8 = f32[3,64]{1,0:T(4,128)S(1)} collective-permute-done((f32[3,64]{1,0:T(4,128)S(1)}, f32[3,64]{1,0:T(4,128)S(1)}, u32[]{:S(2)}, u32[]{:S(2)}) %collective-permute-start.8) | collective-permute-done | bytes 800 | tf_op jit(solution)/shard_map/ppermute | solution.py:25
  34.8 2.6 %collective-permute-start.9 = (f32[3,64]{1,0:T(4,128)S(1)}, f32[3,64]{1,0:T(4,128)S(1)}, u32[]{:S(2)}, u32[]{:S(2)}) collective-permute-start(f32[3,64]{1,0:T(4,128)S(1)} %add.3.mine_ref), channel_id=1, source_target_pairs={{0,2},{1,3},{2,0},{3,1},{4,6},{5,7},{6,4},{7,5},{8,10},{9,11},{10,... | collective-permute-start | bytes 2312 | tf_op jit(solution)/shard_map/ppermute | solution.py:25
  37.4 0.9 %store.1 = f32[3,192,384]{2,1,0:T(8,128)} custom-call(f32[3,192,384]{2,1,0:T(8,128)S(1)} %get-tuple-element.34.source_ref), custom_call_target="tpu_custom_call" | custom-call | flops 500000000 | bytes 2000000 | tf_op jit(solution)/shard_map/store/pallas_call | solution.py:546
  38.3 1.0 %collective-permute-done.9.other_ref = f32[3,64]{1,0:T(4,128)S(1)} collective-permute-done((f32[3,64]{1,0:T(4,128)S(1)}, f32[3,64]{1,0:T(4,128)S(1)}, u32[]{:S(2)}, u32[]{:S(2)}) %collective-permute-start.9) | collective-permute-done | bytes 800 | tf_op jit(solution)/shard_map/ppermute | solution.py:25
  39.3 0.7 %shard_map.125 = f32[1,48]{1,0:T(1,128)} custom-call(s32[1]{0:T(128)} %bitcast.4.at_ref, f32[3,64]{1,0:T(4,128)S(1)} %add.3.mine_ref, f32[3,64]{1,0:T(4,128)S(1)} %collective-permute-done.9.other_ref), custom_call_target="tpu_custom_call" | custom-call | flops 1000 | bytes 1540 | tf_op jit(solution)/shard_map/pallas_call | solution.py:39
  (34 shorter events, 0.3 us)
Async XLA Ops:
  0.6 1.4 %copy-start = (bf16[192,64]{0,1:T(8,128)(2,1)S(1)}, bf16[192,64]{0,1:T(8,128)(2,1)}, u32[]{:S(2)}) copy-start(bf16[192,64]{0,1:T(8,128)(2,1)} %param.14) | copy-start | bytes 73732
  0.6 1.4 %copy-start.1 = (bf16[192,32]{0,1:T(8,128)(2,1)S(1)}, bf16[192,32]{0,1:T(8,128)(2,1)}, u32[]{:S(2)}) copy-start(bf16[192,32]{0,1:T(8,128)(2,1)} %param.15) | copy-start | bytes 36868
  0.7 1.5 %copy-start.2 = (bf16[192,128]{1,0:T(8,128)(2,1)S(1)}, bf16[192,128]{1,0:T(8,128)(2,1)}, u32[]{:S(2)}) copy-start(bf16[192,128]{1,0:T(8,128)(2,1)} %refs_1_.7) | copy-start | bytes 147460
  0.7 6.1 %copy-start.5 = (bf16[3,512,384]{2,1,0:T(8,128)(2,1)S(1)}, bf16[3,512,384]{2,1,0:T(8,128)(2,1)}, u32[]{:S(2)}) copy-start(bf16[3,512,384]{2,1,0:T(8,128)(2,1)} %refs_1_.8) | copy-start | bytes 3538948
  0.7 0.8 %copy-start.8 = (s32[3,512]{1,0:T(4,128)S(1)}, s32[3,512]{1,0:T(4,128)}, u32[]{:S(2)}) copy-start(s32[3,512]{1,0:T(4,128)} %refs_1_.5) | copy-start | bytes 18436
  1.5 9.7 %slice-start = ((s8[6291456]{0:T(1024)(128)(4,1)}), s8[4194304]{0:T(1024)(128)(4,1)S(1)}, s32[]{:S(2)}) async-start(s8[6291456]{0:T(1024)(128)(4,1)} %bitcast.6), calls=%async_computation | async-start | bytes 8388608
  2.2 8.3 %collective-permute-start = (bf16[112,192]{1,0:T(8,128)(2,1)S(1)}, bf16[112,192]{1,0:T(8,128)(2,1)S(1)}, u32[]{:S(2)}, u32[]{:S(2)}) collective-permute-start(bf16[112,192]{1,0:T(8,128)(2,1)S(1)} %get-tuple-element.22), channel_id=1, source_target_pairs={{0,8},{4,12},{8,0},{12,4},{16,24},{20,28},{24,16},{28,20},{1,9},{5... | collective-permute-start | bytes 129032 | tf_op jit(solution)/shard_map/ppermute | solution.py:25
  5.3 5.2 %collective-permute-start.1 = (bf16[48,192]{1,0:T(8,128)(2,1)S(1)}, bf16[48,192]{1,0:T(8,128)(2,1)S(1)}, u32[]{:S(2)}, u32[]{:S(2)}) collective-permute-start(bf16[48,192]{1,0:T(8,128)(2,1)S(1)} %get-tuple-element.23), channel_id=1, source_target_pairs={{0,24},{4,28},{8,16},{12,20},{16,8},{20,12},{24,0},{28,4},{1,25},{... | collective-permute-start | bytes 55304 | tf_op jit(solution)/shard_map/ppermute | solution.py:25
  6.7 3.7 %collective-permute-start.2 = (bf16[32,192]{1,0:T(8,128)(2,1)S(1)}, bf16[32,192]{1,0:T(8,128)(2,1)S(1)}, u32[]{:S(2)}, u32[]{:S(2)}) collective-permute-start(bf16[32,192]{1,0:T(8,128)(2,1)S(1)} %get-tuple-element.24), channel_id=1, source_target_pairs={{0,16},{4,20},{8,24},{12,28},{16,0},{20,4},{24,8},{28,12},{1,17},{... | collective-permute-start | bytes 36872 | tf_op jit(solution)/shard_map/ppermute | solution.py:25
  6.8 3.8 %copy-start.6 = (bf16[8,128,512]{2,1,0:T(8,128)(2,1)S(1)}, bf16[8,128,512]{2,1,0:T(8,128)(2,1)}, u32[]{:S(2)}) copy-start(bf16[8,128,512]{2,1,0:T(8,128)(2,1)} %modes_ref.1) | copy-start | bytes 3145732
  6.8 3.8 %copy-start.7 = (bf16[8,192,128]{2,1,0:T(8,128)(2,1)S(1)}, bf16[8,192,128]{2,1,0:T(8,128)(2,1)}, u32[]{:S(2)}) copy-start(bf16[8,192,128]{2,1,0:T(8,128)(2,1)} %coords_ref.1) | copy-start | bytes 1179652
  6.8 4.4 %slice-start.1 = ((s8[6291456]{0:T(1024)(128)(4,1)}), s8[2097152]{0:T(1024)(128)(4,1)S(1)}, s32[]{:S(2)}) async-start(s8[6291456]{0:T(1024)(128)(4,1)} %bitcast.6), calls=%async_computation.1 | async-start | bytes 4194304
  10.5 1.7 %collective-permute-start.3 = (bf16[400,192]{1,0:T(8,128)(2,1)S(1)}, bf16[400,192]{1,0:T(8,128)(2,1)S(1)}, u32[]{:S(2)}, u32[]{:S(2)}) collective-permute-start(bf16[400,192]{1,0:T(8,128)(2,1)S(1)} %get-tuple-element.25.bag_ref), channel_id=1, source_target_pairs={{0,4},{4,0},{8,12},{12,8},{16,20},{20,16},{24,28},{28,24},{1,5},{5... | collective-permute-start | bytes 460808 | tf_op jit(solution)/shard_map/ppermute | solution.py:25
  16.9 13.6 %collective-permute-start.6 = (bf16[192,384]{1,0:T(8,128)(2,1)S(1)}, bf16[192,384]{1,0:T(8,128)(2,1)S(1)}, u32[]{:S(2)}, u32[]{:S(2)}) collective-permute-start(bf16[192,384]{1,0:T(8,128)(2,1)S(1)} %get-tuple-element.32), channel_id=1, source_target_pairs={{0,24},{4,28},{8,0},{12,4},{16,8},{20,12},{24,16},{28,20},{1,25},{... | collective-permute-start | bytes 442376 | tf_op jit(solution)/shard_map/ppermute | solution.py:21
  18.4 12.1 %collective-permute-start.7 = (bf16[192,384]{1,0:T(8,128)(2,1)S(1)}, bf16[192,384]{1,0:T(8,128)(2,1)S(1)}, u32[]{:S(2)}, u32[]{:S(2)}) collective-permute-start(bf16[192,384]{1,0:T(8,128)(2,1)S(1)} %get-tuple-element.33), channel_id=1, source_target_pairs={{0,8},{4,12},{8,16},{12,20},{16,24},{20,28},{24,0},{28,4},{1,9},{5... | collective-permute-start | bytes 442376 | tf_op jit(solution)/shard_map/ppermute | solution.py:21
  19.0 3.9 %collective-permute-start.4 = (bf16[192,384]{1,0:T(8,128)(2,1)S(1)}, bf16[192,384]{1,0:T(8,128)(2,1)S(1)}, u32[]{:S(2)}, u32[]{:S(2)}) collective-permute-start(bf16[192,384]{1,0:T(8,128)(2,1)S(1)} %get-tuple-element.29), channel_id=1, source_target_pairs={{0,4},{4,0},{8,12},{12,8},{16,20},{20,16},{24,28},{28,24},{1,5},{5... | collective-permute-start | bytes 442376 | tf_op jit(solution)/shard_map/ppermute | solution.py:25
  19.0 10.5 %collective-permute-start.5 = (bf16[192,384]{1,0:T(8,128)(2,1)S(1)}, bf16[192,384]{1,0:T(8,128)(2,1)S(1)}, u32[]{:S(2)}, u32[]{:S(2)}) collective-permute-start(bf16[192,384]{1,0:T(8,128)(2,1)S(1)} %get-tuple-element.31), channel_id=1, source_target_pairs={{0,28},{4,8},{8,4},{12,16},{16,12},{20,24},{24,20},{28,0},{1,29},{... | collective-permute-start | bytes 442376 | tf_op jit(solution)/shard_map/ppermute | solution.py:30
  22.8 7.7 %copy-start.3 = (f32[3,384]{1,0:T(4,128)S(1)}, f32[3,384]{1,0:T(4,128)}, u32[]{:S(2)}) copy-start(f32[3,384]{1,0:T(4,128)} %refs_1_.9) | copy-start | bytes 13828
  22.9 7.7 %copy-start.4 = (f32[192]{0:T(256)S(1)}, f32[192]{0:T(256)}, u32[]{:S(2)}) copy-start(f32[192]{0:T(256)} %param.19) | copy-start | bytes 2308
  31.2 3.6 %collective-permute-start.8 = (f32[3,64]{1,0:T(4,128)S(1)}, f32[3,64]{1,0:T(4,128)S(1)}, u32[]{:S(2)}, u32[]{:S(2)}) collective-permute-start(f32[3,64]{1,0:T(4,128)S(1)} %get-tuple-element.35), channel_id=1, source_target_pairs={{0,1},{1,0},{2,3},{3,2},{4,5},{5,4},{6,7},{7,6},{8,9},{9,8},{10,11... | collective-permute-start | bytes 2312 | tf_op jit(solution)/shard_map/ppermute | solution.py:25
  34.8 4.5 %collective-permute-start.9 = (f32[3,64]{1,0:T(4,128)S(1)}, f32[3,64]{1,0:T(4,128)S(1)}, u32[]{:S(2)}, u32[]{:S(2)}) collective-permute-start(f32[3,64]{1,0:T(4,128)S(1)} %add.3.mine_ref), channel_id=1, source_target_pairs={{0,2},{1,3},{2,0},{3,1},{4,6},{5,7},{6,4},{7,5},{8,10},{9,11},{10,... | collective-permute-start | bytes 2312 | tf_op jit(solution)/shard_map/ppermute | solution.py:25

commit v5 on v4

--- a/solution.py
+++ b/solution.py
@@ -64,6 +64,8 @@
 def filled(rows, count):
     lanes = rows[0].shape[1]
     rest = count - sum(row.shape[0] for row in rows)
+    if not rest:
+        return jnp.concatenate(rows, axis=0)
     return jnp.concatenate(rows + [jnp.zeros((rest, lanes), F32)], axis=0)
 
 
@@ -136,173 +138,159 @@
     )
 
 
-def pack_kernel(
+def pack_kernel(capacity, one_ref, two_ref, three_ref, lists_ref, bag_ref):
+    tail = list_height(capacity, 2)
+    lists = lists_ref[...]
+    at = 0
+    for value in (one_ref[...].astype(F32).T.astype(BF16), two_ref[...], three_ref[...]):
+        bag_ref[at : at + value.shape[0], :] = value
+        at += value.shape[0]
+    put_lists(
+        bag_ref, at, list_rows(lists, PAIR, capacity) + list_rows(lists, CROSS, capacity), tail
+    )
+
+
+def put_lists(ref, at, rows, tail):
+    ref[at : at + tail, :] = jnp.zeros((tail, ref.shape[1]), BF16)
+    ref[at : at + tail, :128] = filled(rows, tail).astype(BF16)
+
+
+def relay_kernel(
+    capacity, rides, half, me_ref, bag_ref, pair_ref, lists_ref, near_ref, diag_ref, far_ref, *rest
+):
+    tail = list_height(capacity, 2)
+    tall = 2 * capacity // 128
+    quarter, eighth = half // 2, half // 4
+    odd = lax.rem(me_ref[0], 2)
+    lists = lists_ref[...]
+    relayed = pair_ref[half + quarter + eighth :, :128].astype(F32)[tall : 2 * tall, :]
+    up = list_rows(lists, PLUS, capacity) + [relayed]
+    down = list_rows(lists, MINUS, capacity) + [relayed]
+
+    def put(ref, at, rows, core, value):
+        ref[pl.ds(pl.multiple_of(at + core * rows, rows), rows), :] = value
+
+    for core, ref in ((odd, bag_ref), (1 - odd, pair_ref)):
+        two = ref[half : half + quarter, :]
+        three = ref[half + quarter : half + quarter + eighth, :]
+        put(near_ref, 0, quarter, core, two)
+        put(near_ref, 2 * quarter, eighth, core, three)
+        put(diag_ref, 0, eighth, core, three)
+        put(far_ref, 0, eighth, core, three)
+    if rides:
+        low = lax.rem(lax.div(me_ref[0], 2), 2) == 0
+        up, down = filled(up, tail), filled(down, tail)
+        put_lists(near_ref, 2 * (quarter + eighth), [jnp.where(low, up, down)], tail)
+        put_lists(diag_ref, 2 * eighth, [jnp.where(low, down, up)], tail)
+    else:
+        put_lists(rest[0], 0, up, tail)
+        put_lists(rest[1], 0, down, tail)
+
+
+def direct_kernel(coords_ref, modes_ref, out_ref):
+    leaves = coords_ref.shape[0]
+    width = modes_ref.shape[2]
+    for leaf in range(leaves):
+        out_ref[:, leaf * width : (leaf + 1) * width] = jnp.dot(
+            coords_ref[leaf], modes_ref[leaf], preferred_element_type=F32
+        )
+
+
+def gathered(disp_ref, wanted):
+    depth = 256
+    total = None
+    for at in range(0, disp_ref.shape[1], depth):
+        part = jnp.dot(
+            disp_ref[:, at : at + depth], one_hot(wanted, at, depth), preferred_element_type=F32
+        )
+        total = part if total is None else total + part
+    return total.astype(BF16)
+
+
+def coupled(pieces, couple_ref):
+    leaves, _, _, width = couple_ref.shape
+    anc = jnp.concatenate([value for level, at, value in pieces], axis=0)
+    anc = anc.astype(F32).T.astype(BF16)
+    for leaf in range(leaves):
+        weights = []
+        for level, at, value in pieces:
+            rows = value.shape[0]
+            start = pl.multiple_of(at * rows, rows)
+            weights.append(couple_ref[leaf, level, pl.ds(start, rows), :])
+        columns = slice(leaf * width, (leaf + 1) * width)
+        yield columns, jnp.dot(
+            anc, jnp.concatenate(weights, axis=0), preferred_element_type=F32
+        )
+
+
+def places(me):
+    chip = lax.rem(lax.div(me, 2), GROUP)
+    near = chip + 1 - 2 * lax.rem(chip, 2)
+    return chip, near, lax.rem(near + 2, GROUP), lax.rem(chip + 2, GROUP)
+
+
+def partial_kernel(me_ref, direct_ref, couple_ref, bag_ref, pair_ref, out_ref):
+    me = me_ref[0]
+    odd = lax.rem(me, 2)
+    chip, _, _, _ = places(me)
+    block = couple_ref.shape[2]
+    half, quarter, eighth = block // 2, block // 4, block // 8
+    pieces = []
+    for core, ref in ((odd, bag_ref), (1 - odd, pair_ref)):
+        pieces += [
+            (0, core, ref[:half, :]),
+            (1, 2 * lax.rem(chip, 2) + core, ref[half : half + quarter, :]),
+            (2, 2 * chip + core, ref[half + quarter : half + quarter + eighth, :]),
+        ]
+    for columns, value in coupled(pieces, couple_ref):
+        out_ref[:, columns] = direct_ref[:, columns] + value
+
+
+def displace_kernel(
     capacity,
     rides,
     me_ref,
-    one_ref,
-    two_ref,
-    three_ref,
-    lists_ref,
-    near_ref,
-    diag_ref,
-    far_ref,
-    one_t_ref,
-    *rest,
-):
-    quarter, eighth = two_ref.shape[0], three_ref.shape[0]
-    tail = list_height(capacity, 2)
-    lists = lists_ref[...]
-    relay = list_rows(lists, CROSS, capacity)
-    up = filled(list_rows(lists, PLUS, capacity) + relay, tail)
-    down = filled(list_rows(lists, MINUS, capacity) + relay, tail)
-    near_ref[:quarter, :] = two_ref[...]
-    near_ref[quarter : quarter + eighth, :] = three_ref[...]
-    diag_ref[:eighth, :] = three_ref[...]
-    far_ref[...] = three_ref[...]
-    lanes = near_ref.shape[1]
-    if rides:
-        low = lax.rem(lax.div(me_ref[0], 2), 2) == 0
-        slots = (
-            (near_ref, quarter + eighth, jnp.where(low, up, down)),
-            (diag_ref, eighth, jnp.where(low, down, up)),
-        )
-    else:
-        slots = ((rest[0], 0, up), (rest[1], 0, down))
-    for ref, at, value in slots:
-        ref[at : at + tail, :] = jnp.zeros((tail, lanes), BF16)
-        ref[at : at + tail, :128] = value.astype(BF16)
-    one_t_ref[...] = one_ref[...].astype(F32).T.astype(BF16)
-
-
-def relay_kernel(
-    capacity,
-    rides,
-    me_ref,
-    one_ref,
-    two_ref,
-    three_ref,
+    partial_ref,
+    couple_ref,
+    pair_ref,
     near_ref,
     diag_ref,
     far_ref,
     lists_ref,
     *rest,
 ):
-    wants_ref, bag_ref = rest[-1], rest[-2]
-    quarter, eighth = two_ref.shape[0], three_ref.shape[0]
-    tall = 2 * capacity // 128
-    tail = list_height(capacity, 2)
-    at = 0
-    for value in (
-        one_ref[...],
-        two_ref[...],
-        three_ref[...],
-        near_ref[: quarter + eighth, :],
-        diag_ref[:eighth, :],
-        far_ref[...],
-    ):
-        bag_ref[at : at + value.shape[0], :] = value
-        at += value.shape[0]
-    if rides:
-        beside = near_ref[quarter + eighth :, :128].astype(F32)
-        opposite = diag_ref[eighth:, :128].astype(F32)
-        low = lax.rem(lax.div(me_ref[0], 2), 2) == 0
-        from_behind = jnp.where(low, opposite, beside)
-        from_ahead = jnp.where(low, beside, opposite)
-    else:
-        from_behind = rest[0][:, :128].astype(F32)
-        from_ahead = rest[1][:, :128].astype(F32)
-    odd = lax.rem(me_ref[0], 2) == 1
-    relayed = jnp.where(odd, from_behind, from_ahead)[tall : 2 * tall, :]
-    bag_ref[at : at + tail, :] = jnp.zeros((tail, bag_ref.shape[1]), BF16)
-    bag_ref[at : at + tail, :128] = filled(
-        list_rows(lists_ref[...], PAIR, capacity) + [relayed], tail
-    ).astype(BF16)
-    wants_ref[...] = filled([from_behind[:tall, :], from_ahead[:tall, :]], tail)
-
-
-def direct_kernel(coords_ref, modes_ref, out_ref):
-    leaves = coords_ref.shape[0]
-    width = modes_ref.shape[2]
-    for leaf in range(leaves):
-        out_ref[:, leaf * width : (leaf + 1) * width] = jnp.dot(
-            coords_ref[leaf], modes_ref[leaf], preferred_element_type=F32
-        )
-
-
-def gathered(disp_ref, wanted):
-    depth = 256
-    total = None
-    for at in range(0, disp_ref.shape[1], depth):
-        part = jnp.dot(
-            disp_ref[:, at : at + depth], one_hot(wanted, at, depth), preferred_element_type=F32
-        )
-        total = part if total is None else total + part
-    return total.astype(BF16)
-
-
-def coupled(me, core, couple_ref, bag_ref):
-    leaves, _, block, width = couple_ref.shape
-    chip = lax.rem(lax.div(me, 2), GROUP)
-    near = chip + 1 - 2 * lax.rem(chip, 2)
-    far = lax.rem(chip + 2, GROUP)
-    diag = lax.rem(near + 2, GROUP)
-    half, quarter, eighth = block // 2, block // 4, block // 8
+    disp_ref, wanted_ref, cross_ref = rest[-3:]
+    me = me_ref[0]
+    chip, near, diag, far = places(me)
+    block = couple_ref.shape[2]
+    quarter, eighth = block // 4, block // 8
     pieces = (
-        (0, core, half),
-        (1, 2 * lax.rem(chip, 2) + core, quarter),
-        (2, 2 * chip + core, eighth),
-        (1, 2 * lax.rem(near, 2) + core, quarter),
-        (2, 2 * near + core, eighth),
-        (2, 2 * diag + core, eighth),
-        (2, 2 * far + core, eighth),
-    )
-    held = sum(rows for level, at, rows in pieces)
-    anc = bag_ref[:held, :].astype(F32).T.astype(BF16)
-    for leaf in range(leaves):
-        weights = jnp.concatenate(
-            [
-                couple_ref[leaf, level, pl.ds(pl.multiple_of(at * rows, rows), rows), :]
-                for level, at, rows in pieces
-            ],
-            axis=0,
-        )
-        columns = slice(leaf * width, (leaf + 1) * width)
-        yield columns, jnp.dot(anc, weights, preferred_element_type=F32)
-
-
-def partial_kernel(me_ref, direct_ref, couple_ref, bag_ref, out_ref):
-    me = me_ref[0]
-    for columns, value in coupled(me, lax.rem(me, 2), couple_ref, bag_ref):
-        out_ref[:, columns] = direct_ref[:, columns] + value
-
-
-def displace_kernel(
-    capacity,
-    me_ref,
-    partial_ref,
-    couple_ref,
-    pair_ref,
-    wants_ref,
-    lists_ref,
-    disp_ref,
-    wanted_ref,
-    cross_ref,
-):
-    me = me_ref[0]
-    for columns, value in coupled(me, 1 - lax.rem(me, 2), couple_ref, pair_ref):
+        (1, lax.rem(near, 2), near_ref[: 2 * quarter, :]),
+        (2, near, near_ref[2 * quarter : 2 * (quarter + eighth), :]),
+        (2, diag, diag_ref[: 2 * eighth, :]),
+        (2, far, far_ref[...]),
+    )
+    for columns, value in coupled(pieces, couple_ref):
         disp_ref[:, columns] = (partial_ref[:, columns] + value).astype(BF16)
     tall = 2 * capacity // 128
     tail = list_height(capacity, 2)
-    ours = pair_ref[pair_ref.shape[0] - tail :, :128]
-    wants = wants_ref[...]
-    wanted_ref[:, :capacity] = unpacked(wants, 0, capacity)
-    wanted_ref[:, capacity : 2 * capacity] = unpacked(wants, tall, capacity)
+    if rides:
+        beside = near_ref[2 * (quarter + eighth) :, :128].astype(F32)
+        opposite = diag_ref[2 * eighth :, :128].astype(F32)
+        low = lax.rem(chip, 2) == 0
+        behind, ahead = jnp.where(low, opposite, beside), jnp.where(low, beside, opposite)
+    else:
+        behind, ahead = rest[0][:, :128].astype(F32), rest[1][:, :128].astype(F32)
+    odd = lax.rem(me, 2) == 1
+    across = jnp.where(odd, ahead, behind)
+    ours = pair_ref[pair_ref.shape[0] - tail :, :128].astype(F32)
+    wanted_ref[:, :capacity] = unpacked(behind, 0, capacity)
+    wanted_ref[:, capacity : 2 * capacity] = unpacked(ahead, 0, capacity)
     wanted_ref[:, 2 * capacity : 3 * capacity] = unpacked(ours, 0, capacity)
     wanted_ref[:, 3 * capacity :] = unpacked(
         filled(list_rows(lists_ref[...], OWN, capacity), tail), 0, capacity
     )
-    cross_ref[...] = gathered(disp_ref, unpacked(ours, tall, capacity))
+    cross_ref[...] = gathered(disp_ref, unpacked(across, tall, capacity))
 
 
 def gather_kernel(capacity, first, disp_ref, wanted_ref, left_ref, right_ref):
@@ -329,21 +317,21 @@
                 )
 
 
-def early_kernel(capacity, moved_ref, pair_ref, own_ref, cross_ref, out_ref):
-    clusters, _, rows = out_ref.shape
+def early_kernel(first, key_ref, operators_ref, pair_ref, own_ref, cross_ref, out_ref):
+    clusters, _, _ = out_ref.shape
+    arrived = jnp.concatenate([pair_ref[...], own_ref[...], cross_ref[...]], axis=1)
     for cluster in range(clusters):
-        value = None
-        for number, ref in enumerate((pair_ref, own_ref, cross_ref)):
-            part = jnp.dot(
-                ref[...],
-                moved_ref[
-                    number * capacity : (number + 1) * capacity,
-                    cluster * rows : (cluster + 1) * rows,
-                ],
-                preferred_element_type=F32,
-            )
-            value = part if value is None else value + part
-        out_ref[cluster] = value
+        place = jnp.concatenate(
+            [
+                one_hot(key_ref[cluster : cluster + 1, :], first + at, 128)
+                for at in range(0, arrived.shape[1], 128)
+            ],
+            axis=0,
+        )
+        placed = jnp.dot(arrived, place, preferred_element_type=F32).astype(BF16)
+        out_ref[cluster] = jnp.dot(
+            placed, operators_ref[cluster], preferred_element_type=F32
+        )
 
 
 def late_kernel(
@@ -433,62 +421,49 @@
         1000000000,
         [smem, vmem],
     )
+    held = half + quarter + eighth + tail
+    bag = call(
+        lambda *refs: pack_kernel(capacity, *refs),
+        (sep_one, two_t, three_t, lists),
+        array((held, modes), BF16),
+        4,
+        10000000,
+    )
+    pair = swap_with(bag, "sub", 1)
     extra = tail if rides else 0
     spare = () if rides else (array((tail, modes), BF16),) * 2
-    near, diag, far, one_t, *loose = call(
-        lambda *refs: pack_kernel(capacity, rides, *refs),
-        (me, sep_one, two_t, three_t, lists),
+    near, diag, far, *loose = call(
+        lambda *refs: relay_kernel(capacity, rides, half, *refs),
+        (me, bag, pair, lists),
         (
-            array((quarter + eighth + extra, modes), BF16),
-            array((eighth + extra, modes), BF16),
-            array((eighth, modes), BF16),
-            array((half, modes), BF16),
+            array((2 * (quarter + eighth) + extra, modes), BF16),
+            array((2 * eighth + extra, modes), BF16),
+            array((2 * eighth, modes), BF16),
         )
         + spare,
         4,
         10000000,
-        [smem, vmem, vmem, vmem, vmem],
-    )
+        [smem, vmem, vmem, vmem],
+    )
+    near = swap_with(near, "sub", 2)
     diag = swap_with(diag, "sub", 6)
-    near = swap_with(near, "sub", 2)
     far = swap_with(far, "sub", 4)
     if loose:
         loose = [shift_by(loose[0], "sub", 2), shift_by(loose[1], "sub", -2)]
     direct = call(
-        direct_kernel,
-        (leaf_coords, leaf_modes),
-        array((modes, dof_count), F32),
-        4,
-        1500000000,
-    )
-    moved_near = call(
-        lambda *refs: permute_kernel(2 * capacity, *refs),
-        (key, operators),
-        array((3 * capacity, clusters * rows), BF16),
-        8,
-        3000000000,
-    )
-    held = half + 2 * quarter + 4 * eighth + tail
-    bag, wants = call(
-        lambda *refs: relay_kernel(capacity, rides, *refs),
-        (me, one_t, two_t, three_t, near, diag, far, lists, *loose),
-        (array((held, modes), BF16), array((tail, 128), F32)),
-        4,
-        10000000,
-        [smem] + [vmem] * (7 + len(loose)),
-    )
-    pair = swap_with(bag, "sub", 1)
+        direct_kernel, (leaf_coords, leaf_modes), array((modes, dof_count), F32), 4, 1500000000
+    )
     partial = call(
         partial_kernel,
-        (me, direct, constraint_modes, bag),
+        (me, direct, constraint_modes, bag, pair),
         array((modes, dof_count), F32),
-        8,
-        1000000000,
-        [smem] + [vmem] * 3,
+        12,
+        1500000000,
+        [smem] + [vmem] * 4,
     )
     disp, wanted, cross = call(
-        lambda *refs: displace_kernel(capacity, *refs),
-        (me, partial, constraint_modes, pair, wants, lists),
+        lambda *refs: displace_kernel(capacity, rides, *refs),
+        (me, partial, constraint_modes, pair, near, diag, far, lists, *loose),
         (
             array((modes, dof_count), BF16),
             array((1, 4 * capacity), I32),
@@ -496,7 +471,7 @@
         ),
         12,
         3000000000,
-        [smem] + [vmem] * 5,
+        [smem] + [vmem] * (7 + len(loose)),
     )
     cross = swap_across(cross, "sub")
     flow = array((modes, capacity), BF16)
@@ -525,8 +500,8 @@
         2000000000,
     )
     early = call(
-        lambda *refs: early_kernel(capacity, *refs),
-        (moved_near, other, own, cross),
+        lambda *refs: early_kernel(2 * capacity, *refs),
+        (key, operators, other, own, cross),
         array((clusters, modes, rows), F32),
         8,
         500000000,
@@ -550,20 +525,13 @@
         out_specs=hbm,
         scratch_shapes=[pltpu.SemaphoreType.DMA],
         compiler_params=pltpu.CompilerParams(vmem_limit_bytes=4 * 1024 * 1024),
-        cost_estimate=pl.CostEstimate(
-            flops=500000000, bytes_accessed=2000000, transcendentals=0
-        ),
+        cost_estimate=pl.CostEstimate(flops=500000000, bytes_accessed=2000000, transcendentals=0),
         name="store",
     )(stresses)
     at = lax.axis_index("mode").astype(I32).reshape(1)
     share = clusters * points // mode_count
     strain_energy = call(
-        share_kernel,
-        (at, energy, arrived),
-        array((1, share), F32),
-        4,
-        1000,
-        [smem, vmem, vmem],
+        share_kernel, (at, energy, arrived), array((1, share), F32), 4, 1000, [smem, vmem, vmem]
     )
     return (stresses, strain_energy.reshape(share))
 

time: 40.1 us -> 39.9 us (level)
  waiting for transfers between devices: 11.3 us -> 13.1 us
  Pallas kernels: 13.6 us -> 12.1 us
  starting transfers between devices: 13.3 us -> 12.8 us
    ppermute x1, waiting for transfers between devices: 6.61 us -> 2.14 us  [swap_across(): lax.ppermute(value, axis, [(i, (i + 2 * (i % 2) - 1) % peers) for i in ra...]
    ppermute x2, waiting for transfers between devices: 0.01 us -> 4.47 us  [shift_by(): lax.ppermute(value, axis, [(i, (i + by) % peers) for i in range(peers)])]
    ppermute x7, waiting for transfers between devices: 4.65 us -> 6.53 us  [swap_with(): lax.ppermute(value, axis, [(i, i ^ mask) for i in range(lax.axis_size(axi...]
    pallas_call x13 -> x12, Pallas kernels: 12.6 us -> 11.2 us  [call(): pl.pallas_call(kernel, out_shape=outputs, in_specs=specs or [vmem] * len(...]
    ppermute x1, starting transfers between devices: 2.44 us -> 1.54 us  [swap_across(): lax.ppermute(value, axis, [(i, (i + 2 * (i % 2) - 1) % peers) for i in ra...]
    ppermute x7, starting transfers between devices: 8.83 us -> 9.24 us  [swap_with(): lax.ppermute(value, axis, [(i, i ^ mask) for i in range(lax.axis_size(axi...]
    unnamed x22 -> x20, local copies, waits for them, and re-layouts: 0.85 us -> 0.86 us
  transfers between devices with their start and end apart: 10 -> 10, of which waited for: 4 -> 7; matrix products, arithmetic and copies ran while one was open for 0% -> 0% of each run, Pallas kernels for 17% -> 14%
where the time goes in v5:
time: 39.9 us; the launch traced here: 39.7 us
  waiting for transfers between devices  13.1 us (33%)
  starting transfers between devices  12.8 us (32%)
  Pallas kernels  12.1 us (30%)
  local copies, waits for them, and re-layouts  0.86 us (2%)
  between operations  0.8 us (2%)
    pallas_call x12, Pallas kernels, call(): pl.pallas_call(kernel, out_shape=outputs, in_specs=specs or [vmem] * len(...  11.2 us
    ppermute x7, starting transfers between devices, swap_with(): lax.ppermute(value, axis, [(i, i ^ mask) for i in range(lax.axis_size(axi...  9.24 us
    ppermute x7, waiting for transfers between devices, swap_with(): lax.ppermute(value, axis, [(i, i ^ mask) for i in range(lax.axis_size(axi...  6.53 us
    ppermute x2, waiting for transfers between devices, shift_by(): lax.ppermute(value, axis, [(i, (i + by) % peers) for i in range(peers)])  4.47 us
    ppermute x1, waiting for transfers between devices, swap_across(): lax.ppermute(value, axis, [(i, (i + 2 * (i % 2) - 1) % peers) for i in ra...  2.14 us
    ppermute x2, starting transfers between devices, shift_by(): lax.ppermute(value, axis, [(i, (i + by) % peers) for i in range(peers)])  2.03 us
    ppermute x1, starting transfers between devices, swap_across(): lax.ppermute(value, axis, [(i, (i + 2 * (i % 2) - 1) % peers) for i in ra...  1.54 us
    pallas_call x1, Pallas kernels, shards(): pl.pallas_call(store_kernel, out_shape=array((clusters, modes, rows), F32...  0.92 us
  transfers between devices with their start and end apart: 10, of which 7 were waited for; matrix products, arithmetic and copies ran while one was open for 0% of the time, Pallas kernels for 14%

profile of v5, /device:TPU:0, one launch (start us, length us, event | category | flops | bytes accessed | tf_op | source)
XLA Modules:
  0.0 39.7 jit_solution(10109331998295786998)
XLA Ops:
  0.7 0.8 %copy-done.9 = s32[3,512]{1,0:T(4,128)S(1)} copy-done((s32[3,512]{1,0:T(4,128)S(1)}, s32[3,512]{1,0:T(4,128)}, u32[]{:S(2)}) %copy-start.9) | copy-done | bytes 6168
  1.5 0.6 %shard_map.113 = (s32[3,512]{1,0:T(4,128)S(1)}, f32[32,128]{1,0:T(8,128)S(1)}) custom-call(s32[1]{0:T(128)} %bitcast.1.refs_0_.me_ref, s32[3,512]{1,0:T(4,128)S(1)} %copy-done.9), custom_call_target="tpu_custom_call" | custom-call | flops 1000000000 | bytes 6148 | tf_op jit(solution)/shard_map/pallas_call | solution.py:39
  3.8 2.9 %collective-permute-start.1 = (bf16[208,192]{1,0:T(8,128)(2,1)S(1)}, bf16[208,192]{1,0:T(8,128)(2,1)S(1)}, u32[]{:S(2)}, u32[]{:S(2)}) collective-permute-start(bf16[208,192]{1,0:T(8,128)(2,1)S(1)} %get-tuple-element.18), channel_id=1, source_target_pairs={{0,8},{4,12},{8,0},{12,4},{16,24},{20,28},{24,16},{28,20},{1,9},{5... | collective-permute-start | bytes 239624 | tf_op jit(solution)/shard_map/ppermute | solution.py:25
  6.7 1.5 %collective-permute-start.2 = (bf16[80,192]{1,0:T(8,128)(2,1)S(1)}, bf16[80,192]{1,0:T(8,128)(2,1)S(1)}, u32[]{:S(2)}, u32[]{:S(2)}) collective-permute-start(bf16[80,192]{1,0:T(8,128)(2,1)S(1)} %get-tuple-element.19), channel_id=1, source_target_pairs={{0,24},{4,28},{8,16},{12,20},{16,8},{20,12},{24,0},{28,4},{1,25},{... | collective-permute-start | bytes 92168 | tf_op jit(solution)/shard_map/ppermute | solution.py:25
  8.2 1.0 %shard_map.116.refs_1_ = f32[192,4096]{1,0:T(8,128)S(1)} custom-call(s32[1]{0:T(128)} %bitcast.1.refs_0_.me_ref, f32[192,4096]{1,0:T(8,128)S(1)} %shard_map.114.direct_ref, bf16[8,3,256,512]{3,2,1,0:T(8,128)(2,1)S(1)} %copy-done, bf16[240,192]{1,0:T(8,128)(2,1)S(1)} %shard_map.115.bag_ref.refs_1_, ...), custom_call_target="tpu_custom_call" | custom-call | flops 1500000000 | bytes 9621508 | tf_op jit(solution)/shard_map/pallas_call | solution.py:39
  9.3 3.1 %collective-permute-done.3.refs_6_ = bf16[64,192]{1,0:T(8,128)(2,1)S(1)} collective-permute-done((bf16[64,192]{1,0:T(8,128)(2,1)S(1)}, bf16[64,192]{1,0:T(8,128)(2,1)S(1)}, u32[]{:S(2)}, u32[]{:S(2)}) %collective-permute-start.3) | collective-permute-done | bytes 24608 | tf_op jit(solution)/shard_map/ppermute | solution.py:25
  12.4 1.9 %shard_map.118 = (bf16[192,4096]{1,0:T(8,128)(2,1)S(1)}, s32[1,1536]{1,0:T(1,128)S(1)}, bf16[192,384]{1,0:T(8,128)(2,1)S(1)}) custom-call(s32[1]{0:T(128)} %bitcast.1.refs_0_.me_ref, f32[192,4096]{1,0:T(8,128)S(1)} %shard_map.116.refs_1_, bf16[8,3,256,512]{3,2,1,0:T(8,128)(2,1)S(1)} %copy-done, ...), custom_call_target="tpu_custom_call" | custom-call | flops 3000000000 | bytes 9680900 | tf_op jit(solution)/shard_map/pallas_call | solution.py:39
  14.3 1.4 %shard_map.119 = (bf16[192,384]{1,0:T(8,128)(2,1)S(1)}, bf16[192,384]{1,0:T(8,128)(2,1)S(1)}) custom-call(bf16[192,4096]{1,0:T(8,128)(2,1)S(1)} %get-tuple-element.21.refs_0_, s32[1,1536]{1,0:T(1,128)S(1)} %get-tuple-element.22.refs_1_), custom_call_target="tpu_custom_call" | custom-call | flops 2000000000 | bytes 1579008 | tf_op jit(solution)/shard_map/pallas_call | solution.py:39
  15.7 1.4 %shard_map.122 = (bf16[192,384]{1,0:T(8,128)(2,1)S(1)}, bf16[192,384]{1,0:T(8,128)(2,1)S(1)}) custom-call(bf16[192,4096]{1,0:T(8,128)(2,1)S(1)} %get-tuple-element.21.refs_0_, s32[1,1536]{1,0:T(1,128)S(1)} %get-tuple-element.22.refs_1_), custom_call_target="tpu_custom_call" | custom-call | flops 2000000000 | bytes 1579008 | tf_op jit(solution)/shard_map/pallas_call | solution.py:39
  17.2 1.5 %collective-permute-start.5 = (bf16[192,384]{1,0:T(8,128)(2,1)S(1)}, bf16[192,384]{1,0:T(8,128)(2,1)S(1)}, u32[]{:S(2)}, u32[]{:S(2)}) collective-permute-start(bf16[192,384]{1,0:T(8,128)(2,1)S(1)} %get-tuple-element.25), channel_id=1, source_target_pairs={{0,28},{4,8},{8,4},{12,16},{16,12},{20,24},{24,20},{28,0},{1,29},{... | collective-permute-start | bytes 442376 | tf_op jit(solution)/shard_map/ppermute | solution.py:30
  18.7 0.7 %collective-permute-start.6 = (bf16[192,384]{1,0:T(8,128)(2,1)S(1)}, bf16[192,384]{1,0:T(8,128)(2,1)S(1)}, u32[]{:S(2)}, u32[]{:S(2)}) collective-permute-start(bf16[192,384]{1,0:T(8,128)(2,1)S(1)} %get-tuple-element.26), channel_id=1, source_target_pairs={{0,24},{4,28},{8,0},{12,4},{16,8},{20,12},{24,16},{28,20},{1,25},{... | collective-permute-start | bytes 442376 | tf_op jit(solution)/shard_map/ppermute | solution.py:21
  19.5 1.3 %collective-permute-start.7 = (bf16[192,384]{1,0:T(8,128)(2,1)S(1)}, bf16[192,384]{1,0:T(8,128)(2,1)S(1)}, u32[]{:S(2)}, u32[]{:S(2)}) collective-permute-start(bf16[192,384]{1,0:T(8,128)(2,1)S(1)} %get-tuple-element.27), channel_id=1, source_target_pairs={{0,8},{4,12},{8,16},{12,20},{16,24},{20,28},{24,0},{28,4},{1,9},{5... | collective-permute-start | bytes 442376 | tf_op jit(solution)/shard_map/ppermute | solution.py:21
  20.8 1.4 %shard_map.121.refs_3_ = bf16[768,1152]{1,0:T(8,128)(2,1)S(1)} custom-call(s32[3,512]{1,0:T(4,128)S(1)} %get-tuple-element.16.refs_0_, bf16[3,512,384]{2,1,0:T(8,128)(2,1)S(1)} %copy-done.1), custom_call_target="tpu_custom_call" | custom-call | flops 2000000000 | bytes 1185792 | tf_op jit(solution)/shard_map/pallas_call | solution.py:39
  22.2 2.1 %collective-permute-done.5.refs_4_ = bf16[192,384]{1,0:T(8,128)(2,1)S(1)} collective-permute-done((bf16[192,384]{1,0:T(8,128)(2,1)S(1)}, bf16[192,384]{1,0:T(8,128)(2,1)S(1)}, u32[]{:S(2)}, u32[]{:S(2)}) %collective-permute-start.5) | collective-permute-done | bytes 147488 | tf_op jit(solution)/shard_map/ppermute | solution.py:30
  24.3 1.5 %shard_map.120.refs_2_ = f32[3,192,384]{2,1,0:T(8,128)S(1)} custom-call(s32[3,512]{1,0:T(4,128)S(1)} %get-tuple-element.16.refs_0_, bf16[3,512,384]{2,1,0:T(8,128)(2,1)S(1)} %copy-done.1, bf16[192,384]{1,0:T(8,128)(2,1)S(1)} %collective-permute-done.4.refs_2_, bf16[192,384]{1,0:T(8,128)(2,1)S(1)} %get-tuple-element.24.refs_3_, ...), custom_call_target="tpu_custom_call" | custom-call | flops 500000000 | bytes 1628160 | tf_op jit(solution)/shard_map/pallas_call | solution.py:39
  25.8 1.3 %collective-permute-done.6.refs_4_ = bf16[192,384]{1,0:T(8,128)(2,1)S(1)} collective-permute-done((bf16[192,384]{1,0:T(8,128)(2,1)S(1)}, bf16[192,384]{1,0:T(8,128)(2,1)S(1)}, u32[]{:S(2)}, u32[]{:S(2)}) %collective-permute-start.6) | collective-permute-done | bytes 147488 | tf_op jit(solution)/shard_map/ppermute | solution.py:21
  27.2 3.1 %collective-permute-done.7.refs_5_ = bf16[192,384]{1,0:T(8,128)(2,1)S(1)} collective-permute-done((bf16[192,384]{1,0:T(8,128)(2,1)S(1)}, bf16[192,384]{1,0:T(8,128)(2,1)S(1)}, u32[]{:S(2)}, u32[]{:S(2)}) %collective-permute-start.7) | collective-permute-done | bytes 147488 | tf_op jit(solution)/shard_map/ppermute | solution.py:21
  30.3 0.6 %shard_map.123 = (f32[3,192,384]{2,1,0:T(8,128)S(1)}, f32[3,64]{1,0:T(4,128)S(1)}) custom-call(f32[1,192]{1,0:T(1,128)S(1)} %bitcast.8, f32[3,384]{1,0:T(4,128)S(1)} %copy-done.5, f32[3,192,384]{2,1,0:T(8,128)S(1)} %shard_map.120.refs_2_, bf16[768,1152]{1,0:T(8,128)(2,1)S(1)} %shard_map.121.refs_3_, bf16[192,384]{1,0:T(8,128)(2,1)S(1)} %collective-permute-done.6.refs_4_, ...), custom_call_target="tpu_custom_call" | custom-call | flops 500000000 | bytes 2954496 | tf_op jit(solution)/shard_map/pallas_call | solution.py:39
  31.0 1.6 %collective-permute-start.8 = (f32[3,64]{1,0:T(4,128)S(1)}, f32[3,64]{1,0:T(4,128)S(1)}, u32[]{:S(2)}, u32[]{:S(2)}) collective-permute-start(f32[3,64]{1,0:T(4,128)S(1)} %get-tuple-element.29), channel_id=1, source_target_pairs={{0,1},{1,0},{2,3},{3,2},{4,5},{5,4},{6,7},{7,6},{8,9},{9,8},{10,11... | collective-permute-start | bytes 2312 | tf_op jit(solution)/shard_map/ppermute | solution.py:25
  32.5 2.0 %collective-permute-done.8 = f32[3,64]{1,0:T(4,128)S(1)} collective-permute-done((f32[3,64]{1,0:T(4,128)S(1)}, f32[3,64]{1,0:T(4,128)S(1)}, u32[]{:S(2)}, u32[]{:S(2)}) %collective-permute-start.8) | collective-permute-done | bytes 800 | tf_op jit(solution)/shard_map/ppermute | solution.py:25
  34.6 2.6 %collective-permute-start.9 = (f32[3,64]{1,0:T(4,128)S(1)}, f32[3,64]{1,0:T(4,128)S(1)}, u32[]{:S(2)}, u32[]{:S(2)}) collective-permute-start(f32[3,64]{1,0:T(4,128)S(1)} %add.3.mine_ref), channel_id=1, source_target_pairs={{0,2},{1,3},{2,0},{3,1},{4,6},{5,7},{6,4},{7,5},{8,10},{9,11},{10,... | collective-permute-start | bytes 2312 | tf_op jit(solution)/shard_map/ppermute | solution.py:25
  37.2 0.9 %store.1 = f32[3,192,384]{2,1,0:T(8,128)} custom-call(f32[3,192,384]{2,1,0:T(8,128)S(1)} %get-tuple-element.28.source_ref), custom_call_target="tpu_custom_call" | custom-call | flops 500000000 | bytes 2000000 | tf_op jit(solution)/shard_map/store/pallas_call | solution.py:521
  38.1 1.0 %collective-permute-done.9.other_ref = f32[3,64]{1,0:T(4,128)S(1)} collective-permute-done((f32[3,64]{1,0:T(4,128)S(1)}, f32[3,64]{1,0:T(4,128)S(1)}, u32[]{:S(2)}, u32[]{:S(2)}) %collective-permute-start.9) | collective-permute-done | bytes 800 | tf_op jit(solution)/shard_map/ppermute | solution.py:25
  39.0 0.7 %shard_map.124 = f32[1,48]{1,0:T(1,128)} custom-call(s32[1]{0:T(128)} %bitcast.4.at_ref, f32[3,64]{1,0:T(4,128)S(1)} %add.3.mine_ref, f32[3,64]{1,0:T(4,128)S(1)} %collective-permute-done.9.other_ref), custom_call_target="tpu_custom_call" | custom-call | flops 1000 | bytes 1540 | tf_op jit(solution)/shard_map/pallas_call | solution.py:39
  (30 shorter events, 1.8 us)
Async XLA Ops:
  0.6 1.5 %copy-start.2 = (bf16[192,128]{1,0:T(8,128)(2,1)S(1)}, bf16[192,128]{1,0:T(8,128)(2,1)}, u32[]{:S(2)}) copy-start(bf16[192,128]{1,0:T(8,128)(2,1)} %refs_0_.1) | copy-start | bytes 147460
  0.6 1.5 %copy-start.3 = (bf16[192,64]{0,1:T(8,128)(2,1)S(1)}, bf16[192,64]{0,1:T(8,128)(2,1)}, u32[]{:S(2)}) copy-start(bf16[192,64]{0,1:T(8,128)(2,1)} %param.14) | copy-start | bytes 73732
  0.7 1.5 %copy-start.4 = (bf16[192,32]{0,1:T(8,128)(2,1)S(1)}, bf16[192,32]{0,1:T(8,128)(2,1)}, u32[]{:S(2)}) copy-start(bf16[192,32]{0,1:T(8,128)(2,1)} %param.15) | copy-start | bytes 36868
  0.7 2.1 %copy-start.8 = (bf16[8,192,128]{2,1,0:T(8,128)(2,1)S(1)}, bf16[8,192,128]{2,1,0:T(8,128)(2,1)}, u32[]{:S(2)}) copy-start(bf16[8,192,128]{2,1,0:T(8,128)(2,1)} %coords_ref.1) | copy-start | bytes 1179652
  0.7 2.1 %copy-start.7 = (bf16[8,128,512]{2,1,0:T(8,128)(2,1)S(1)}, bf16[8,128,512]{2,1,0:T(8,128)(2,1)}, u32[]{:S(2)}) copy-start(bf16[8,128,512]{2,1,0:T(8,128)(2,1)} %modes_ref.1) | copy-start | bytes 3145732
  0.7 0.8 %copy-start.9 = (s32[3,512]{1,0:T(4,128)S(1)}, s32[3,512]{1,0:T(4,128)}, u32[]{:S(2)}) copy-start(s32[3,512]{1,0:T(4,128)} %refs_1_.4) | copy-start | bytes 18436
  1.5 6.7 %copy-start = (bf16[8,3,256,512]{3,2,1,0:T(8,128)(2,1)S(1)}, bf16[8,3,256,512]{3,2,1,0:T(8,128)(2,1)}, u32[]{:S(2)}) copy-start(bf16[8,3,256,512]{3,2,1,0:T(8,128)(2,1)} %refs_2_.1) | copy-start | bytes 18874372
  2.2 1.5 %collective-permute-start = (bf16[240,192]{1,0:T(8,128)(2,1)S(1)}, bf16[240,192]{1,0:T(8,128)(2,1)S(1)}, u32[]{:S(2)}, u32[]{:S(2)}) collective-permute-start(bf16[240,192]{1,0:T(8,128)(2,1)S(1)} %shard_map.115.bag_ref.refs_1_), channel_id=1, source_target_pairs={{0,4},{4,0},{8,12},{12,8},{16,20},{20,16},{24,28},{28,24},{1,5},{5... | collective-permute-start | bytes 276488 | tf_op jit(solution)/shard_map/ppermute | solution.py:25
  3.8 8.6 %collective-permute-start.1 = (bf16[208,192]{1,0:T(8,128)(2,1)S(1)}, bf16[208,192]{1,0:T(8,128)(2,1)S(1)}, u32[]{:S(2)}, u32[]{:S(2)}) collective-permute-start(bf16[208,192]{1,0:T(8,128)(2,1)S(1)} %get-tuple-element.18), channel_id=1, source_target_pairs={{0,8},{4,12},{8,0},{12,4},{16,24},{20,28},{24,16},{28,20},{1,9},{5... | collective-permute-start | bytes 239624 | tf_op jit(solution)/shard_map/ppermute | solution.py:25
  6.7 5.7 %collective-permute-start.2 = (bf16[80,192]{1,0:T(8,128)(2,1)S(1)}, bf16[80,192]{1,0:T(8,128)(2,1)S(1)}, u32[]{:S(2)}, u32[]{:S(2)}) collective-permute-start(bf16[80,192]{1,0:T(8,128)(2,1)S(1)} %get-tuple-element.19), channel_id=1, source_target_pairs={{0,24},{4,28},{8,16},{12,20},{16,8},{20,12},{24,0},{28,4},{1,25},{... | collective-permute-start | bytes 92168 | tf_op jit(solution)/shard_map/ppermute | solution.py:25
  8.2 4.2 %collective-permute-start.3 = (bf16[64,192]{1,0:T(8,128)(2,1)S(1)}, bf16[64,192]{1,0:T(8,128)(2,1)S(1)}, u32[]{:S(2)}, u32[]{:S(2)}) collective-permute-start(bf16[64,192]{1,0:T(8,128)(2,1)S(1)} %get-tuple-element.20), channel_id=1, source_target_pairs={{0,16},{4,20},{8,24},{12,28},{16,0},{20,4},{24,8},{28,12},{1,17},{... | collective-permute-start | bytes 73736 | tf_op jit(solution)/shard_map/ppermute | solution.py:25
  15.7 5.1 %copy-start.1 = (bf16[3,512,384]{2,1,0:T(8,128)(2,1)S(1)}, bf16[3,512,384]{2,1,0:T(8,128)(2,1)}, u32[]{:S(2)}) copy-start(bf16[3,512,384]{2,1,0:T(8,128)(2,1)} %refs_1_.6) | copy-start | bytes 3538948
  17.1 5.0 %collective-permute-start.4 = (bf16[192,384]{1,0:T(8,128)(2,1)S(1)}, bf16[192,384]{1,0:T(8,128)(2,1)S(1)}, u32[]{:S(2)}, u32[]{:S(2)}) collective-permute-start(bf16[192,384]{1,0:T(8,128)(2,1)S(1)} %get-tuple-element.23), channel_id=1, source_target_pairs={{0,4},{4,0},{8,12},{12,8},{16,20},{20,16},{24,28},{28,24},{1,5},{5... | collective-permute-start | bytes 442376 | tf_op jit(solution)/shard_map/ppermute | solution.py:25
  17.2 7.1 %collective-permute-start.5 = (bf16[192,384]{1,0:T(8,128)(2,1)S(1)}, bf16[192,384]{1,0:T(8,128)(2,1)S(1)}, u32[]{:S(2)}, u32[]{:S(2)}) collective-permute-start(bf16[192,384]{1,0:T(8,128)(2,1)S(1)} %get-tuple-element.25), channel_id=1, source_target_pairs={{0,28},{4,8},{8,4},{12,16},{16,12},{20,24},{24,20},{28,0},{1,29},{... | collective-permute-start | bytes 442376 | tf_op jit(solution)/shard_map/ppermute | solution.py:30
  18.7 8.4 %collective-permute-start.6 = (bf16[192,384]{1,0:T(8,128)(2,1)S(1)}, bf16[192,384]{1,0:T(8,128)(2,1)S(1)}, u32[]{:S(2)}, u32[]{:S(2)}) collective-permute-start(bf16[192,384]{1,0:T(8,128)(2,1)S(1)} %get-tuple-element.26), channel_id=1, source_target_pairs={{0,24},{4,28},{8,0},{12,4},{16,8},{20,12},{24,16},{28,20},{1,25},{... | collective-permute-start | bytes 442376 | tf_op jit(solution)/shard_map/ppermute | solution.py:21
  19.5 10.9 %collective-permute-start.7 = (bf16[192,384]{1,0:T(8,128)(2,1)S(1)}, bf16[192,384]{1,0:T(8,128)(2,1)S(1)}, u32[]{:S(2)}, u32[]{:S(2)}) collective-permute-start(bf16[192,384]{1,0:T(8,128)(2,1)S(1)} %get-tuple-element.27), channel_id=1, source_target_pairs={{0,8},{4,12},{8,16},{12,20},{16,24},{20,28},{24,0},{28,4},{1,9},{5... | collective-permute-start | bytes 442376 | tf_op jit(solution)/shard_map/ppermute | solution.py:21
  20.8 9.6 %copy-start.5 = (f32[3,384]{1,0:T(4,128)S(1)}, f32[3,384]{1,0:T(4,128)}, u32[]{:S(2)}) copy-start(f32[3,384]{1,0:T(4,128)} %refs_1_.7) | copy-start | bytes 13828
  20.8 9.6 %copy-start.6 = (f32[192]{0:T(256)S(1)}, f32[192]{0:T(256)}, u32[]{:S(2)}) copy-start(f32[192]{0:T(256)} %param.19) | copy-start | bytes 2308
  31.0 3.6 %collective-permute-start.8 = (f32[3,64]{1,0:T(4,128)S(1)}, f32[3,64]{1,0:T(4,128)S(1)}, u32[]{:S(2)}, u32[]{:S(2)}) collective-permute-start(f32[3,64]{1,0:T(4,128)S(1)} %get-tuple-element.29), channel_id=1, source_target_pairs={{0,1},{1,0},{2,3},{3,2},{4,5},{5,4},{6,7},{7,6},{8,9},{9,8},{10,11... | collective-permute-start | bytes 2312 | tf_op jit(solution)/shard_map/ppermute | solution.py:25
  34.6 4.5 %collective-permute-start.9 = (f32[3,64]{1,0:T(4,128)S(1)}, f32[3,64]{1,0:T(4,128)S(1)}, u32[]{:S(2)}, u32[]{:S(2)}) collective-permute-start(f32[3,64]{1,0:T(4,128)S(1)} %add.3.mine_ref), channel_id=1, source_target_pairs={{0,2},{1,3},{2,0},{3,1},{4,6},{5,7},{6,4},{7,5},{8,10},{9,11},{10,... | collective-permute-start | bytes 2312 | tf_op jit(solution)/shard_map/ppermute | solution.py:25

commit v6 on v5

--- a/solution.py
+++ b/solution.py
@@ -13,12 +13,7 @@
 BASE = 64
 GROUP = 4
 
-PLUS, MINUS, PAIR, OWN, CROSS = range(5)
-
-
-def shift_by(value, axis, by):
-    peers = lax.axis_size(axis)
-    return lax.ppermute(value, axis, [(i, (i + by) % peers) for i in range(peers)])
+OUTER, CROSS, PAIR, OWN, NEAR = range(5)
 
 
 def swap_with(value, axis, mask):
@@ -29,6 +24,13 @@
     peers = lax.axis_size(axis)
     return lax.ppermute(
         value, axis, [(i, (i + 2 * (i % 2) - 1) % peers) for i in range(peers)]
+    )
+
+
+def swap_outer(value, axis):
+    peers = lax.axis_size(axis)
+    return lax.ppermute(
+        value, axis, [(i, (i + 4 * (i // 2 % 2) - 2) % peers) for i in range(peers)]
     )
 
 
@@ -99,7 +101,8 @@
     distance = jnp.where(distance < 0, distance + sub_count, distance)
     offset = jnp.where(distance > sub_count // 2, distance - sub_count, distance)
     cross = 2 * odd - 1
-    classes = (2, -2, -cross, 0, cross)
+    outer = 4 * lax.rem(lax.div(me, 2), 2) - 2
+    classes = (outer, cross, -cross, 0, -outer)
     masks = jnp.concatenate(
         [jnp.where((offset == each) & (row >= 0), 1.0, 0.0) for each in classes], axis=0
     )
@@ -164,8 +167,8 @@
     odd = lax.rem(me_ref[0], 2)
     lists = lists_ref[...]
     relayed = pair_ref[half + quarter + eighth :, :128].astype(F32)[tall : 2 * tall, :]
-    up = list_rows(lists, PLUS, capacity) + [relayed]
-    down = list_rows(lists, MINUS, capacity) + [relayed]
+    beside = list_rows(lists, NEAR, capacity) + [relayed]
+    opposite = list_rows(lists, OUTER, capacity) + [relayed]
 
     def put(ref, at, rows, core, value):
         ref[pl.ds(pl.multiple_of(at + core * rows, rows), rows), :] = value
@@ -177,14 +180,11 @@
         put(near_ref, 2 * quarter, eighth, core, three)
         put(diag_ref, 0, eighth, core, three)
         put(far_ref, 0, eighth, core, three)
+    put_lists(near_ref, 2 * (quarter + eighth), beside, tail)
     if rides:
-        low = lax.rem(lax.div(me_ref[0], 2), 2) == 0
-        up, down = filled(up, tail), filled(down, tail)
-        put_lists(near_ref, 2 * (quarter + eighth), [jnp.where(low, up, down)], tail)
-        put_lists(diag_ref, 2 * eighth, [jnp.where(low, down, up)], tail)
+        put_lists(diag_ref, 2 * eighth, opposite, tail)
     else:
-        put_lists(rest[0], 0, up, tail)
-        put_lists(rest[1], 0, down, tail)
+        put_lists(rest[0], 0, opposite, tail)
 
 
 def direct_kernel(coords_ref, modes_ref, out_ref):
@@ -259,7 +259,7 @@
     lists_ref,
     *rest,
 ):
-    disp_ref, wanted_ref, cross_ref = rest[-3:]
+    disp_ref, wanted_ref, first_ref = rest[-3:]
     me = me_ref[0]
     chip, near, diag, far = places(me)
     block = couple_ref.shape[2]
@@ -274,23 +274,18 @@
         disp_ref[:, columns] = (partial_ref[:, columns] + value).astype(BF16)
     tall = 2 * capacity // 128
     tail = list_height(capacity, 2)
-    if rides:
-        beside = near_ref[2 * (quarter + eighth) :, :128].astype(F32)
-        opposite = diag_ref[2 * eighth :, :128].astype(F32)
-        low = lax.rem(chip, 2) == 0
-        behind, ahead = jnp.where(low, opposite, beside), jnp.where(low, beside, opposite)
-    else:
-        behind, ahead = rest[0][:, :128].astype(F32), rest[1][:, :128].astype(F32)
-    odd = lax.rem(me, 2) == 1
-    across = jnp.where(odd, ahead, behind)
+    beside = near_ref[2 * (quarter + eighth) :, :128].astype(F32)
+    opposite = (diag_ref[2 * eighth :, :128] if rides else rest[0][:, :128]).astype(F32)
+    odd, high = lax.rem(me, 2), lax.rem(chip, 2)
+    across = jnp.where(odd != high, beside, opposite)
     ours = pair_ref[pair_ref.shape[0] - tail :, :128].astype(F32)
-    wanted_ref[:, :capacity] = unpacked(behind, 0, capacity)
-    wanted_ref[:, capacity : 2 * capacity] = unpacked(ahead, 0, capacity)
+    wanted_ref[:, :capacity] = unpacked(opposite, 0, capacity)
+    wanted_ref[:, capacity : 2 * capacity] = unpacked(across, tall, capacity)
     wanted_ref[:, 2 * capacity : 3 * capacity] = unpacked(ours, 0, capacity)
     wanted_ref[:, 3 * capacity :] = unpacked(
         filled(list_rows(lists_ref[...], OWN, capacity), tail), 0, capacity
     )
-    cross_ref[...] = gathered(disp_ref, unpacked(across, tall, capacity))
+    first_ref[...] = gathered(disp_ref, unpacked(beside, 0, capacity))
 
 
 def gather_kernel(capacity, first, disp_ref, wanted_ref, left_ref, right_ref):
@@ -317,9 +312,9 @@
                 )
 
 
-def early_kernel(first, key_ref, operators_ref, pair_ref, own_ref, cross_ref, out_ref):
+def early_kernel(first, key_ref, operators_ref, pair_ref, own_ref, near_ref, out_ref):
     clusters, _, _ = out_ref.shape
-    arrived = jnp.concatenate([pair_ref[...], own_ref[...], cross_ref[...]], axis=1)
+    arrived = jnp.concatenate([pair_ref[...], own_ref[...], near_ref[...]], axis=1)
     for cluster in range(clusters):
         place = jnp.concatenate(
             [
@@ -340,15 +335,15 @@
     compliance_ref,
     early_ref,
     moved_ref,
-    plus_ref,
-    minus_ref,
+    outer_ref,
+    cross_ref,
     stress_ref,
     energy_ref,
 ):
     clusters, modes, rows = stress_ref.shape
     points = energy_ref.shape[1]
     weight = jnp.broadcast_to(weight_ref[...], (8, modes)).T[:, :1]
-    arrived = jnp.concatenate([plus_ref[...], minus_ref[...]], axis=1)
+    arrived = jnp.concatenate([outer_ref[...], cross_ref[...]], axis=1)
     late = jnp.dot(arrived, moved_ref[...], preferred_element_type=F32)
     for cluster in range(clusters):
         value = early_ref[cluster] + late[:, cluster * rows : (cluster + 1) * rows]
@@ -431,12 +426,12 @@
     )
     pair = swap_with(bag, "sub", 1)
     extra = tail if rides else 0
-    spare = () if rides else (array((tail, modes), BF16),) * 2
+    spare = () if rides else (array((tail, modes), BF16),)
     near, diag, far, *loose = call(
         lambda *refs: relay_kernel(capacity, rides, half, *refs),
         (me, bag, pair, lists),
         (
-            array((2 * (quarter + eighth) + extra, modes), BF16),
+            array((2 * (quarter + eighth) + tail, modes), BF16),
             array((2 * eighth + extra, modes), BF16),
             array((2 * eighth, modes), BF16),
         )
@@ -448,8 +443,7 @@
     near = swap_with(near, "sub", 2)
     diag = swap_with(diag, "sub", 6)
     far = swap_with(far, "sub", 4)
-    if loose:
-        loose = [shift_by(loose[0], "sub", 2), shift_by(loose[1], "sub", -2)]
+    loose = [swap_outer(value, "sub") for value in loose]
     direct = call(
         direct_kernel, (leaf_coords, leaf_modes), array((modes, dof_count), F32), 4, 1500000000
     )
@@ -461,7 +455,7 @@
         1500000000,
         [smem] + [vmem] * 4,
     )
-    disp, wanted, cross = call(
+    disp, wanted, beside = call(
         lambda *refs: displace_kernel(capacity, rides, *refs),
         (me, partial, constraint_modes, pair, near, diag, far, lists, *loose),
         (
@@ -473,17 +467,17 @@
         3000000000,
         [smem] + [vmem] * (7 + len(loose)),
     )
-    cross = swap_across(cross, "sub")
+    beside = swap_with(beside, "sub", 2)
     flow = array((modes, capacity), BF16)
-    plus, minus = call(
+    outer, cross = call(
         lambda *refs: gather_kernel(capacity, 0, *refs),
         (disp, wanted),
         (flow, flow),
         12,
         2000000000,
     )
-    plus = shift_by(plus, "sub", -2)
-    minus = shift_by(minus, "sub", 2)
+    outer = swap_outer(outer, "sub")
+    cross = swap_across(cross, "sub")
     other, own = call(
         lambda *refs: gather_kernel(capacity, 2, *refs),
         (disp, wanted),
@@ -501,14 +495,14 @@
     )
     early = call(
         lambda *refs: early_kernel(2 * capacity, *refs),
-        (key, operators, other, own, cross),
+        (key, operators, other, own, beside),
         array((clusters, modes, rows), F32),
         8,
         500000000,
     )
     stresses, energy = call(
         lambda *refs: late_kernel(0.5 / (modes * mode_count), *refs),
-        (modal_weight.reshape(1, modes), compliance, early, moved_far, plus, minus),
+        (modal_weight.reshape(1, modes), compliance, early, moved_far, outer, cross),
         (array((clusters, modes, rows), F32), array((clusters, points), F32)),
         8,
         500000000,

time: 39.9 us -> 39 us (0.977)
  waiting for transfers between devices: 13.1 us -> 11.8 us
  starting transfers between devices: 12.8 us -> 13.2 us
    ppermute x2 -> x1, waiting for transfers between devices: 4.47 us -> 1.75 us  [swap_outer(): lax.ppermute(value, axis, [(i, (i + 4 * (i // 2 % 2) - 2) % peers) for i...]
    ppermute x7 -> x8, starting transfers between devices: 9.24 us -> 10.8 us  [swap_with(): lax.ppermute(value, axis, [(i, i ^ mask) for i in range(lax.axis_size(axi...]
    ppermute x7 -> x8, waiting for transfers between devices: 6.53 us -> 7.94 us  [swap_with(): lax.ppermute(value, axis, [(i, i ^ mask) for i in range(lax.axis_size(axi...]
    ppermute x2 -> x1, starting transfers between devices: 2.03 us -> 0.67 us  [swap_outer(): lax.ppermute(value, axis, [(i, (i + 4 * (i // 2 % 2) - 2) % peers) for i...]
where the time goes in v6:
time: 39 us; the launch traced here: 38.7 us
  starting transfers between devices  13.2 us (34%)
  Pallas kernels  12.1 us (31%)
  waiting for transfers between devices  11.8 us (30%)
  local copies, waits for them, and re-layouts  0.86 us (2%)
  between operations  0.8 us (2%)
    pallas_call x12, Pallas kernels, call(): pl.pallas_call(kernel, out_shape=outputs, in_specs=specs or [vmem] * len(...  11.2 us
    ppermute x8, starting transfers between devices, swap_with(): lax.ppermute(value, axis, [(i, i ^ mask) for i in range(lax.axis_size(axi...  10.8 us
    ppermute x8, waiting for transfers between devices, swap_with(): lax.ppermute(value, axis, [(i, i ^ mask) for i in range(lax.axis_size(axi...  7.94 us
    ppermute x1, waiting for transfers between devices, swap_across(): lax.ppermute(value, axis, [(i, (i + 2 * (i % 2) - 1) % peers) for i in ra...  2.08 us
    ppermute x1, waiting for transfers between devices, swap_outer(): lax.ppermute(value, axis, [(i, (i + 4 * (i // 2 % 2) - 2) % peers) for i...  1.75 us
    ppermute x1, starting transfers between devices, swap_across(): lax.ppermute(value, axis, [(i, (i + 2 * (i % 2) - 1) % peers) for i in ra...  1.73 us
    pallas_call x1, Pallas kernels, shards(): pl.pallas_call(store_kernel, out_shape=array((clusters, modes, rows), F32...  0.92 us
    unnamed x20, local copies, waits for them, and re-layouts  0.86 us
  transfers between devices with their start and end apart: 10, of which 7 were waited for; matrix products, arithmetic and copies ran while one was open for 0% of the time, Pallas kernels for 14%

profile of v6, /device:TPU:0, one launch (start us, length us, event | category | flops | bytes accessed | tf_op | source)
XLA Modules:
  0.0 38.7 jit_solution(10970061079654445982)
XLA Ops:
  0.7 0.8 %copy-done.9 = s32[3,512]{1,0:T(4,128)S(1)} copy-done((s32[3,512]{1,0:T(4,128)S(1)}, s32[3,512]{1,0:T(4,128)}, u32[]{:S(2)}) %copy-start.9) | copy-done | bytes 6168
  1.5 0.6 %shard_map.113 = (s32[3,512]{1,0:T(4,128)S(1)}, f32[32,128]{1,0:T(8,128)S(1)}) custom-call(s32[1]{0:T(128)} %bitcast.1.refs_0_.me_ref, s32[3,512]{1,0:T(4,128)S(1)} %copy-done.9), custom_call_target="tpu_custom_call" | custom-call | flops 1000000000 | bytes 6148 | tf_op jit(solution)/shard_map/pallas_call | solution.py:41
  3.8 2.9 %collective-permute-start.1 = (bf16[208,192]{1,0:T(8,128)(2,1)S(1)}, bf16[208,192]{1,0:T(8,128)(2,1)S(1)}, u32[]{:S(2)}, u32[]{:S(2)}) collective-permute-start(bf16[208,192]{1,0:T(8,128)(2,1)S(1)} %get-tuple-element.18), channel_id=1, source_target_pairs={{0,8},{4,12},{8,0},{12,4},{16,24},{20,28},{24,16},{28,20},{1,9},{5... | collective-permute-start | bytes 239624 | tf_op jit(solution)/shard_map/ppermute | solution.py:20
  6.7 1.5 %collective-permute-start.2 = (bf16[80,192]{1,0:T(8,128)(2,1)S(1)}, bf16[80,192]{1,0:T(8,128)(2,1)S(1)}, u32[]{:S(2)}, u32[]{:S(2)}) collective-permute-start(bf16[80,192]{1,0:T(8,128)(2,1)S(1)} %get-tuple-element.19), channel_id=1, source_target_pairs={{0,24},{4,28},{8,16},{12,20},{16,8},{20,12},{24,0},{28,4},{1,25},{... | collective-permute-start | bytes 92168 | tf_op jit(solution)/shard_map/ppermute | solution.py:20
  8.2 1.0 %shard_map.116.refs_1_ = f32[192,4096]{1,0:T(8,128)S(1)} custom-call(s32[1]{0:T(128)} %bitcast.1.refs_0_.me_ref, f32[192,4096]{1,0:T(8,128)S(1)} %shard_map.114.direct_ref, bf16[8,3,256,512]{3,2,1,0:T(8,128)(2,1)S(1)} %copy-done, bf16[240,192]{1,0:T(8,128)(2,1)S(1)} %shard_map.115.bag_ref.refs_1_, ...), custom_call_target="tpu_custom_call" | custom-call | flops 1500000000 | bytes 9621508 | tf_op jit(solution)/shard_map/pallas_call | solution.py:41
  9.3 3.1 %collective-permute-done.3.refs_6_ = bf16[64,192]{1,0:T(8,128)(2,1)S(1)} collective-permute-done((bf16[64,192]{1,0:T(8,128)(2,1)S(1)}, bf16[64,192]{1,0:T(8,128)(2,1)S(1)}, u32[]{:S(2)}, u32[]{:S(2)}) %collective-permute-start.3) | collective-permute-done | bytes 24608 | tf_op jit(solution)/shard_map/ppermute | solution.py:20
  12.4 1.9 %shard_map.118 = (bf16[192,4096]{1,0:T(8,128)(2,1)S(1)}, s32[1,1536]{1,0:T(1,128)S(1)}, bf16[192,384]{1,0:T(8,128)(2,1)S(1)}) custom-call(s32[1]{0:T(128)} %bitcast.1.refs_0_.me_ref, f32[192,4096]{1,0:T(8,128)S(1)} %shard_map.116.refs_1_, bf16[8,3,256,512]{3,2,1,0:T(8,128)(2,1)S(1)} %copy-done, ...), custom_call_target="tpu_custom_call" | custom-call | flops 3000000000 | bytes 9680900 | tf_op jit(solution)/shard_map/pallas_call | solution.py:41
  14.3 1.4 %shard_map.119 = (bf16[192,384]{1,0:T(8,128)(2,1)S(1)}, bf16[192,384]{1,0:T(8,128)(2,1)S(1)}) custom-call(bf16[192,4096]{1,0:T(8,128)(2,1)S(1)} %get-tuple-element.21.refs_0_, s32[1,1536]{1,0:T(1,128)S(1)} %get-tuple-element.22.refs_1_), custom_call_target="tpu_custom_call" | custom-call | flops 2000000000 | bytes 1579008 | tf_op jit(solution)/shard_map/pallas_call | solution.py:41
  15.7 1.4 %shard_map.122 = (bf16[192,384]{1,0:T(8,128)(2,1)S(1)}, bf16[192,384]{1,0:T(8,128)(2,1)S(1)}) custom-call(bf16[192,4096]{1,0:T(8,128)(2,1)S(1)} %get-tuple-element.21.refs_0_, s32[1,1536]{1,0:T(1,128)S(1)} %get-tuple-element.22.refs_1_), custom_call_target="tpu_custom_call" | custom-call | flops 2000000000 | bytes 1579008 | tf_op jit(solution)/shard_map/pallas_call | solution.py:41
  17.2 1.6 %collective-permute-start.5 = (bf16[192,384]{1,0:T(8,128)(2,1)S(1)}, bf16[192,384]{1,0:T(8,128)(2,1)S(1)}, u32[]{:S(2)}, u32[]{:S(2)}) collective-permute-start(bf16[192,384]{1,0:T(8,128)(2,1)S(1)} %get-tuple-element.25), channel_id=1, source_target_pairs={{0,8},{4,12},{8,0},{12,4},{16,24},{20,28},{24,16},{28,20},{1,9},{5... | collective-permute-start | bytes 442376 | tf_op jit(solution)/shard_map/ppermute | solution.py:20
  18.8 0.7 %collective-permute-start.6 = (bf16[192,384]{1,0:T(8,128)(2,1)S(1)}, bf16[192,384]{1,0:T(8,128)(2,1)S(1)}, u32[]{:S(2)}, u32[]{:S(2)}) collective-permute-start(bf16[192,384]{1,0:T(8,128)(2,1)S(1)} %get-tuple-element.26), channel_id=1, source_target_pairs={{0,24},{4,28},{8,16},{12,20},{16,8},{20,12},{24,0},{28,4},{1,25},{... | collective-permute-start | bytes 442376 | tf_op jit(solution)/shard_map/ppermute | solution.py:32
  19.4 1.7 %collective-permute-start.7 = (bf16[192,384]{1,0:T(8,128)(2,1)S(1)}, bf16[192,384]{1,0:T(8,128)(2,1)S(1)}, u32[]{:S(2)}, u32[]{:S(2)}) collective-permute-start(bf16[192,384]{1,0:T(8,128)(2,1)S(1)} %get-tuple-element.27), channel_id=1, source_target_pairs={{0,28},{4,8},{8,4},{12,16},{16,12},{20,24},{24,20},{28,0},{1,29},{... | collective-permute-start | bytes 442376 | tf_op jit(solution)/shard_map/ppermute | solution.py:25
  21.2 1.4 %shard_map.121.refs_3_ = bf16[768,1152]{1,0:T(8,128)(2,1)S(1)} custom-call(s32[3,512]{1,0:T(4,128)S(1)} %get-tuple-element.16.refs_0_, bf16[3,512,384]{2,1,0:T(8,128)(2,1)S(1)} %copy-done.1), custom_call_target="tpu_custom_call" | custom-call | flops 2000000000 | bytes 1185792 | tf_op jit(solution)/shard_map/pallas_call | solution.py:41
  22.6 1.4 %collective-permute-done.5.refs_4_ = bf16[192,384]{1,0:T(8,128)(2,1)S(1)} collective-permute-done((bf16[192,384]{1,0:T(8,128)(2,1)S(1)}, bf16[192,384]{1,0:T(8,128)(2,1)S(1)}, u32[]{:S(2)}, u32[]{:S(2)}) %collective-permute-start.5) | collective-permute-done | bytes 147488 | tf_op jit(solution)/shard_map/ppermute | solution.py:20
  24.0 1.5 %shard_map.120.refs_2_ = f32[3,192,384]{2,1,0:T(8,128)S(1)} custom-call(s32[3,512]{1,0:T(4,128)S(1)} %get-tuple-element.16.refs_0_, bf16[3,512,384]{2,1,0:T(8,128)(2,1)S(1)} %copy-done.1, bf16[192,384]{1,0:T(8,128)(2,1)S(1)} %collective-permute-done.4.refs_2_, bf16[192,384]{1,0:T(8,128)(2,1)S(1)} %get-tuple-element.24.refs_3_, ...), custom_call_target="tpu_custom_call" | custom-call | flops 500000000 | bytes 1628160 | tf_op jit(solution)/shard_map/pallas_call | solution.py:41
  25.5 1.8 %collective-permute-done.6.refs_4_ = bf16[192,384]{1,0:T(8,128)(2,1)S(1)} collective-permute-done((bf16[192,384]{1,0:T(8,128)(2,1)S(1)}, bf16[192,384]{1,0:T(8,128)(2,1)S(1)}, u32[]{:S(2)}, u32[]{:S(2)}) %collective-permute-start.6) | collective-permute-done | bytes 147488 | tf_op jit(solution)/shard_map/ppermute | solution.py:32
  27.3 2.1 %collective-permute-done.7.refs_5_ = bf16[192,384]{1,0:T(8,128)(2,1)S(1)} collective-permute-done((bf16[192,384]{1,0:T(8,128)(2,1)S(1)}, bf16[192,384]{1,0:T(8,128)(2,1)S(1)}, u32[]{:S(2)}, u32[]{:S(2)}) %collective-permute-start.7) | collective-permute-done | bytes 147488 | tf_op jit(solution)/shard_map/ppermute | solution.py:25
  29.4 0.6 %shard_map.123 = (f32[3,192,384]{2,1,0:T(8,128)S(1)}, f32[3,64]{1,0:T(4,128)S(1)}) custom-call(f32[1,192]{1,0:T(1,128)S(1)} %bitcast.8, f32[3,384]{1,0:T(4,128)S(1)} %copy-done.5, f32[3,192,384]{2,1,0:T(8,128)S(1)} %shard_map.120.refs_2_, bf16[768,1152]{1,0:T(8,128)(2,1)S(1)} %shard_map.121.refs_3_, bf16[192,384]{1,0:T(8,128)(2,1)S(1)} %collective-permute-done.6.refs_4_, ...), custom_call_target="tpu_custom_call" | custom-call | flops 500000000 | bytes 2954496 | tf_op jit(solution)/shard_map/pallas_call | solution.py:41
  30.0 1.6 %collective-permute-start.8 = (f32[3,64]{1,0:T(4,128)S(1)}, f32[3,64]{1,0:T(4,128)S(1)}, u32[]{:S(2)}, u32[]{:S(2)}) collective-permute-start(f32[3,64]{1,0:T(4,128)S(1)} %get-tuple-element.29), channel_id=1, source_target_pairs={{0,1},{1,0},{2,3},{3,2},{4,5},{5,4},{6,7},{7,6},{8,9},{9,8},{10,11... | collective-permute-start | bytes 2312 | tf_op jit(solution)/shard_map/ppermute | solution.py:20
  31.6 2.0 %collective-permute-done.8 = f32[3,64]{1,0:T(4,128)S(1)} collective-permute-done((f32[3,64]{1,0:T(4,128)S(1)}, f32[3,64]{1,0:T(4,128)S(1)}, u32[]{:S(2)}, u32[]{:S(2)}) %collective-permute-start.8) | collective-permute-done | bytes 800 | tf_op jit(solution)/shard_map/ppermute | solution.py:20
  33.6 2.6 %collective-permute-start.9 = (f32[3,64]{1,0:T(4,128)S(1)}, f32[3,64]{1,0:T(4,128)S(1)}, u32[]{:S(2)}, u32[]{:S(2)}) collective-permute-start(f32[3,64]{1,0:T(4,128)S(1)} %add.3.mine_ref), channel_id=1, source_target_pairs={{0,2},{1,3},{2,0},{3,1},{4,6},{5,7},{6,4},{7,5},{8,10},{9,11},{10,... | collective-permute-start | bytes 2312 | tf_op jit(solution)/shard_map/ppermute | solution.py:20
  36.2 0.9 %store.1 = f32[3,192,384]{2,1,0:T(8,128)} custom-call(f32[3,192,384]{2,1,0:T(8,128)S(1)} %get-tuple-element.28.source_ref), custom_call_target="tpu_custom_call" | custom-call | flops 500000000 | bytes 2000000 | tf_op jit(solution)/shard_map/store/pallas_call | solution.py:515
  37.1 1.0 %collective-permute-done.9.other_ref = f32[3,64]{1,0:T(4,128)S(1)} collective-permute-done((f32[3,64]{1,0:T(4,128)S(1)}, f32[3,64]{1,0:T(4,128)S(1)}, u32[]{:S(2)}, u32[]{:S(2)}) %collective-permute-start.9) | collective-permute-done | bytes 800 | tf_op jit(solution)/shard_map/ppermute | solution.py:20
  38.1 0.7 %shard_map.124 = f32[1,48]{1,0:T(1,128)} custom-call(s32[1]{0:T(128)} %bitcast.4.at_ref, f32[3,64]{1,0:T(4,128)S(1)} %add.3.mine_ref, f32[3,64]{1,0:T(4,128)S(1)} %collective-permute-done.9.other_ref), custom_call_target="tpu_custom_call" | custom-call | flops 1000 | bytes 1540 | tf_op jit(solution)/shard_map/pallas_call | solution.py:41
  (30 shorter events, 1.8 us)
Async XLA Ops:
  0.6 1.5 %copy-start.2 = (bf16[192,128]{1,0:T(8,128)(2,1)S(1)}, bf16[192,128]{1,0:T(8,128)(2,1)}, u32[]{:S(2)}) copy-start(bf16[192,128]{1,0:T(8,128)(2,1)} %refs_0_.1) | copy-start | bytes 147460
  0.6 1.5 %copy-start.3 = (bf16[192,64]{0,1:T(8,128)(2,1)S(1)}, bf16[192,64]{0,1:T(8,128)(2,1)}, u32[]{:S(2)}) copy-start(bf16[192,64]{0,1:T(8,128)(2,1)} %param.14) | copy-start | bytes 73732
  0.7 1.5 %copy-start.4 = (bf16[192,32]{0,1:T(8,128)(2,1)S(1)}, bf16[192,32]{0,1:T(8,128)(2,1)}, u32[]{:S(2)}) copy-start(bf16[192,32]{0,1:T(8,128)(2,1)} %param.15) | copy-start | bytes 36868
  0.7 2.1 %copy-start.8 = (bf16[8,192,128]{2,1,0:T(8,128)(2,1)S(1)}, bf16[8,192,128]{2,1,0:T(8,128)(2,1)}, u32[]{:S(2)}) copy-start(bf16[8,192,128]{2,1,0:T(8,128)(2,1)} %coords_ref.1) | copy-start | bytes 1179652
  0.7 2.1 %copy-start.7 = (bf16[8,128,512]{2,1,0:T(8,128)(2,1)S(1)}, bf16[8,128,512]{2,1,0:T(8,128)(2,1)}, u32[]{:S(2)}) copy-start(bf16[8,128,512]{2,1,0:T(8,128)(2,1)} %modes_ref.1) | copy-start | bytes 3145732
  0.7 0.8 %copy-start.9 = (s32[3,512]{1,0:T(4,128)S(1)}, s32[3,512]{1,0:T(4,128)}, u32[]{:S(2)}) copy-start(s32[3,512]{1,0:T(4,128)} %refs_1_.4) | copy-start | bytes 18436
  1.5 6.7 %copy-start = (bf16[8,3,256,512]{3,2,1,0:T(8,128)(2,1)S(1)}, bf16[8,3,256,512]{3,2,1,0:T(8,128)(2,1)}, u32[]{:S(2)}) copy-start(bf16[8,3,256,512]{3,2,1,0:T(8,128)(2,1)} %refs_2_.1) | copy-start | bytes 18874372
  2.2 1.5 %collective-permute-start = (bf16[240,192]{1,0:T(8,128)(2,1)S(1)}, bf16[240,192]{1,0:T(8,128)(2,1)S(1)}, u32[]{:S(2)}, u32[]{:S(2)}) collective-permute-start(bf16[240,192]{1,0:T(8,128)(2,1)S(1)} %shard_map.115.bag_ref.refs_1_), channel_id=1, source_target_pairs={{0,4},{4,0},{8,12},{12,8},{16,20},{20,16},{24,28},{28,24},{1,5},{5... | collective-permute-start | bytes 276488 | tf_op jit(solution)/shard_map/ppermute | solution.py:20
  3.8 8.6 %collective-permute-start.1 = (bf16[208,192]{1,0:T(8,128)(2,1)S(1)}, bf16[208,192]{1,0:T(8,128)(2,1)S(1)}, u32[]{:S(2)}, u32[]{:S(2)}) collective-permute-start(bf16[208,192]{1,0:T(8,128)(2,1)S(1)} %get-tuple-element.18), channel_id=1, source_target_pairs={{0,8},{4,12},{8,0},{12,4},{16,24},{20,28},{24,16},{28,20},{1,9},{5... | collective-permute-start | bytes 239624 | tf_op jit(solution)/shard_map/ppermute | solution.py:20
  6.7 5.7 %collective-permute-start.2 = (bf16[80,192]{1,0:T(8,128)(2,1)S(1)}, bf16[80,192]{1,0:T(8,128)(2,1)S(1)}, u32[]{:S(2)}, u32[]{:S(2)}) collective-permute-start(bf16[80,192]{1,0:T(8,128)(2,1)S(1)} %get-tuple-element.19), channel_id=1, source_target_pairs={{0,24},{4,28},{8,16},{12,20},{16,8},{20,12},{24,0},{28,4},{1,25},{... | collective-permute-start | bytes 92168 | tf_op jit(solution)/shard_map/ppermute | solution.py:20
  8.2 4.2 %collective-permute-start.3 = (bf16[64,192]{1,0:T(8,128)(2,1)S(1)}, bf16[64,192]{1,0:T(8,128)(2,1)S(1)}, u32[]{:S(2)}, u32[]{:S(2)}) collective-permute-start(bf16[64,192]{1,0:T(8,128)(2,1)S(1)} %get-tuple-element.20), channel_id=1, source_target_pairs={{0,16},{4,20},{8,24},{12,28},{16,0},{20,4},{24,8},{28,12},{1,17},{... | collective-permute-start | bytes 73736 | tf_op jit(solution)/shard_map/ppermute | solution.py:20
  15.7 5.5 %copy-start.1 = (bf16[3,512,384]{2,1,0:T(8,128)(2,1)S(1)}, bf16[3,512,384]{2,1,0:T(8,128)(2,1)}, u32[]{:S(2)}) copy-start(bf16[3,512,384]{2,1,0:T(8,128)(2,1)} %refs_1_.6) | copy-start | bytes 3538948
  17.1 5.4 %collective-permute-start.4 = (bf16[192,384]{1,0:T(8,128)(2,1)S(1)}, bf16[192,384]{1,0:T(8,128)(2,1)S(1)}, u32[]{:S(2)}, u32[]{:S(2)}) collective-permute-start(bf16[192,384]{1,0:T(8,128)(2,1)S(1)} %get-tuple-element.23), channel_id=1, source_target_pairs={{0,4},{4,0},{8,12},{12,8},{16,20},{20,16},{24,28},{28,24},{1,5},{5... | collective-permute-start | bytes 442376 | tf_op jit(solution)/shard_map/ppermute | solution.py:20
  17.2 6.8 %collective-permute-start.5 = (bf16[192,384]{1,0:T(8,128)(2,1)S(1)}, bf16[192,384]{1,0:T(8,128)(2,1)S(1)}, u32[]{:S(2)}, u32[]{:S(2)}) collective-permute-start(bf16[192,384]{1,0:T(8,128)(2,1)S(1)} %get-tuple-element.25), channel_id=1, source_target_pairs={{0,8},{4,12},{8,0},{12,4},{16,24},{20,28},{24,16},{28,20},{1,9},{5... | collective-permute-start | bytes 442376 | tf_op jit(solution)/shard_map/ppermute | solution.py:20
  18.8 8.5 %collective-permute-start.6 = (bf16[192,384]{1,0:T(8,128)(2,1)S(1)}, bf16[192,384]{1,0:T(8,128)(2,1)S(1)}, u32[]{:S(2)}, u32[]{:S(2)}) collective-permute-start(bf16[192,384]{1,0:T(8,128)(2,1)S(1)} %get-tuple-element.26), channel_id=1, source_target_pairs={{0,24},{4,28},{8,16},{12,20},{16,8},{20,12},{24,0},{28,4},{1,25},{... | collective-permute-start | bytes 442376 | tf_op jit(solution)/shard_map/ppermute | solution.py:32
  19.4 9.9 %collective-permute-start.7 = (bf16[192,384]{1,0:T(8,128)(2,1)S(1)}, bf16[192,384]{1,0:T(8,128)(2,1)S(1)}, u32[]{:S(2)}, u32[]{:S(2)}) collective-permute-start(bf16[192,384]{1,0:T(8,128)(2,1)S(1)} %get-tuple-element.27), channel_id=1, source_target_pairs={{0,28},{4,8},{8,4},{12,16},{16,12},{20,24},{24,20},{28,0},{1,29},{... | collective-permute-start | bytes 442376 | tf_op jit(solution)/shard_map/ppermute | solution.py:25
  21.2 8.2 %copy-start.5 = (f32[3,384]{1,0:T(4,128)S(1)}, f32[3,384]{1,0:T(4,128)}, u32[]{:S(2)}) copy-start(f32[3,384]{1,0:T(4,128)} %refs_1_.7) | copy-start | bytes 13828
  21.2 8.2 %copy-start.6 = (f32[192]{0:T(256)S(1)}, f32[192]{0:T(256)}, u32[]{:S(2)}) copy-start(f32[192]{0:T(256)} %param.19) | copy-start | bytes 2308
  30.0 3.6 %collective-permute-start.8 = (f32[3,64]{1,0:T(4,128)S(1)}, f32[3,64]{1,0:T(4,128)S(1)}, u32[]{:S(2)}, u32[]{:S(2)}) collective-permute-start(f32[3,64]{1,0:T(4,128)S(1)} %get-tuple-element.29), channel_id=1, source_target_pairs={{0,1},{1,0},{2,3},{3,2},{4,5},{5,4},{6,7},{7,6},{8,9},{9,8},{10,11... | collective-permute-start | bytes 2312 | tf_op jit(solution)/shard_map/ppermute | solution.py:20
  33.6 4.5 %collective-permute-start.9 = (f32[3,64]{1,0:T(4,128)S(1)}, f32[3,64]{1,0:T(4,128)S(1)}, u32[]{:S(2)}, u32[]{:S(2)}) collective-permute-start(f32[3,64]{1,0:T(4,128)S(1)} %add.3.mine_ref), channel_id=1, source_target_pairs={{0,2},{1,3},{2,0},{3,1},{4,6},{5,7},{6,4},{7,5},{8,10},{9,11},{10,... | collective-permute-start | bytes 2312 | tf_op jit(solution)/shard_map/ppermute | solution.py:20

commit v7 on v6

--- a/solution.py
+++ b/solution.py
@@ -246,6 +246,18 @@
         out_ref[:, columns] = direct_ref[:, columns] + value
 
 
+def near_kernel(me_ref, partial_ref, couple_ref, near_ref, out_ref):
+    _, near, _, _ = places(me_ref[0])
+    block = couple_ref.shape[2]
+    quarter, eighth = block // 4, block // 8
+    pieces = (
+        (1, lax.rem(near, 2), near_ref[: 2 * quarter, :]),
+        (2, near, near_ref[2 * quarter : 2 * (quarter + eighth), :]),
+    )
+    for columns, value in coupled(pieces, couple_ref):
+        out_ref[:, columns] = partial_ref[:, columns] + value
+
+
 def displace_kernel(
     capacity,
     rides,
@@ -261,15 +273,10 @@
 ):
     disp_ref, wanted_ref, first_ref = rest[-3:]
     me = me_ref[0]
-    chip, near, diag, far = places(me)
+    chip, _, diag, far = places(me)
     block = couple_ref.shape[2]
     quarter, eighth = block // 4, block // 8
-    pieces = (
-        (1, lax.rem(near, 2), near_ref[: 2 * quarter, :]),
-        (2, near, near_ref[2 * quarter : 2 * (quarter + eighth), :]),
-        (2, diag, diag_ref[: 2 * eighth, :]),
-        (2, far, far_ref[...]),
-    )
+    pieces = ((2, diag, diag_ref[: 2 * eighth, :]), (2, far, far_ref[...]))
     for columns, value in coupled(pieces, couple_ref):
         disp_ref[:, columns] = (partial_ref[:, columns] + value).astype(BF16)
     tall = 2 * capacity // 128
@@ -371,7 +378,7 @@
         row.append(jnp.zeros((1, lanes - clusters * points), F32))
     flat = jnp.broadcast_to(jnp.concatenate(row, axis=1), (8, lanes))
     share = out_ref.shape[1]
-    moved = pltpu.roll(flat, lanes - at_ref[0] * share, 1)
+    moved = pltpu.roll(flat, lax.rem(lanes - at_ref[0] * share, lanes), 1)
     out_ref[...] = moved[0:1, :share]
 
 
@@ -455,6 +462,14 @@
         1500000000,
         [smem] + [vmem] * 4,
     )
+    partial = call(
+        near_kernel,
+        (me, partial, constraint_modes, near),
+        array((modes, dof_count), F32),
+        8,
+        700000000,
+        [smem] + [vmem] * 3,
+    )
     disp, wanted, beside = call(
         lambda *refs: displace_kernel(capacity, rides, *refs),
         (me, partial, constraint_modes, pair, near, diag, far, lists, *loose),

time: 39 us -> 38.5 us (0.987)
  waiting for transfers between devices: 11.8 us -> 11.2 us
    ppermute x8, waiting for transfers between devices: 7.94 us -> 7.32 us  [swap_with(): lax.ppermute(value, axis, [(i, i ^ mask) for i in range(lax.axis_size(axi...]
    pallas_call x12 -> x13, Pallas kernels: 11.2 us -> 11.4 us  [call(): pl.pallas_call(kernel, out_shape=outputs, in_specs=specs or [vmem] * len(...]
  transfers between devices with their start and end apart: 10 -> 10, of which waited for: 7 -> 8; matrix products, arithmetic and copies ran while one was open for 0% -> 0% of each run, Pallas kernels for 14% -> 16%
where the time goes in v7:
time: 38.5 us; the launch traced here: 38.3 us
  starting transfers between devices  13.2 us (34%)
  Pallas kernels  12.3 us (32%)
  waiting for transfers between devices  11.2 us (29%)
  local copies, waits for them, and re-layouts  0.86 us (2%)
  between operations  0.81 us (2%)
    pallas_call x13, Pallas kernels, call(): pl.pallas_call(kernel, out_shape=outputs, in_specs=specs or [vmem] * len(...  11.4 us
    ppermute x8, starting transfers between devices, swap_with(): lax.ppermute(value, axis, [(i, i ^ mask) for i in range(lax.axis_size(axi...  10.8 us
    ppermute x8, waiting for transfers between devices, swap_with(): lax.ppermute(value, axis, [(i, i ^ mask) for i in range(lax.axis_size(axi...  7.32 us
    ppermute x1, waiting for transfers between devices, swap_across(): lax.ppermute(value, axis, [(i, (i + 2 * (i % 2) - 1) % peers) for i in ra...  2.08 us
    ppermute x1, waiting for transfers between devices, swap_outer(): lax.ppermute(value, axis, [(i, (i + 4 * (i // 2 % 2) - 2) % peers) for i...  1.75 us
    ppermute x1, starting transfers between devices, swap_across(): lax.ppermute(value, axis, [(i, (i + 2 * (i % 2) - 1) % peers) for i in ra...  1.74 us
    pallas_call x1, Pallas kernels, shards(): pl.pallas_call(store_kernel, out_shape=array((clusters, modes, rows), F32...  0.92 us
    unnamed x20, local copies, waits for them, and re-layouts  0.86 us
  transfers between devices with their start and end apart: 10, of which 8 were waited for; matrix products, arithmetic and copies ran while one was open for 0% of the time, Pallas kernels for 16%

profile of v7, /device:TPU:0, one launch (start us, length us, event | category | flops | bytes accessed | tf_op | source)
XLA Modules:
  0.0 38.3 jit_solution(14895691298765452169)
XLA Ops:
  0.7 0.8 %copy-done.9 = s32[3,512]{1,0:T(4,128)S(1)} copy-done((s32[3,512]{1,0:T(4,128)S(1)}, s32[3,512]{1,0:T(4,128)}, u32[]{:S(2)}) %copy-start.9) | copy-done | bytes 6168
  3.8 2.9 %collective-permute-start.1 = (bf16[208,192]{1,0:T(8,128)(2,1)S(1)}, bf16[208,192]{1,0:T(8,128)(2,1)S(1)}, u32[]{:S(2)}, u32[]{:S(2)}) collective-permute-start(bf16[208,192]{1,0:T(8,128)(2,1)S(1)} %get-tuple-element.18), channel_id=1, source_target_pairs={{0,8},{4,12},{8,0},{12,4},{16,24},{20,28},{24,16},{28,20},{1,9},{5... | collective-permute-start | bytes 239624 | tf_op jit(solution)/shard_map/ppermute | solution.py:20
  6.7 1.5 %collective-permute-start.2 = (bf16[80,192]{1,0:T(8,128)(2,1)S(1)}, bf16[80,192]{1,0:T(8,128)(2,1)S(1)}, u32[]{:S(2)}, u32[]{:S(2)}) collective-permute-start(bf16[80,192]{1,0:T(8,128)(2,1)S(1)} %get-tuple-element.19), channel_id=1, source_target_pairs={{0,24},{4,28},{8,16},{12,20},{16,8},{20,12},{24,0},{28,4},{1,25},{... | collective-permute-start | bytes 92168 | tf_op jit(solution)/shard_map/ppermute | solution.py:20
  8.2 1.0 %shard_map.116.partial_ref = f32[192,4096]{1,0:T(8,128)S(1)} custom-call(s32[1]{0:T(128)} %bitcast.1.refs_0_.me_ref, f32[192,4096]{1,0:T(8,128)S(1)} %shard_map.114.direct_ref, bf16[8,3,256,512]{3,2,1,0:T(8,128)(2,1)S(1)} %copy-done, bf16[240,192]{1,0:T(8,128)(2,1)S(1)} %shard_map.115.bag_ref.refs_1_, ...), custom_call_target="tpu_custom_call" | custom-call | flops 1500000000 | bytes 9621508 | tf_op jit(solution)/shard_map/pallas_call | solution.py:41
  9.3 0.7 %collective-permute-done.1.near_ref.refs_4_ = bf16[208,192]{1,0:T(8,128)(2,1)S(1)} collective-permute-done((bf16[208,192]{1,0:T(8,128)(2,1)S(1)}, bf16[208,192]{1,0:T(8,128)(2,1)S(1)}, u32[]{:S(2)}, u32[]{:S(2)}) %collective-permute-start.1) | collective-permute-done | bytes 79904 | tf_op jit(solution)/shard_map/ppermute | solution.py:20
  10.6 1.8 %collective-permute-done.3.refs_6_ = bf16[64,192]{1,0:T(8,128)(2,1)S(1)} collective-permute-done((bf16[64,192]{1,0:T(8,128)(2,1)S(1)}, bf16[64,192]{1,0:T(8,128)(2,1)S(1)}, u32[]{:S(2)}, u32[]{:S(2)}) %collective-permute-start.3) | collective-permute-done | bytes 24608 | tf_op jit(solution)/shard_map/ppermute | solution.py:20
  12.4 1.4 %shard_map.119 = (bf16[192,4096]{1,0:T(8,128)(2,1)S(1)}, s32[1,1536]{1,0:T(1,128)S(1)}, bf16[192,384]{1,0:T(8,128)(2,1)S(1)}) custom-call(s32[1]{0:T(128)} %bitcast.1.refs_0_.me_ref, f32[192,4096]{1,0:T(8,128)S(1)} %shard_map.118.refs_1_, bf16[8,3,256,512]{3,2,1,0:T(8,128)(2,1)S(1)} %copy-done, ...), custom_call_target="tpu_custom_call" | custom-call | flops 3000000000 | bytes 9680900 | tf_op jit(solution)/shard_map/pallas_call | solution.py:41
  13.9 1.4 %shard_map.120 = (bf16[192,384]{1,0:T(8,128)(2,1)S(1)}, bf16[192,384]{1,0:T(8,128)(2,1)S(1)}) custom-call(bf16[192,4096]{1,0:T(8,128)(2,1)S(1)} %get-tuple-element.21.refs_0_, s32[1,1536]{1,0:T(1,128)S(1)} %get-tuple-element.22.refs_1_), custom_call_target="tpu_custom_call" | custom-call | flops 2000000000 | bytes 1579008 | tf_op jit(solution)/shard_map/pallas_call | solution.py:41
  15.3 1.4 %shard_map.123 = (bf16[192,384]{1,0:T(8,128)(2,1)S(1)}, bf16[192,384]{1,0:T(8,128)(2,1)S(1)}) custom-call(bf16[192,4096]{1,0:T(8,128)(2,1)S(1)} %get-tuple-element.21.refs_0_, s32[1,1536]{1,0:T(1,128)S(1)} %get-tuple-element.22.refs_1_), custom_call_target="tpu_custom_call" | custom-call | flops 2000000000 | bytes 1579008 | tf_op jit(solution)/shard_map/pallas_call | solution.py:41
  16.8 1.6 %collective-permute-start.5 = (bf16[192,384]{1,0:T(8,128)(2,1)S(1)}, bf16[192,384]{1,0:T(8,128)(2,1)S(1)}, u32[]{:S(2)}, u32[]{:S(2)}) collective-permute-start(bf16[192,384]{1,0:T(8,128)(2,1)S(1)} %get-tuple-element.25), channel_id=1, source_target_pairs={{0,8},{4,12},{8,0},{12,4},{16,24},{20,28},{24,16},{28,20},{1,9},{5... | collective-permute-start | bytes 442376 | tf_op jit(solution)/shard_map/ppermute | solution.py:20
  18.3 0.7 %collective-permute-start.6 = (bf16[192,384]{1,0:T(8,128)(2,1)S(1)}, bf16[192,384]{1,0:T(8,128)(2,1)S(1)}, u32[]{:S(2)}, u32[]{:S(2)}) collective-permute-start(bf16[192,384]{1,0:T(8,128)(2,1)S(1)} %get-tuple-element.26), channel_id=1, source_target_pairs={{0,24},{4,28},{8,16},{12,20},{16,8},{20,12},{24,0},{28,4},{1,25},{... | collective-permute-start | bytes 442376 | tf_op jit(solution)/shard_map/ppermute | solution.py:32
  19.0 1.7 %collective-permute-start.7 = (bf16[192,384]{1,0:T(8,128)(2,1)S(1)}, bf16[192,384]{1,0:T(8,128)(2,1)S(1)}, u32[]{:S(2)}, u32[]{:S(2)}) collective-permute-start(bf16[192,384]{1,0:T(8,128)(2,1)S(1)} %get-tuple-element.27), channel_id=1, source_target_pairs={{0,28},{4,8},{8,4},{12,16},{16,12},{20,24},{24,20},{28,0},{1,29},{... | collective-permute-start | bytes 442376 | tf_op jit(solution)/shard_map/ppermute | solution.py:25
  20.7 1.4 %shard_map.122.refs_3_ = bf16[768,1152]{1,0:T(8,128)(2,1)S(1)} custom-call(s32[3,512]{1,0:T(4,128)S(1)} %get-tuple-element.16.refs_0_, bf16[3,512,384]{2,1,0:T(8,128)(2,1)S(1)} %copy-done.1), custom_call_target="tpu_custom_call" | custom-call | flops 2000000000 | bytes 1185792 | tf_op jit(solution)/shard_map/pallas_call | solution.py:41
  22.1 1.4 %collective-permute-done.5.refs_4_ = bf16[192,384]{1,0:T(8,128)(2,1)S(1)} collective-permute-done((bf16[192,384]{1,0:T(8,128)(2,1)S(1)}, bf16[192,384]{1,0:T(8,128)(2,1)S(1)}, u32[]{:S(2)}, u32[]{:S(2)}) %collective-permute-start.5) | collective-permute-done | bytes 147488 | tf_op jit(solution)/shard_map/ppermute | solution.py:20
  23.6 1.5 %shard_map.121.refs_2_ = f32[3,192,384]{2,1,0:T(8,128)S(1)} custom-call(s32[3,512]{1,0:T(4,128)S(1)} %get-tuple-element.16.refs_0_, bf16[3,512,384]{2,1,0:T(8,128)(2,1)S(1)} %copy-done.1, bf16[192,384]{1,0:T(8,128)(2,1)S(1)} %collective-permute-done.4.refs_2_, bf16[192,384]{1,0:T(8,128)(2,1)S(1)} %get-tuple-element.24.refs_3_, ...), custom_call_target="tpu_custom_call" | custom-call | flops 500000000 | bytes 1628160 | tf_op jit(solution)/shard_map/pallas_call | solution.py:41
  25.1 1.8 %collective-permute-done.6.refs_4_ = bf16[192,384]{1,0:T(8,128)(2,1)S(1)} collective-permute-done((bf16[192,384]{1,0:T(8,128)(2,1)S(1)}, bf16[192,384]{1,0:T(8,128)(2,1)S(1)}, u32[]{:S(2)}, u32[]{:S(2)}) %collective-permute-start.6) | collective-permute-done | bytes 147488 | tf_op jit(solution)/shard_map/ppermute | solution.py:32
  26.9 2.1 %collective-permute-done.7.refs_5_ = bf16[192,384]{1,0:T(8,128)(2,1)S(1)} collective-permute-done((bf16[192,384]{1,0:T(8,128)(2,1)S(1)}, bf16[192,384]{1,0:T(8,128)(2,1)S(1)}, u32[]{:S(2)}, u32[]{:S(2)}) %collective-permute-start.7) | collective-permute-done | bytes 147488 | tf_op jit(solution)/shard_map/ppermute | solution.py:25
  28.9 0.7 %shard_map.124 = (f32[3,192,384]{2,1,0:T(8,128)S(1)}, f32[3,64]{1,0:T(4,128)S(1)}) custom-call(f32[1,192]{1,0:T(1,128)S(1)} %bitcast.8, f32[3,384]{1,0:T(4,128)S(1)} %copy-done.5, f32[3,192,384]{2,1,0:T(8,128)S(1)} %shard_map.121.refs_2_, bf16[768,1152]{1,0:T(8,128)(2,1)S(1)} %shard_map.122.refs_3_, bf16[192,384]{1,0:T(8,128)(2,1)S(1)} %collective-permute-done.6.refs_4_, ...), custom_call_target="tpu_custom_call" | custom-call | flops 500000000 | bytes 2954496 | tf_op jit(solution)/shard_map/pallas_call | solution.py:41
  29.6 1.6 %collective-permute-start.8 = (f32[3,64]{1,0:T(4,128)S(1)}, f32[3,64]{1,0:T(4,128)S(1)}, u32[]{:S(2)}, u32[]{:S(2)}) collective-permute-start(f32[3,64]{1,0:T(4,128)S(1)} %get-tuple-element.29), channel_id=1, source_target_pairs={{0,1},{1,0},{2,3},{3,2},{4,5},{5,4},{6,7},{7,6},{8,9},{9,8},{10,11... | collective-permute-start | bytes 2312 | tf_op jit(solution)/shard_map/ppermute | solution.py:20
  31.2 2.0 %collective-permute-done.8 = f32[3,64]{1,0:T(4,128)S(1)} collective-permute-done((f32[3,64]{1,0:T(4,128)S(1)}, f32[3,64]{1,0:T(4,128)S(1)}, u32[]{:S(2)}, u32[]{:S(2)}) %collective-permute-start.8) | collective-permute-done | bytes 800 | tf_op jit(solution)/shard_map/ppermute | solution.py:20
  33.2 2.6 %collective-permute-start.9 = (f32[3,64]{1,0:T(4,128)S(1)}, f32[3,64]{1,0:T(4,128)S(1)}, u32[]{:S(2)}, u32[]{:S(2)}) collective-permute-start(f32[3,64]{1,0:T(4,128)S(1)} %add.3.mine_ref), channel_id=1, source_target_pairs={{0,2},{1,3},{2,0},{3,1},{4,6},{5,7},{6,4},{7,5},{8,10},{9,11},{10,... | collective-permute-start | bytes 2312 | tf_op jit(solution)/shard_map/ppermute | solution.py:20
  35.8 0.9 %store.1 = f32[3,192,384]{2,1,0:T(8,128)} custom-call(f32[3,192,384]{2,1,0:T(8,128)S(1)} %get-tuple-element.28.source_ref), custom_call_target="tpu_custom_call" | custom-call | flops 500000000 | bytes 2000000 | tf_op jit(solution)/shard_map/store/pallas_call | solution.py:530
  36.7 1.0 %collective-permute-done.9.other_ref = f32[3,64]{1,0:T(4,128)S(1)} collective-permute-done((f32[3,64]{1,0:T(4,128)S(1)}, f32[3,64]{1,0:T(4,128)S(1)}, u32[]{:S(2)}, u32[]{:S(2)}) %collective-permute-start.9) | collective-permute-done | bytes 800 | tf_op jit(solution)/shard_map/ppermute | solution.py:20
  37.7 0.7 %shard_map.125 = f32[1,48]{1,0:T(1,128)} custom-call(s32[1]{0:T(128)} %bitcast.4.at_ref, f32[3,64]{1,0:T(4,128)S(1)} %add.3.mine_ref, f32[3,64]{1,0:T(4,128)S(1)} %collective-permute-done.9.other_ref), custom_call_target="tpu_custom_call" | custom-call | flops 1000 | bytes 1540 | tf_op jit(solution)/shard_map/pallas_call | solution.py:41
  (31 shorter events, 3.0 us)
Async XLA Ops:
  0.6 1.5 %copy-start.2 = (bf16[192,128]{1,0:T(8,128)(2,1)S(1)}, bf16[192,128]{1,0:T(8,128)(2,1)}, u32[]{:S(2)}) copy-start(bf16[192,128]{1,0:T(8,128)(2,1)} %refs_0_.1) | copy-start | bytes 147460
  0.6 1.5 %copy-start.3 = (bf16[192,64]{0,1:T(8,128)(2,1)S(1)}, bf16[192,64]{0,1:T(8,128)(2,1)}, u32[]{:S(2)}) copy-start(bf16[192,64]{0,1:T(8,128)(2,1)} %param.14) | copy-start | bytes 73732
  0.7 1.5 %copy-start.4 = (bf16[192,32]{0,1:T(8,128)(2,1)S(1)}, bf16[192,32]{0,1:T(8,128)(2,1)}, u32[]{:S(2)}) copy-start(bf16[192,32]{0,1:T(8,128)(2,1)} %param.15) | copy-start | bytes 36868
  0.7 2.1 %copy-start.8 = (bf16[8,192,128]{2,1,0:T(8,128)(2,1)S(1)}, bf16[8,192,128]{2,1,0:T(8,128)(2,1)}, u32[]{:S(2)}) copy-start(bf16[8,192,128]{2,1,0:T(8,128)(2,1)} %coords_ref.1) | copy-start | bytes 1179652
  0.7 2.1 %copy-start.7 = (bf16[8,128,512]{2,1,0:T(8,128)(2,1)S(1)}, bf16[8,128,512]{2,1,0:T(8,128)(2,1)}, u32[]{:S(2)}) copy-start(bf16[8,128,512]{2,1,0:T(8,128)(2,1)} %modes_ref.1) | copy-start | bytes 3145732
  0.7 0.8 %copy-start.9 = (s32[3,512]{1,0:T(4,128)S(1)}, s32[3,512]{1,0:T(4,128)}, u32[]{:S(2)}) copy-start(s32[3,512]{1,0:T(4,128)} %refs_1_.4) | copy-start | bytes 18436
  1.5 6.7 %copy-start = (bf16[8,3,256,512]{3,2,1,0:T(8,128)(2,1)S(1)}, bf16[8,3,256,512]{3,2,1,0:T(8,128)(2,1)}, u32[]{:S(2)}) copy-start(bf16[8,3,256,512]{3,2,1,0:T(8,128)(2,1)} %refs_2_.1) | copy-start | bytes 18874372
  2.2 1.5 %collective-permute-start = (bf16[240,192]{1,0:T(8,128)(2,1)S(1)}, bf16[240,192]{1,0:T(8,128)(2,1)S(1)}, u32[]{:S(2)}, u32[]{:S(2)}) collective-permute-start(bf16[240,192]{1,0:T(8,128)(2,1)S(1)} %shard_map.115.bag_ref.refs_1_), channel_id=1, source_target_pairs={{0,4},{4,0},{8,12},{12,8},{16,20},{20,16},{24,28},{28,24},{1,5},{5... | collective-permute-start | bytes 276488 | tf_op jit(solution)/shard_map/ppermute | solution.py:20
  3.8 6.2 %collective-permute-start.1 = (bf16[208,192]{1,0:T(8,128)(2,1)S(1)}, bf16[208,192]{1,0:T(8,128)(2,1)S(1)}, u32[]{:S(2)}, u32[]{:S(2)}) collective-permute-start(bf16[208,192]{1,0:T(8,128)(2,1)S(1)} %get-tuple-element.18), channel_id=1, source_target_pairs={{0,8},{4,12},{8,0},{12,4},{16,24},{20,28},{24,16},{28,20},{1,9},{5... | collective-permute-start | bytes 239624 | tf_op jit(solution)/shard_map/ppermute | solution.py:20
  6.7 5.7 %collective-permute-start.2 = (bf16[80,192]{1,0:T(8,128)(2,1)S(1)}, bf16[80,192]{1,0:T(8,128)(2,1)S(1)}, u32[]{:S(2)}, u32[]{:S(2)}) collective-permute-start(bf16[80,192]{1,0:T(8,128)(2,1)S(1)} %get-tuple-element.19), channel_id=1, source_target_pairs={{0,24},{4,28},{8,16},{12,20},{16,8},{20,12},{24,0},{28,4},{1,25},{... | collective-permute-start | bytes 92168 | tf_op jit(solution)/shard_map/ppermute | solution.py:20
  8.2 4.2 %collective-permute-start.3 = (bf16[64,192]{1,0:T(8,128)(2,1)S(1)}, bf16[64,192]{1,0:T(8,128)(2,1)S(1)}, u32[]{:S(2)}, u32[]{:S(2)}) collective-permute-start(bf16[64,192]{1,0:T(8,128)(2,1)S(1)} %get-tuple-element.20), channel_id=1, source_target_pairs={{0,16},{4,20},{8,24},{12,28},{16,0},{20,4},{24,8},{28,12},{1,17},{... | collective-permute-start | bytes 73736 | tf_op jit(solution)/shard_map/ppermute | solution.py:20
  15.3 5.5 %copy-start.1 = (bf16[3,512,384]{2,1,0:T(8,128)(2,1)S(1)}, bf16[3,512,384]{2,1,0:T(8,128)(2,1)}, u32[]{:S(2)}) copy-start(bf16[3,512,384]{2,1,0:T(8,128)(2,1)} %refs_1_.6) | copy-start | bytes 3538948
  16.7 5.4 %collective-permute-start.4 = (bf16[192,384]{1,0:T(8,128)(2,1)S(1)}, bf16[192,384]{1,0:T(8,128)(2,1)S(1)}, u32[]{:S(2)}, u32[]{:S(2)}) collective-permute-start(bf16[192,384]{1,0:T(8,128)(2,1)S(1)} %get-tuple-element.23), channel_id=1, source_target_pairs={{0,4},{4,0},{8,12},{12,8},{16,20},{20,16},{24,28},{28,24},{1,5},{5... | collective-permute-start | bytes 442376 | tf_op jit(solution)/shard_map/ppermute | solution.py:20
  16.8 6.8 %collective-permute-start.5 = (bf16[192,384]{1,0:T(8,128)(2,1)S(1)}, bf16[192,384]{1,0:T(8,128)(2,1)S(1)}, u32[]{:S(2)}, u32[]{:S(2)}) collective-permute-start(bf16[192,384]{1,0:T(8,128)(2,1)S(1)} %get-tuple-element.25), channel_id=1, source_target_pairs={{0,8},{4,12},{8,0},{12,4},{16,24},{20,28},{24,16},{28,20},{1,9},{5... | collective-permute-start | bytes 442376 | tf_op jit(solution)/shard_map/ppermute | solution.py:20
  18.3 8.5 %collective-permute-start.6 = (bf16[192,384]{1,0:T(8,128)(2,1)S(1)}, bf16[192,384]{1,0:T(8,128)(2,1)S(1)}, u32[]{:S(2)}, u32[]{:S(2)}) collective-permute-start(bf16[192,384]{1,0:T(8,128)(2,1)S(1)} %get-tuple-element.26), channel_id=1, source_target_pairs={{0,24},{4,28},{8,16},{12,20},{16,8},{20,12},{24,0},{28,4},{1,25},{... | collective-permute-start | bytes 442376 | tf_op jit(solution)/shard_map/ppermute | solution.py:32
  19.0 9.9 %collective-permute-start.7 = (bf16[192,384]{1,0:T(8,128)(2,1)S(1)}, bf16[192,384]{1,0:T(8,128)(2,1)S(1)}, u32[]{:S(2)}, u32[]{:S(2)}) collective-permute-start(bf16[192,384]{1,0:T(8,128)(2,1)S(1)} %get-tuple-element.27), channel_id=1, source_target_pairs={{0,28},{4,8},{8,4},{12,16},{16,12},{20,24},{24,20},{28,0},{1,29},{... | collective-permute-start | bytes 442376 | tf_op jit(solution)/shard_map/ppermute | solution.py:25
  20.7 8.2 %copy-start.5 = (f32[3,384]{1,0:T(4,128)S(1)}, f32[3,384]{1,0:T(4,128)}, u32[]{:S(2)}) copy-start(f32[3,384]{1,0:T(4,128)} %refs_1_.7) | copy-start | bytes 13828
  20.7 8.2 %copy-start.6 = (f32[192]{0:T(256)S(1)}, f32[192]{0:T(256)}, u32[]{:S(2)}) copy-start(f32[192]{0:T(256)} %param.19) | copy-start | bytes 2308
  29.6 3.6 %collective-permute-start.8 = (f32[3,64]{1,0:T(4,128)S(1)}, f32[3,64]{1,0:T(4,128)S(1)}, u32[]{:S(2)}, u32[]{:S(2)}) collective-permute-start(f32[3,64]{1,0:T(4,128)S(1)} %get-tuple-element.29), channel_id=1, source_target_pairs={{0,1},{1,0},{2,3},{3,2},{4,5},{5,4},{6,7},{7,6},{8,9},{9,8},{10,11... | collective-permute-start | bytes 2312 | tf_op jit(solution)/shard_map/ppermute | solution.py:20
  33.2 4.5 %collective-permute-start.9 = (f32[3,64]{1,0:T(4,128)S(1)}, f32[3,64]{1,0:T(4,128)S(1)}, u32[]{:S(2)}, u32[]{:S(2)}) collective-permute-start(f32[3,64]{1,0:T(4,128)S(1)} %add.3.mine_ref), channel_id=1, source_target_pairs={{0,2},{1,3},{2,0},{3,1},{4,6},{5,7},{6,4},{7,5},{8,10},{9,11},{10,... | collective-permute-start | bytes 2312 | tf_op jit(solution)/shard_map/ppermute | solution.py:20
